TPU v7x, 16 devices: a whole 2x2x2 slice. The times are simulated.
16 devices in a mesh: fsdp: 16 (over z, y, x, core).
Axes of the slice: x: 2, y: 2, z: 2, core: 2. Of those that a mesh axis runs over, the one named last changes fastest.
Arguments:
- tokens_x: bfloat16 [96, 256, 640], P('fsdp')
- context: bfloat16 [96, 77, 2048], P('fsdp')
- cot_out: bfloat16 [96, 256, 640], P('fsdp')
- w_qkv: bfloat16 [2, 1228800], P(None, 'fsdp')
- w_out: bfloat16 [2, 409600], P(None, 'fsdp')
- w_q2: bfloat16 [2, 409600], P(None, 'fsdp')
- w_kv2: bfloat16 [2, 2621440], P(None, 'fsdp')
- w_out2: bfloat16 [2, 409600], P(None, 'fsdp')
- w_ff1: bfloat16 [2, 3276800], P(None, 'fsdp')
- w_ff2: bfloat16 [2, 1638400], P(None, 'fsdp')
- w_vecs: bfloat16 [2, 10880], P(None, 'fsdp')
Outputs:
- output 1: bfloat16 [96, 256, 640], P('fsdp')
- output 2: bfloat16 [96, 256, 640], P('fsdp')
- output 3: float32 [2, 1228800], P(None, 'fsdp')
- output 4: float32 [2, 409600], P(None, 'fsdp')
- output 5: float32 [2, 409600], P(None, 'fsdp')
- output 6: float32 [2, 2621440], P(None, 'fsdp')
- output 7: float32 [2, 409600], P(None, 'fsdp')
- output 8: float32 [2, 3276800], P(None, 'fsdp')
- output 9: float32 [2, 1638400], P(None, 'fsdp')
- output 10: float32 [2, 10880], P(None, 'fsdp')
All inputs are finite; a program needn't handle non-finite values.
Results may differ from a plain program's by a relative error of at most 0.0199622.
Values are sent between devices in bfloat16 or wider.
A program may use at most 1 GiB of HBM per device.

v0:
```python
import math
import jax
import jax.numpy as jnp
from jax import lax
from jax.sharding import PartitionSpec as P

HEAD = 64
AXIS = 'fsdp'


def weight_shapes(width, ctx_width):
    return ((width, 3 * width), (width, width), (width, width), (ctx_width, 2 * width),
            (width, width), (width, 8 * width), (4 * width, width), (17 * width,))


def layer_norm(residual, gain, shift):
    average = jnp.mean(residual, axis=-1, keepdims=True)
    centered = residual - average
    variance = jnp.mean(centered * centered, axis=-1, keepdims=True)
    return centered * lax.rsqrt(variance + 1e-5) * gain + shift


def attend(query, keys, values):
    scores = jnp.einsum('bqhe,bkhe->bhqk', query, keys, preferred_element_type=jnp.float32) * HEAD ** -0.5
    probabilities = jax.nn.softmax(scores, axis=-1).astype(jnp.bfloat16)
    mixed = jnp.einsum('bhqk,bkhe->bqhe', probabilities, values, preferred_element_type=jnp.float32)
    return mixed.astype(jnp.bfloat16)


def self_attend(qkv_heads):
    return attend(qkv_heads[:, :, 0], qkv_heads[:, :, 1], qkv_heads[:, :, 2])


def cross_attend(query, kv_heads):
    return attend(query, kv_heads[:, :, 0], kv_heads[:, :, 1])


def geglu(hidden):
    half = hidden.shape[-1] // 2
    return (hidden[..., :half] * jax.nn.gelu(hidden[..., half:], approximate=False)).astype(jnp.bfloat16)


def project(inputs, weight):
    return jnp.einsum('btd,de->bte', inputs, weight, preferred_element_type=jnp.float32)


def project_back(grads, weight):
    return jnp.einsum('bte,de->btd', grads, weight, preferred_element_type=jnp.float32)


def weight_grad(inputs, grads):
    return jnp.einsum('btd,bte->de', inputs, grads, preferred_element_type=jnp.float32)


def gather_block(shards, width, ctx_width):
    full = []
    for shard, shape in zip(shards, weight_shapes(width, ctx_width)):
        whole = lax.all_gather(shard, AXIS, axis=0, tiled=True)
        full.append(whole[:math.prod(shape)].reshape(shape))
    vec_flat = full[7]
    return dict(w_qkv=full[0], w_out=full[1], w_q2=full[2], w_kv2=full[3], w_out2=full[4],
                w_ff1=full[5], w_ff2=full[6],
                rows=vec_flat[:9 * width].reshape(9, width).astype(jnp.float32),
                bias_ff1=vec_flat[9 * width:].astype(jnp.float32))


def block_forward(residual, context, weights):
    batch, tokens, width = residual.shape
    heads = width // HEAD
    rows = weights['rows']
    norm1, ln1_back = jax.vjp(layer_norm, residual, rows[0], rows[1])
    norm1 = norm1.astype(jnp.bfloat16)
    qkv_heads = project(norm1, weights['w_qkv']).astype(jnp.bfloat16).reshape(batch, tokens, 3, heads, HEAD)
    self_out, self_back = jax.vjp(self_attend, qkv_heads)
    self_out = self_out.reshape(batch, tokens, width)
    residual = residual + project(self_out, weights['w_out']) + rows[6]
    norm2, ln2_back = jax.vjp(layer_norm, residual, rows[2], rows[3])
    norm2 = norm2.astype(jnp.bfloat16)
    query = project(norm2, weights['w_q2']).astype(jnp.bfloat16).reshape(batch, tokens, heads, HEAD)
    kv_heads = project(context, weights['w_kv2']).astype(jnp.bfloat16).reshape(batch, context.shape[1], 2, heads, HEAD)
    cross_out, cross_back = jax.vjp(cross_attend, query, kv_heads)
    cross_out = cross_out.reshape(batch, tokens, width)
    residual = residual + project(cross_out, weights['w_out2']) + rows[7]
    norm3, ln3_back = jax.vjp(layer_norm, residual, rows[4], rows[5])
    norm3 = norm3.astype(jnp.bfloat16)
    gated, geglu_back = jax.vjp(geglu, project(norm3, weights['w_ff1']) + weights['bias_ff1'])
    residual = residual + project(gated, weights['w_ff2']) + rows[8]
    saved = dict(ln1_back=ln1_back, norm1=norm1, self_back=self_back, self_out=self_out,
                 ln2_back=ln2_back, norm2=norm2, cross_back=cross_back, cross_out=cross_out,
                 ln3_back=ln3_back, norm3=norm3, geglu_back=geglu_back, gated=gated)
    return residual, saved


def block_backward(grad, context, weights, saved):
    batch, tokens, width = grad.shape
    heads = width // HEAD
    grad_bf = grad.astype(jnp.bfloat16)
    g_bias_ff2 = jnp.sum(grad, axis=(0, 1))
    g_ff2 = weight_grad(saved['gated'], grad_bf)
    d_gated = project_back(grad_bf, weights['w_ff2']).astype(jnp.bfloat16)
    (d_hidden,) = saved['geglu_back'](d_gated)
    g_bias_ff1 = jnp.sum(d_hidden, axis=(0, 1))
    d_hidden = d_hidden.astype(jnp.bfloat16)
    g_ff1 = weight_grad(saved['norm3'], d_hidden)
    d_res, g_ln3_gain, g_ln3_shift = saved['ln3_back'](project_back(d_hidden, weights['w_ff1']))
    grad = grad + d_res
    grad_bf = grad.astype(jnp.bfloat16)
    g_bias_out2 = jnp.sum(grad, axis=(0, 1))
    g_out2 = weight_grad(saved['cross_out'], grad_bf)
    d_cross = project_back(grad_bf, weights['w_out2']).astype(jnp.bfloat16).reshape(batch, tokens, heads, HEAD)
    d_query, d_kv = saved['cross_back'](d_cross)
    d_query = d_query.reshape(batch, tokens, width)
    g_q2 = weight_grad(saved['norm2'], d_query)
    g_kv2 = weight_grad(context, d_kv.reshape(batch, context.shape[1], 2 * width))
    d_res, g_ln2_gain, g_ln2_shift = saved['ln2_back'](project_back(d_query, weights['w_q2']))
    grad = grad + d_res
    grad_bf = grad.astype(jnp.bfloat16)
    g_bias_out = jnp.sum(grad, axis=(0, 1))
    g_out = weight_grad(saved['self_out'], grad_bf)
    d_self = project_back(grad_bf, weights['w_out']).astype(jnp.bfloat16).reshape(batch, tokens, heads, HEAD)
    (d_qkv,) = saved['self_back'](d_self)
    d_qkv = d_qkv.reshape(batch, tokens, 3 * width)
    g_qkv = weight_grad(saved['norm1'], d_qkv)
    d_res, g_ln1_gain, g_ln1_shift = saved['ln1_back'](project_back(d_qkv, weights['w_qkv']))
    grad = grad + d_res
    g_vecs = jnp.concatenate([g_ln1_gain, g_ln1_shift, g_ln2_gain, g_ln2_shift, g_ln3_gain, g_ln3_shift,
                              g_bias_out, g_bias_out2, g_bias_ff2, g_bias_ff1])
    return grad, [g_qkv, g_out, g_q2, g_kv2, g_out2, g_ff1, g_ff2, g_vecs]


def scatter_grads(grads, shard_lens, n_dev, total):
    result = []
    for grad_full, shard_len in zip(grads, shard_lens):
        flat = grad_full.reshape(-1)
        flat = jnp.pad(flat, (0, shard_len * n_dev - flat.shape[0]))
        result.append(lax.psum_scatter(flat, AXIS, scatter_dimension=0, tiled=True) / total)
    return result


def solution(mesh):
    n_dev = mesh.shape[AXIS]

    def local(tokens_x, context, cot_out, *shards):
        batch, tokens, width = tokens_x.shape
        ctx_width = context.shape[-1]
        blocks = shards[0].shape[0]
        shard_lens = [shard.shape[1] for shard in shards]
        total = batch * n_dev
        residual = tokens_x.astype(jnp.float32)
        saved_list = []
        for layer in range(blocks):
            weights = gather_block([shard[layer] for shard in shards], width, ctx_width)
            residual, saved = block_forward(residual, context, weights)
            saved_list.append(saved)
        grad = cot_out.astype(jnp.float32)
        grad_shards = []
        for layer in reversed(range(blocks)):
            grad, layer_shards = lax.optimization_barrier((grad, [shard[layer] for shard in shards]))
            weights = gather_block(layer_shards, width, ctx_width)
            grad, block_grads = block_backward(grad, context, weights, saved_list[layer])
            grad_shards.insert(0, scatter_grads(block_grads, shard_lens, n_dev, total))
        stacked = [jnp.stack([per_layer[index] for per_layer in grad_shards]) for index in range(len(shards))]
        return tuple([residual.astype(jnp.bfloat16), grad.astype(jnp.bfloat16)] + stacked)

    param_spec = P(None, AXIS)
    in_specs = (P(AXIS), P(AXIS), P(AXIS)) + (param_spec,) * 8
    out_specs = (P(AXIS), P(AXIS)) + (param_spec,) * 8
    return jax.shard_map(local, mesh=mesh, in_specs=in_specs, out_specs=out_specs, check_vma=False)
```

profile of v0, /device:TPU:0, one launch (start us, length us, event | category | flops | bytes accessed | tf_op | source)
XLA Modules:
  0.0 2969.8 jit_solution(7425032357652016097)
XLA Ops:
  43.2 35.7 %all-reduce.34 = (bf16[10880]{0:T(1024)(128)(2,1)S(1)}, bf16[10880]{0:T(1024)(128)(2,1)S(1)}) all-reduce(bf16[10880]{0:T(1024)(128)(2,1)S(1)} %dynamic-update-slice, bf16[10880]{0:T(1024)(128)(2,1)S(1)} %dynamic-update-slice.1), channel_id=2, replica_groups=mesh['fsdp'=16] {'fsdp'}, use_global_device_ids=true, to_apply=%add.14 | all-reduce | flops 21760 | bytes 87040
  154.4 19.4 all-gather.5
  265.6 18.7 all-gather.13
  351.5 53.7 %reduce.3 = bf16[1228800]{0:T(1024)(128)(2,1)} reduce(bf16[1,1228800]{1,0:T(2,128)(2,1)} %all-gather.43.cloned.1.call-done, bf16[]{:T(256)} %constant.214), dimensions={0}, to_apply=%all-gather.1.reduce_sub_computation | reduce | bytes 4915202 | tf_op jit(solution)/shard_map/all_gather | solution.py:58
  438.3 18.4 fusion.139
  480.4 53.6 %reduce.20 = bf16[1228800]{0:T(1024)(128)(2,1)} reduce(bf16[1,1228800]{1,0:T(2,128)(2,1)} %all-gather.51.cloned.1.call-done, bf16[]{:T(256)} %constant.214), dimensions={0}, to_apply=%all-gather.9.reduce_sub_computation | reduce | bytes 4915202 | tf_op jit(solution)/shard_map/all_gather | solution.py:58
  545.3 71.2 %reduce.15 = bf16[1638400]{0:T(1024)(128)(2,1)} reduce(bf16[1,1638400]{1,0:T(2,128)(2,1)} %all-gather.49.cloned.1.call-done, bf16[]{:T(256)} %constant.214), dimensions={0}, to_apply=%all-gather.7.reduce_sub_computation | reduce | bytes 6553602 | tf_op jit(solution)/shard_map/all_gather | solution.py:58
  629.5 112.1 %reduce.6 = bf16[2621440]{0:T(1024)(128)(2,1)} reduce(bf16[1,2621440]{1,0:T(2,128)(2,1)} %all-gather.45.cloned.1.call-done, bf16[]{:T(256)} %constant.214), dimensions={0}, to_apply=%all-gather.3.reduce_sub_computation | reduce | bytes 10485762 | tf_op jit(solution)/shard_map/all_gather | solution.py:58
  781.8 112.1 %reduce.23 = bf16[2621440]{0:T(1024)(128)(2,1)} reduce(bf16[1,2621440]{1,0:T(2,128)(2,1)} %all-gather.53.cloned.1.call-done, bf16[]{:T(256)} %constant.214), dimensions={0}, to_apply=%all-gather.11.reduce_sub_computation | reduce | bytes 10485762 | tf_op jit(solution)/shard_map/all_gather | solution.py:58
  912.4 139.8 %reduce.14 = bf16[3276800]{0:T(1024)(128)(2,1)} reduce(bf16[1,3276800]{1,0:T(2,128)(2,1)} %all-gather.47.cloned.1.call-done, bf16[]{:T(256)} %constant.214), dimensions={0}, to_apply=%all-gather.6.reduce_sub_computation | reduce | bytes 13107202 | tf_op jit(solution)/shard_map/all_gather | solution.py:58
  1062.5 22.0 broadcast_add_fusion.1
  1084.5 37.3 %multiply_convert_fusion.1 = (bf16[6,256,2560]{2,1,0:T(8,128)(2,1)S(1)}, f32[6,256,2560]{2,1,0:T(8,128)}) fusion(f32[6,256,5120]{2,1,0:T(8,128)} %broadcast_add_fusion.1), kind=kLoop, calls=%fused_computation.50 | loop fusion | flops 259522560 | bytes 55050240 | tf_op jit(solution)/shard_map/jvp()/convert_element_type | solution.py:40
  1157.3 18.0 fusion.144
  1216.0 139.8 %reduce.31 = bf16[3276800]{0:T(1024)(128)(2,1)} reduce(bf16[1,3276800]{1,0:T(2,128)(2,1)} %all-gather.55.cloned.1.call-done, bf16[]{:T(256)} %constant.214), dimensions={0}, to_apply=%all-gather.14.reduce_sub_computation | reduce | bytes 13107202 | tf_op jit(solution)/shard_map/all_gather | solution.py:58
  1372.3 20.1 broadcast_add_fusion
  1392.4 45.4 %multiply_add_fusion.1 = (f32[6,256,2560]{2,1,0:T(8,128)}, f32[6,256,2560]{2,1,0:T(8,128)}, bf16[6,256,2560]{2,1,0:T(8,128)(2,1)}) fusion(f32[6,256,5120]{2,1,0:T(8,128)} %broadcast_add_fusion, bf16[2560,640,1]{1,0,2:T(8,128)(2,1)} %reshape.638, f32[6,256,640]{2,1,0:T(8,128)S(1)} %copy-done.37), kind=kOutput, calls=%fused_computation.33 | convolution fusion | flops 5325127680 | bytes 77987840 | tf_op jit(solution)/shard_map/bte,de->btd/dot_general | solution.py:48
  1437.8 27.3 convert_multiply_fusion.4
  1475.5 22.0 fusion.129
  1624.4 21.4 convolution_bitcast_fusion.2
  1815.6 30.0 %multiply_add_fusion = (f32[6,256,2560]{2,1,0:T(8,128)}, f32[6,256,2560]{2,1,0:T(8,128)}) fusion(f32[6,256,2560]{2,1,0:T(8,128)} %get-tuple-element.123, f32[6,256,5120]{2,1,0:T(8,128)} %broadcast_add_fusion.1, bf16[2560,640,1]{1,0,2:T(8,128)(2,1)} %reshape.644, f32[6,256,640]{2,1,0:T(8,128)} %add_add_fusion.8), kind=kOutput, calls=%fused_computation.32 | convolution fusion | flops 5104926720 | bytes 85852160 | tf_op jit(solution)/shard_map/bte,de->btd/dot_general | solution.py:48
  1845.6 21.2 convolution_bitcast_fusion.3
  1900.9 20.7 fusion.126
  2089.3 70.9 %reduce.32 = bf16[1638400]{0:T(1024)(128)(2,1)} reduce(bf16[1,1638400]{1,0:T(2,128)(2,1)} %all-gather.57.cloned.1.call-done, bf16[]{:T(256)} %constant.214), dimensions={0}, to_apply=%all-gather.15.reduce_sub_computation | reduce | bytes 6553602 | tf_op jit(solution)/shard_map/all_gather | solution.py:58
  2182.7 755.5 %all-reduce.40.cloned.1.call-done = (f32[1228800]{0:T(1024)}, f32[1228800]{0:T(1024)}, f32[409600]{0:T(1024)}, f32[409600]{0:T(1024)}, f32[409600]{0:T(1024)}, /...) async-done(((f32[1228800]{0:T(1024)}, f32[1228800]{0:T(1024)}, ...) | async-done | bytes 79953936
  (717 shorter events, 1066.8 us)
Async XLA Ops:
  7.2 745.2 %copy-start = (bf16[6,77,2048]{2,1,0:T(8,128)(2,1)S(1)}, bf16[6,77,2048]{2,1,0:T(8,128)(2,1)}, u32[]{:S(2)}) copy-start(bf16[6,77,2048]{2,1,0:T(8,128)(2,1)} %param.12) | copy-start | bytes 5677060
  7.2 344.3 %all-gather.43.cloned.1.call-start = ((), (), s32[]{:S(2)}) async-start(), calls=%async_computation.6 | async-start | bytes 5222400 | tf_op jit(solution)/shard_map/all_gather | solution.py:58
  11.1 469.3 %all-gather.51.cloned.1.call-start = ((), (), s32[]{:S(2)}) async-start(), calls=%async_computation.10 | async-start | bytes 5222400 | tf_op jit(solution)/shard_map/all_gather | solution.py:58
  11.9 527.8 %all-gather.35.cloned.1.call-start = ((), (), s32[]{:S(2)}) async-start(), calls=%async_computation.2 | async-start | bytes 2611200 | tf_op jit(solution)/shard_map/all_gather | solution.py:58
  36.5 508.8 %all-gather.49.cloned.1.call-start = ((), (), s32[]{:S(2)}) async-start(), calls=%async_computation.9 | async-start | bytes 6963200 | tf_op jit(solution)/shard_map/all_gather | solution.py:58
  37.1 585.9 %all-gather.31.cloned.1.call-start = ((), (), s32[]{:S(2)}) async-start(), calls=%async_computation | async-start | bytes 3481600 | tf_op jit(solution)/shard_map/all_gather | solution.py:58
  37.7 591.8 %all-gather.45.cloned.1.call-start = ((), (), s32[]{:S(2)}) async-start(), calls=%async_computation.7 | async-start | bytes 11141120 | tf_op jit(solution)/shard_map/all_gather | solution.py:58
  39.6 742.3 %all-gather.53.cloned.1.call-start = ((), (), s32[]{:S(2)}) async-start(), calls=%async_computation.11 | async-start | bytes 11141120 | tf_op jit(solution)/shard_map/all_gather | solution.py:58
  40.3 872.0 %all-gather.47.cloned.1.call-start = ((), (), s32[]{:S(2)}) async-start(), calls=%async_computation.8 | async-start | bytes 13926400 | tf_op jit(solution)/shard_map/all_gather | solution.py:58
  41.1 1174.9 %all-gather.55.cloned.1.call-start = ((), (), s32[]{:S(2)}) async-start(), calls=%async_computation.12 | async-start | bytes 13926400 | tf_op jit(solution)/shard_map/all_gather | solution.py:58
  41.8 1423.3 %all-gather.33.cloned.1.call-start = ((), (), s32[]{:S(2)}) async-start(), calls=%async_computation.1 | async-start | bytes 6963200 | tf_op jit(solution)/shard_map/all_gather | solution.py:58
  42.4 1760.9 %all-gather.41.cloned.1.call-start = ((), (), s32[]{:S(2)}) async-start(), calls=%async_computation.5 | async-start | bytes 2611200 | tf_op jit(solution)/shard_map/all_gather | solution.py:58
  80.9 330.0 %copy-start.170 = (f32[640]{0:T(1024)}, f32[640]{0:T(1024)S(1)}, u32[]{:S(2)}) copy-start(f32[640]{0:T(1024)S(1)} %get-tuple-element.90) | copy-start | bytes 7684
  81.0 330.0 %copy-start.182 = (f32[640]{0:T(1024)}, f32[640]{0:T(1024)S(1)}, u32[]{:S(2)}) copy-start(f32[640]{0:T(1024)S(1)} %get-tuple-element.89) | copy-start | bytes 7684
  81.0 391.3 %copy-start.161 = (f32[640]{0:T(1024)}, f32[640]{0:T(1024)S(1)}, u32[]{:S(2)}) copy-start(f32[640]{0:T(1024)S(1)} %get-tuple-element.87) | copy-start | bytes 7684
  81.0 391.3 %copy-start.184 = (f32[640]{0:T(1024)}, f32[640]{0:T(1024)S(1)}, u32[]{:S(2)}) copy-start(f32[640]{0:T(1024)S(1)} %get-tuple-element.86) | copy-start | bytes 7684
  81.0 981.6 %copy-start.120 = (f32[640]{0:T(1024)}, f32[640]{0:T(1024)S(1)}, u32[]{:S(2)}) copy-start(f32[640]{0:T(1024)S(1)} %get-tuple-element.83) | copy-start | bytes 7684
  81.0 981.6 %copy-start.133 = (f32[640]{0:T(1024)}, f32[640]{0:T(1024)S(1)}, u32[]{:S(2)}) copy-start(f32[640]{0:T(1024)S(1)} %get-tuple-element.84) | copy-start | bytes 7684
  82.9 328.0 %copy-start.139 = (f32[6,256]{1,0:T(8,128)}, f32[6,256]{1,0:T(8,128)S(1)}, u32[]{:S(2)}) copy-start(f32[6,256]{1,0:T(8,128)S(1)} %broadcast_multiply_fusion.5) | copy-start | bytes 18436
  1595.5 213.6 %all-gather.37.cloned.1.call-start = ((), (), s32[]{:S(2)}) async-start(), calls=%async_computation.3 | async-start | bytes 3481600 | tf_op jit(solution)/shard_map/all_gather | solution.py:58
  1596.1 294.4 %all-gather.39.cloned.1.call-start = ((), (), s32[]{:S(2)}) async-start(), calls=%async_computation.4 | async-start | bytes 6963200 | tf_op jit(solution)/shard_map/all_gather | solution.py:58
  1596.8 492.4 %all-gather.57.cloned.1.call-start = ((), (), s32[]{:S(2)}) async-start(), calls=%async_computation.13 | async-start | bytes 6963200 | tf_op jit(solution)/shard_map/all_gather | solution.py:58
  1597.4 583.2 %all-reduce.38.cloned.1.call-start = ((), (), s32[]{:S(2)}) async-start(), calls=%async_computation.14 | async-start | bytes 180224
  2047.7 890.6 %all-reduce.40.cloned.1.call-start = ((), (), s32[]{:S(2)}) async-start(), calls=%async_computation.15 | async-start | bytes 159907840
  (195 other events, 2570.4 us)
Sparse Core Ops, SparseCore 0:
  11.2 40.1 all-gather.42
  53.6 37.6 all-gather.50
  93.6 29.2 all-gather.34
  125.0 45.2 all-gather.48
  172.9 33.9 all-gather.30
  209.0 57.4 all-gather.44
  268.7 59.8 all-gather.52
  330.9 66.1 all-gather.46
  399.4 64.0 all-gather.54
  465.5 42.7 all-gather.32
  1595.6 28.9 all-gather.40
  1627.3 31.9 all-gather.36
  1662.1 47.2 all-gather.38
  1711.5 42.6 all-gather.56
  2047.8 64.7 all-reduce.37
  2119.5 818.7 all-reduce.39
where the time goes:
time: 2980 us; the launch traced here: 2970 us
  other arithmetic  1090 us (37%)
  waiting for transfers between devices  762 us (26%)
  matrix products  510 us (17%)
  local copies, waits for them, and re-layouts  362 us (12%)
  blocking collectives  226 us (8%)
    all_gather x14, other arithmetic, gather_block(): whole = lax.all_gather(shard, AXIS, axis=0, tiled=True)  861 us
    unnamed x18, waiting for transfers between devices  762 us
    all_gather x12, blocking collectives, gather_block(): whole = lax.all_gather(shard, AXIS, axis=0, tiled=True)  190 us
    dot_general x12, matrix products, project_back(): jnp.einsum('bte,de->btd', grads, weight, preferred_element_type=jnp.float32)  148 us
    reshape x26, local copies, waits for them, and re-layouts, gather_block(): full.append(whole[:math.prod(shape)].reshape(shape))  133 us
    dot_general x14, matrix products, weight_grad(): jnp.einsum('btd,bte->de', inputs, grads, preferred_element_type=jnp.float32)  120 us
    dot_general x14, matrix products, project(): jnp.einsum('btd,de->bte', inputs, weight, preferred_element_type=jnp.floa...  106 us
    dot_general x12, matrix products, attend(): jnp.einsum('bqhe,bkhe->bhqk', query, keys, preferred_element_type=jnp.flo...  82.8 us
  transfers between devices with their start and end apart: 16, of which 1 were waited for; matrix products, arithmetic and copies ran while one was open for 60% of the time, Pallas kernels for 0%

commit v1 on v0

--- a/solution.py
+++ b/solution.py
@@ -52,16 +52,18 @@
     return jnp.einsum('btd,bte->de', inputs, grads, preferred_element_type=jnp.float32)
 
 
-def gather_block(shards, width, ctx_width):
-    full = []
-    for shard, shape in zip(shards, weight_shapes(width, ctx_width)):
-        whole = lax.all_gather(shard, AXIS, axis=0, tiled=True)
-        full.append(whole[:math.prod(shape)].reshape(shape))
-    vec_flat = full[7]
-    return dict(w_qkv=full[0], w_out=full[1], w_q2=full[2], w_kv2=full[3], w_out2=full[4],
-                w_ff1=full[5], w_ff2=full[6],
-                rows=vec_flat[:9 * width].reshape(9, width).astype(jnp.float32),
-                bias_ff1=vec_flat[9 * width:].astype(jnp.float32))
+def gather_block(shards, width):
+    shapes = weight_shapes(width, shards[3].shape[0] * lax.axis_size(AXIS) // (2 * width))
+    n_dev = lax.axis_size(AXIS)
+    local = [shard.reshape(shape[0] // n_dev, shape[1]) for shard, shape in zip(shards[:7], shapes[:7])]
+    small = jnp.concatenate([local[1], local[2], local[4]], axis=1)
+    first = lax.all_gather(local[0], AXIS, axis=0, tiled=True)
+    small = lax.all_gather(small, AXIS, axis=0, tiled=True)
+    kv2 = lax.all_gather(local[3], AXIS, axis=0, tiled=True)
+    ff1 = lax.all_gather(local[5], AXIS, axis=0, tiled=True)
+    ff2 = lax.all_gather(local[6], AXIS, axis=0, tiled=True)
+    return dict(w_qkv=first, w_out=small[:, :width], w_q2=small[:, width:2 * width], w_kv2=kv2,
+                w_out2=small[:, 2 * width:], w_ff1=ff1, w_ff2=ff2)
 
 
 def block_forward(residual, context, weights):
@@ -128,12 +130,11 @@
     return grad, [g_qkv, g_out, g_q2, g_kv2, g_out2, g_ff1, g_ff2, g_vecs]
 
 
-def scatter_grads(grads, shard_lens, n_dev, total):
+def scatter_grads(grads, n_dev, total):
     result = []
-    for grad_full, shard_len in zip(grads, shard_lens):
-        flat = grad_full.reshape(-1)
-        flat = jnp.pad(flat, (0, shard_len * n_dev - flat.shape[0]))
-        result.append(lax.psum_scatter(flat, AXIS, scatter_dimension=0, tiled=True) / total)
+    for grad_full in grads[:7]:
+        shard = lax.psum_scatter(grad_full, AXIS, scatter_dimension=0, tiled=True)
+        result.append(shard.reshape(-1) / total)
     return result
 
 
@@ -142,25 +143,32 @@
 
     def local(tokens_x, context, cot_out, *shards):
         batch, tokens, width = tokens_x.shape
-        ctx_width = context.shape[-1]
         blocks = shards[0].shape[0]
-        shard_lens = [shard.shape[1] for shard in shards]
         total = batch * n_dev
         residual = tokens_x.astype(jnp.float32)
         saved_list = []
+        all_weights = []
+        vecs = lax.all_gather(shards[7].reshape(1, blocks, -1), AXIS, axis=0, tiled=True)
+        vecs = jnp.swapaxes(vecs, 0, 1).reshape(blocks, -1)
         for layer in range(blocks):
-            weights = gather_block([shard[layer] for shard in shards], width, ctx_width)
+            weights = gather_block([shard[layer] for shard in shards[:7]], width)
+            weights['rows'] = vecs[layer, :9 * width].reshape(9, width).astype(jnp.float32)
+            weights['bias_ff1'] = vecs[layer, 9 * width:17 * width].astype(jnp.float32)
             residual, saved = block_forward(residual, context, weights)
             saved_list.append(saved)
+            all_weights.append(weights)
         grad = cot_out.astype(jnp.float32)
         grad_shards = []
+        vec_grads = []
         for layer in reversed(range(blocks)):
-            grad, layer_shards = lax.optimization_barrier((grad, [shard[layer] for shard in shards]))
-            weights = gather_block(layer_shards, width, ctx_width)
-            grad, block_grads = block_backward(grad, context, weights, saved_list[layer])
-            grad_shards.insert(0, scatter_grads(block_grads, shard_lens, n_dev, total))
-        stacked = [jnp.stack([per_layer[index] for per_layer in grad_shards]) for index in range(len(shards))]
-        return tuple([residual.astype(jnp.bfloat16), grad.astype(jnp.bfloat16)] + stacked)
+            grad, block_grads = block_backward(grad, context, all_weights[layer], saved_list[layer])
+            grad_shards.insert(0, scatter_grads(block_grads, n_dev, total))
+            vec_grads.insert(0, block_grads[7])
+        vec = jnp.stack(vec_grads)
+        length = shards[7].shape[1]
+        vec = lax.psum_scatter(vec.reshape(blocks, n_dev, length), AXIS, scatter_dimension=1, tiled=False) / total
+        stacked = [jnp.stack([per_layer[index] for per_layer in grad_shards]) for index in range(7)]
+        return tuple([residual.astype(jnp.bfloat16), grad.astype(jnp.bfloat16)] + stacked + [vec])
 
     param_spec = P(None, AXIS)
     in_specs = (P(AXIS), P(AXIS), P(AXIS)) + (param_spec,) * 8

time: 2980 us -> 1980 us (0.66)
  other arithmetic: 1090 us -> 220 us
  waiting for transfers between devices: 762 us -> 1020 us
  local copies, waits for them, and re-layouts: 362 us -> 149 us
  blocking collectives: 226 us -> 14.5 us
  matrix products: 510 us -> 548 us
    all_gather x14 -> x0, other arithmetic: 861 us -> none  [gather_block(): whole = lax.all_gather(shard, AXIS, axis=0, tiled=True)]
    reduce_scatter x0 -> x6, waiting for transfers between devices: none -> 645 us  [scatter_grads(): shard = lax.psum_scatter(grad_full, AXIS, scatter_dimension=0, tiled=True)]
    unnamed x18 -> x34, waiting for transfers between devices: 762 us -> 359 us
    reshape x38 -> x1, local copies, waits for them, and re-layouts: 197 us -> 0.18 us  [local(): vecs = jnp.swapaxes(vecs, 0, 1).reshape(blocks, -1)]
    all_gather x12 -> x1, blocking collectives: 190 us -> 14.5 us  [local(): lax.all_gather(shards[7].reshape(1, blocks, -1), AXIS, axis=0, tiled=True)]
    unnamed x1 -> x0, blocking collectives: 35.7 us -> none
    unnamed x432 -> x378, local copies, waits for them, and re-layouts: 66.2 us -> 52.7 us
  transfers between devices with their start and end apart: 16 -> 25, of which waited for: 1 -> 14; matrix products, arithmetic and copies ran while one was open for 60% -> 26% of each run, Pallas kernels for 0% -> 0%
where the time goes in v1:
time: 1980 us; the launch traced here: 1970 us
  waiting for transfers between devices  1020 us (52%)
  matrix products  548 us (28%)
  other arithmetic  220 us (11%)
  local copies, waits for them, and re-layouts  149 us (8%)
    reduce_scatter x6, waiting for transfers between devices, scatter_grads(): shard = lax.psum_scatter(grad_full, AXIS, scatter_dimension=0, tiled=True)  645 us
    unnamed x34, waiting for transfers between devices  359 us
    dot_general x12, matrix products, project_back(): jnp.einsum('bte,de->btd', grads, weight, preferred_element_type=jnp.float32)  156 us
    dot_general x14, matrix products, weight_grad(): jnp.einsum('btd,bte->de', inputs, grads, preferred_element_type=jnp.float32)  132 us
    dot_general x14, matrix products, project(): jnp.einsum('btd,de->bte', inputs, weight, preferred_element_type=jnp.floa...  121 us
    dot_general x12, matrix products, attend(): jnp.einsum('bqhe,bkhe->bhqk', query, keys, preferred_element_type=jnp.flo...  84.8 us
    dot_general x12, matrix products, attend(): jnp.einsum('bhqk,bkhe->bqhe', probabilities, values, preferred_element_ty...  55.5 us
    unnamed x378, local copies, waits for them, and re-layouts  52.7 us
  transfers between devices with their start and end apart: 25, of which 14 were waited for; matrix products, arithmetic and copies ran while one was open for 26% of the time, Pallas kernels for 0%

profile of v1, /device:TPU:0, one launch (start us, length us, event | category | flops | bytes accessed | tf_op | source)
XLA Modules:
  0.0 1970.0 jit_solution(9113957717719362023)
XLA Ops:
  104.0 18.0 fusion.168
  204.9 22.2 %broadcast_add_fusion.1 = f32[6,256,5120]{2,1,0:T(8,128)} fusion(f32[5120]{0:T(1024)S(1)} %bitcast.458, bf16[640,5120]{1,0:T(8,128)(2,1)} %all-gather.19.cloned.1.call-done, f32[6,256,640]{2,1,0:T(8,128)} %copy-done.9, f32[640]{0:T(1024)S(1)} %get-tuple-element.60, f32[640]{0:T(1024)S(1)} %get-tuple-element.58, f32[6,256]{1,0:T(8,128)S(1)} %fusion.135, ...), kind=kOutput, calls=%fused_computation.63 | convolution fusion | flops 10079109120 | bytes 41980928 | tf_op jit(solution)/shard_map/btd,de->bte/dot_general | solution.py:44
  227.1 37.4 %multiply_convert_fusion.1 = (bf16[6,256,2560]{2,1,0:T(8,128)(2,1)}, f32[6,256,2560]{2,1,0:T(8,128)}) fusion(f32[6,256,5120]{2,1,0:T(8,128)} %broadcast_add_fusion.1), kind=kLoop, calls=%fused_computation.50 | loop fusion | flops 259522560 | bytes 55050240 | tf_op jit(solution)/shard_map/jvp()/convert_element_type | solution.py:40
  306.0 18.0 fusion.173
  377.8 21.8 %broadcast_add_fusion = f32[6,256,5120]{2,1,0:T(8,128)} fusion(f32[5120]{0:T(1024)S(1)} %bitcast.457, bf16[640,5120]{1,0:T(8,128)(2,1)} %all-gather.29.cloned.1.call-done, f32[6,256,640]{2,1,0:T(8,128)} %copy-done.17, f32[640]{0:T(1024)S(1)} %copy-done.94, f32[640]{0:T(1024)S(1)} %copy-done.84, f32[6,256]{1,0:T(8,128)S(1)} %fusion.138, ...), kind=kOutput, calls=%fused_computation.47 | convolution fusion | flops 10079109120 | bytes 41980928 | tf_op jit(solution)/shard_map/btd,de->bte/dot_general | solution.py:44
  399.6 46.0 %multiply_add_fusion.1 = (f32[6,256,2560]{2,1,0:T(8,128)}, f32[6,256,2560]{2,1,0:T(8,128)S(1)}, bf16[6,256,2560]{2,1,0:T(8,128)(2,1)}) fusion(f32[6,256,5120]{2,1,0:T(8,128)} %broadcast_add_fusion, bf16[6,256,640]{2,1,0:T(8,128)(2,1)} %param.13, bf16[2560,640]{1,0:T(8,128)(2,1)} %all-gather.31.cloned.1.call-done), kind=kOutput, calls=%fused_computation.33 | convolution fusion | flops 5324144640 | bytes 76021760 | tf_op jit(solution)/shard_map/bte,de->btd/dot_general | solution.py:48
  445.6 21.1 %convert_multiply_fusion.4 = (f32[6,256,2560]{2,1,0:T(8,128)}, bf16[6,256,2560]{2,1,0:T(8,128)(2,1)}) fusion(bf16[6,256,2560]{2,1,0:T(8,128)(2,1)} %get-tuple-element.109, f32[6,256,2560]{2,1,0:T(8,128)S(1)} %get-tuple-element.78, f32[6,256,5120]{2,1,0:T(8,128)} %broadcast_add_fusion), kind=kLoop, calls=%fused_computation.18 | loop fusion | flops 23592960 | bytes 78643200 | tf_op jit(solution)/shard_map/transpose(jvp())/mul | solution.py:40
  466.7 21.6 %multiply_reduce_fusion.4 = (f32[640]{0:T(1024)}, f32[6,256]{1,0:T(8,128)S(1)}, f32[640]{0:T(1024)}, f32[6,256,640]{2,1,0:T(8,128)}) fusion(f32[6,256,640]{2,1,0:T(8,128)} %copy-done.17, f32[6,256]{1,0:T(8,128)S(1)} %fusion.138, f32[6,256]{1,0:T(8,128)S(1)} %broadcast_multiply_fusion.2, f32[640]{0:T(1024)S(1)} %copy-done.84, ...), kind=kOutput, calls=%fused_computation.147 | convolution fusion | flops 10089919488 | bytes 45901312 | tf_op jit(solution)/shard_map/bte,de->btd/dot_general | solution.py:48
  585.9 29.0 %multiply_add_fusion = (f32[6,256,2560]{2,1,0:T(8,128)}, f32[6,256,2560]{2,1,0:T(8,128)}) fusion(f32[6,256,2560]{2,1,0:T(8,128)} %get-tuple-element.80, f32[6,256,5120]{2,1,0:T(8,128)} %broadcast_add_fusion.1, bf16[2560,640]{1,0:T(8,128)(2,1)} %all-gather.21.cloned.1.call-done, f32[6,256,640]{2,1,0:T(8,128)S(1)} %get-tuple-element.68), kind=kOutput, calls=%fused_computation.32 | convolution fusion | flops 5104926720 | bytes 85852160 | tf_op jit(solution)/shard_map/bte,de->btd/dot_general | solution.py:48
  615.0 20.9 %fusion.156 = (f32[640]{0:T(1024)S(1)}, f32[6,256]{1,0:T(8,128)S(1)}, f32[6,256,640]{2,1,0:T(8,128)}) fusion(f32[640]{0:T(1024)S(1)} %copy-done.80, f32[6,256,640]{2,1,0:T(8,128)} %copy-done.9, f32[6,256]{1,0:T(8,128)S(1)} %copy-done.65, bf16[640,5120]{1,0:T(8,128)(2,1)} %all-gather.19.cloned.1.call-done, f32[6,256,2560]{2,1,0:T(8,128)} %get-tuple-element.82, ...), kind=kOutput, calls=%fused_computation.392 | convolution fusion | flops 10086971392 | bytes 45892608 | tf_op jit(solution)/shard_map/bte,de->btd/dot_general | solution.py:48
  866.4 21.1 %convolution_bitcast_fusion = f32[640,5120]{1,0:T(8,128)} fusion(f32[6,256,2560]{2,1,0:T(8,128)} %get-tuple-element.83, f32[6,256,2560]{2,1,0:T(8,128)} %get-tuple-element.77, f32[6,256,640]{2,1,0:T(8,128)} %copy-done.17, f32[640]{0:T(1024)S(1)} %copy-done.95, f32[640]{0:T(1024)S(1)} %copy-done.85, f32[6,256]{1,0:T(8,128)S(1)} %copy-done.74, ...), kind=kOutput, calls=%fused_computation.76 | convolution fusion | flops 10086973440 | bytes 48514048 | tf_op jit(solution)/shard_map/btd,bte->de/dot_general | solution.py:52
  893.5 21.2 %convolution_bitcast_fusion.1 = f32[640,5120]{1,0:T(8,128)} fusion(f32[6,256,2560]{2,1,0:T(8,128)} %get-tuple-element.82, f32[6,256,2560]{2,1,0:T(8,128)} %get-tuple-element.81, f32[6,256,640]{2,1,0:T(8,128)} %copy-done.9, f32[640]{0:T(1024)S(1)} %copy-done.93, f32[640]{0:T(1024)S(1)} %copy-done.81, f32[6,256]{1,0:T(8,128)S(1)} %copy-done.69, ...), kind=kOutput, calls=%fused_computation.77 | convolution fusion | flops 10086973440 | bytes 48514048 | tf_op jit(solution)/shard_map/btd,bte->de/dot_general | solution.py:52
  938.9 56.2 %reduce-scatter.59.cloned.1.call-done = f32[40,640]{1,0:T(8,128)} async-done(((f32[640,640]{1,0:T(8,128)}), f32[40,640]{1,0:T(8,128)}) %reduce-scatter.59.cloned.1.call-update) | async-done | bytes 102416
  996.1 56.1 %reduce-scatter.57.cloned.1.call-done = f32[40,640]{1,0:T(8,128)} async-done(((f32[640,640]{1,0:T(8,128)}), f32[40,640]{1,0:T(8,128)}) %reduce-scatter.57.cloned.1.call-update) | async-done | bytes 102416
  1053.2 56.1 %reduce-scatter.63.cloned.1.call-done = f32[40,640]{1,0:T(8,128)} async-done(((f32[640,640]{1,0:T(8,128)}), f32[40,640]{1,0:T(8,128)}) %reduce-scatter.63.cloned.1.call-update) | async-done | bytes 102416
  1110.3 56.1 %reduce-scatter.61.cloned.1.call-done = f32[40,640]{1,0:T(8,128)} async-done(((f32[640,640]{1,0:T(8,128)}), f32[40,640]{1,0:T(8,128)}) %reduce-scatter.61.cloned.1.call-update) | async-done | bytes 102416
  1169.4 60.8 %reduce-scatter.51.cloned.1.call-done = f32[40,1920]{1,0:T(8,128)} async-done(((f32[640,1920]{1,0:T(8,128)}), f32[40,1920]{1,0:T(8,128)}) %reduce-scatter.51.cloned.1.call-update) | async-done | bytes 307216
  1231.5 64.4 %reduce-scatter.49.cloned.1.call-done = f32[40,1920]{1,0:T(8,128)} async-done(((f32[640,1920]{1,0:T(8,128)}), f32[40,1920]{1,0:T(8,128)}) %reduce-scatter.49.cloned.1.call-update) | async-done | bytes 307216
  1298.6 73.7 %reduce-scatter.47.cloned.1.call-done = f32[160,640]{1,0:T(8,128)} async-done(((f32[2560,640]{1,0:T(8,128)}), f32[160,640]{1,0:T(8,128)}) %reduce-scatter.47.cloned.1.call-update) | async-done | bytes 409616 | tf_op jit(solution)/shard_map/reduce_scatter | solution.py:136
  1373.8 74.0 %reduce-scatter.45.cloned.1.call-done = f32[160,640]{1,0:T(8,128)} async-done(((f32[2560,640]{1,0:T(8,128)}), f32[160,640]{1,0:T(8,128)}) %reduce-scatter.45.cloned.1.call-update) | async-done | bytes 409616 | tf_op jit(solution)/shard_map/reduce_scatter | solution.py:136
  1450.8 112.0 %reduce-scatter.39.cloned.1.call-done = f32[128,1280]{0,1:T(8,128)} async-done(((f32[2048,1280]{0,1:T(8,128)}), f32[128,1280]{0,1:T(8,128)}) %reduce-scatter.39.cloned.1.call-update) | async-done | bytes 655376 | tf_op jit(solution)/shard_map/reduce_scatter | solution.py:136
  1564.9 112.3 %reduce-scatter.37.cloned.1.call-done = f32[128,1280]{0,1:T(8,128)} async-done(((f32[2048,1280]{0,1:T(8,128)}), f32[128,1280]{0,1:T(8,128)}) %reduce-scatter.37.cloned.1.call-update) | async-done | bytes 655376 | tf_op jit(solution)/shard_map/reduce_scatter | solution.py:136
  1683.3 134.6 %reduce-scatter.43.cloned.1.call-done = f32[40,5120]{1,0:T(8,128)} async-done(((f32[640,5120]{1,0:T(8,128)}), f32[40,5120]{1,0:T(8,128)}) %reduce-scatter.43.cloned.1.call-update) | async-done | bytes 819216 | tf_op jit(solution)/shard_map/reduce_scatter | solution.py:136
  1820.0 138.8 %reduce-scatter.41.cloned.1.call-done = f32[40,5120]{1,0:T(8,128)} async-done(((f32[640,5120]{1,0:T(8,128)}), f32[40,5120]{1,0:T(8,128)}) %reduce-scatter.41.cloned.1.call-update) | async-done | bytes 819216 | tf_op jit(solution)/shard_map/reduce_scatter | solution.py:136
  (638 shorter events, 659.8 us)
Async XLA Ops:
  12.7 124.2 %all-gather.15.cloned.1.call-start = ((), (), s32[]{:S(2)}) async-start(), calls=%async_computation.15 | async-start | bytes 2611200 | tf_op jit(solution)/shard_map/all_gather | solution.py:61
  23.8 128.9 %all-gather.17.cloned.1.call-start = ((), (), s32[]{:S(2)}) async-start(), calls=%async_computation.16 | async-start | bytes 5570560 | tf_op jit(solution)/shard_map/all_gather | solution.py:62
  33.7 149.0 %all-gather.27.cloned.1.call-start = ((), (), s32[]{:S(2)}) async-start(), calls=%async_computation.21 | async-start | bytes 5570560 | tf_op jit(solution)/shard_map/all_gather | solution.py:62
  35.9 169.0 %all-gather.19.cloned.1.call-start = ((), (), s32[]{:S(2)}) async-start(), calls=%async_computation.17 | async-start | bytes 6963200 | tf_op jit(solution)/shard_map/all_gather | solution.py:63
  47.8 216.7 %all-gather.21.cloned.1.call-start = ((), (), s32[]{:S(2)}) async-start(), calls=%async_computation.18 | async-start | bytes 3481600 | tf_op jit(solution)/shard_map/all_gather | solution.py:64
  52.1 226.0 %all-gather.23.cloned.1.call-start = ((), (), s32[]{:S(2)}) async-start(), calls=%async_computation.19 | async-start | bytes 2611200 | tf_op jit(solution)/shard_map/all_gather | solution.py:60
  53.0 285.1 %all-gather.25.cloned.1.call-start = ((), (), s32[]{:S(2)}) async-start(), calls=%async_computation.20 | async-start | bytes 2611200 | tf_op jit(solution)/shard_map/all_gather | solution.py:61
  54.0 323.9 %all-gather.29.cloned.1.call-start = ((), (), s32[]{:S(2)}) async-start(), calls=%async_computation.22 | async-start | bytes 6963200 | tf_op jit(solution)/shard_map/all_gather | solution.py:63
  55.0 344.6 %all-gather.31.cloned.1.call-start = ((), (), s32[]{:S(2)}) async-start(), calls=%async_computation.23 | async-start | bytes 3481600 | tf_op jit(solution)/shard_map/all_gather | solution.py:64
  55.9 870.8 %all-reduce.25.cloned.1.call-start = ((), (), s32[]{:S(2)}) async-start(), calls=%async_computation.30 | async-start | bytes 196608
  757.8 170.2 %reduce-scatter.55.cloned.1.call-start = ((), (), s32[]{:S(2)}) async-start(), calls=%async_computation.34 | async-start | bytes 1740800
  763.4 174.5 %reduce-scatter.53.cloned.1.call-start = ((), (), s32[]{:S(2)}) async-start(), calls=%async_computation.33 | async-start | bytes 1740800
  769.2 225.9 %reduce-scatter.59.cloned.1.call-start = ((), (), s32[]{:S(2)}) async-start(), calls=%async_computation.36 | async-start | bytes 1740800
  775.7 276.5 %reduce-scatter.57.cloned.1.call-start = ((), (), s32[]{:S(2)}) async-start(), calls=%async_computation.35 | async-start | bytes 1740800
  782.0 327.3 %reduce-scatter.63.cloned.1.call-start = ((), (), s32[]{:S(2)}) async-start(), calls=%async_computation.38 | async-start | bytes 1740800
  787.1 379.3 %reduce-scatter.61.cloned.1.call-start = ((), (), s32[]{:S(2)}) async-start(), calls=%async_computation.37 | async-start | bytes 1740800
  792.7 437.5 %reduce-scatter.51.cloned.1.call-start = ((), (), s32[]{:S(2)}) async-start(), calls=%async_computation.32 | async-start | bytes 5222400
  803.8 492.1 %reduce-scatter.49.cloned.1.call-start = ((), (), s32[]{:S(2)}) async-start(), calls=%async_computation.31 | async-start | bytes 5222400
  814.7 557.6 %reduce-scatter.47.cloned.1.call-start = ((), (), s32[]{:S(2)}) async-start(), calls=%async_computation.29 | async-start | bytes 6963200 | tf_op jit(solution)/shard_map/reduce_scatter | solution.py:136
  825.8 621.9 %reduce-scatter.45.cloned.1.call-start = ((), (), s32[]{:S(2)}) async-start(), calls=%async_computation.28 | async-start | bytes 6963200 | tf_op jit(solution)/shard_map/reduce_scatter | solution.py:136
  837.5 725.3 %reduce-scatter.39.cloned.1.call-start = ((), (), s32[]{:S(2)}) async-start(), calls=%async_computation.25 | async-start | bytes 11141120 | tf_op jit(solution)/shard_map/reduce_scatter | solution.py:136
  851.9 825.4 %reduce-scatter.37.cloned.1.call-start = ((), (), s32[]{:S(2)}) async-start(), calls=%async_computation.24 | async-start | bytes 11141120 | tf_op jit(solution)/shard_map/reduce_scatter | solution.py:136
  865.7 952.2 %reduce-scatter.43.cloned.1.call-start = ((), (), s32[]{:S(2)}) async-start(), calls=%async_computation.27 | async-start | bytes 13926400 | tf_op jit(solution)/shard_map/reduce_scatter | solution.py:136
  887.6 1071.1 %reduce-scatter.41.cloned.1.call-start = ((), (), s32[]{:S(2)}) async-start(), calls=%async_computation.26 | async-start | bytes 13926400 | tf_op jit(solution)/shard_map/reduce_scatter | solution.py:136
  (174 other events, 2468.8 us)
Sparse Core Ops, SparseCore 0:
  12.8 32.1 all-gather.12
  47.8 29.3 all-gather.14
  80.0 38.3 all-gather.16
  121.1 38.3 all-gather.26
  162.1 42.7 all-gather.18
  207.5 31.9 all-gather.20
  241.8 29.3 all-gather.22
  305.5 42.6 all-gather.28
  350.9 31.9 all-gather.30
  757.9 64.8 all-reduce.24
  825.5 55.1 reduce-scatter.54
  882.9 54.9 reduce-scatter.52
  940.0 55.0 reduce-scatter.58
  997.2 54.9 reduce-scatter.56
  1054.3 54.9 reduce-scatter.62
  1111.4 54.9 reduce-scatter.60
  1170.8 59.3 reduce-scatter.50
  1234.7 61.1 reduce-scatter.48
  1298.0 74.2 reduce-scatter.46
  1374.6 73.1 reduce-scatter.44
  1450.0 112.7 reduce-scatter.38
  1565.1 112.0 reduce-scatter.36
  1679.4 138.4 reduce-scatter.42
  1820.2 138.4 reduce-scatter.40
  (1 shorter events, 29.2 us)

commit v2 on v0

v2 whole, which is shorter than its diff:
```python
import math
import jax
import jax.numpy as jnp
from jax import lax
from jax.experimental import pallas as pl
from jax.experimental.pallas import tpu as pltpu
from jax.sharding import PartitionSpec as P

AXIS = 'fsdp'
HEAD = 64
EPS = 1e-5
F32 = jnp.float32
BF16 = jnp.bfloat16
LANES = 128
SLOT = 128
PAIR_ROWS = 512
FF_COLS = 256

TAIL_P = 0.265
TAIL = (0.10574158579953814, 0.10524628753634038, 0.10270369607548423, 0.0603023517537824, 0.13797880111692826,
        -0.11640058407079061, 0.2178489286936914, -0.1442454807654402, 0.03082441619112092)


def weight_shapes(width, ctx_width):
    return ((width, 3 * width), (width, width), (width, width), (ctx_width, 2 * width),
            (width, width), (width, 8 * width), (4 * width, width), (17 * width,))


def mm(lhs, rhs):
    return jnp.dot(lhs, rhs, preferred_element_type=F32)


def mm_nt(lhs, rhs):
    return lax.dot_general(lhs, rhs, (((1,), (1,)), ((), ())), preferred_element_type=F32)


def mm_tn(lhs, rhs):
    return lax.dot_general(lhs, rhs, (((0,), (0,)), ((), ())), preferred_element_type=F32)


def normalize(x):
    centered = x - jnp.mean(x, axis=-1, keepdims=True)
    scale = lax.rsqrt(jnp.mean(centered * centered, axis=-1, keepdims=True) + EPS)
    return centered * scale, scale


def norm_back(x, d_norm, gain):
    hat, scale = normalize(x)
    d_hat = d_norm * gain
    pulled = d_hat - jnp.mean(d_hat, axis=-1, keepdims=True) - hat * jnp.mean(d_hat * hat, axis=-1, keepdims=True)
    return pulled * scale, jnp.sum(d_norm * hat, axis=0, keepdims=True), jnp.sum(d_norm, axis=0, keepdims=True)


def low_half(rows):
    return lax.broadcasted_iota(jnp.int32, (rows, LANES), 1) < HEAD


def head_stack(pair, low):
    zero = jnp.zeros_like(pair)
    return jnp.concatenate([jnp.where(low, pair, zero), jnp.where(low, zero, pair)], axis=0)


def head_unstack(stacked, low):
    half = stacked.shape[0] // 2
    return jnp.where(low, stacked[:half], stacked[half:])


def softmax_halves(scores, valid):
    half = scores.shape[1] // 2
    parts = []
    for index in range(2):
        part = scores[:, index * half:(index + 1) * half]
        if valid < half:
            part = jnp.where(lax.broadcasted_iota(jnp.int32, part.shape, 1) < valid, part, -jnp.inf)
        part = jnp.exp(part - jnp.max(part, axis=-1, keepdims=True))
        parts.append(part * (1.0 / jnp.sum(part, axis=-1, keepdims=True)))
    return parts


def pair_forward(query, keys, values, valid):
    low = low_half(keys.shape[0])
    scores = mm_nt(query * BF16(HEAD ** -0.5), head_stack(keys, low))
    probs = jnp.concatenate([part.astype(BF16) for part in softmax_halves(scores, valid)], axis=1)
    return mm(probs, head_stack(values, low)).astype(BF16)


def pair_backward(query, keys, values, d_out, valid):
    low = low_half(keys.shape[0])
    half = keys.shape[0]
    query = query * BF16(HEAD ** -0.5)
    key_stack = head_stack(keys, low)
    value_stack = head_stack(values, low)
    parts = softmax_halves(mm_nt(query, key_stack), valid)
    probs = jnp.concatenate([part.astype(BF16) for part in parts], axis=1)
    d_values = head_unstack(mm_tn(probs, d_out), low).astype(BF16)
    d_probs = mm_nt(d_out, value_stack)
    d_scores = []
    for index in range(2):
        part, d_part = parts[index], d_probs[:, index * half:(index + 1) * half]
        d_scores.append((part * (d_part - jnp.sum(part * d_part, axis=-1, keepdims=True))).astype(BF16))
    d_scores = jnp.concatenate(d_scores, axis=1)
    d_query = (mm(d_scores, key_stack) * HEAD ** -0.5).astype(BF16)
    d_keys = head_unstack(mm_tn(d_scores, query), low).astype(BF16)
    return d_query, d_keys, d_values


def self_forward_kernel(heads, tokens, h_ref, w_qkv_ref, w_out_ref, rows_ref, h1_ref, qkv_ref, out_ref):
    width = heads * HEAD
    hat, unused = normalize(h_ref[...].astype(F32))
    norm1 = (hat * rows_ref[0:1] + rows_ref[1:2]).astype(BF16)
    qkv_ref[...] = mm(norm1, w_qkv_ref[...]).astype(BF16)

    def sample(index, carry):
        rows = pl.ds(pl.multiple_of(index * tokens, tokens), tokens)
        for pair in range(heads // 2):
            cols = pair * LANES
            out_ref[rows, cols:cols + LANES] = pair_forward(
                qkv_ref[rows, cols:cols + LANES], qkv_ref[rows, width + cols:width + cols + LANES],
                qkv_ref[rows, 2 * width + cols:2 * width + cols + LANES], tokens)
        return carry

    lax.fori_loop(0, h_ref.shape[0] // tokens, sample, 0)
    h1_ref[...] = h_ref[...].astype(F32) + mm(out_ref[...], w_out_ref[...]) + rows_ref[6:7]


def cross_forward_kernel(heads, tokens, ctx_len, h1_ref, context_ref, w_q_ref, w_kv_ref, w_out_ref, rows_ref,
                         h2_ref, q_ref, kv_ref, out_ref):
    width = heads * HEAD
    samples = kv_ref.shape[0] // SLOT
    pad = context_ref.shape[0] // samples
    step = pl.program_id(0)

    @pl.when(step == 0)
    def _():
        kv = mm(context_ref[...], w_kv_ref[...]).astype(BF16)
        for index in range(samples):
            kv_ref[index * SLOT:index * SLOT + pad] = kv[index * pad:(index + 1) * pad]
            kv_ref[index * SLOT + pad:(index + 1) * SLOT] = jnp.zeros((SLOT - pad, 2 * width), BF16)

    hat, unused = normalize(h1_ref[...])
    norm2 = (hat * rows_ref[2:3] + rows_ref[3:4]).astype(BF16)
    q_ref[...] = mm(norm2, w_q_ref[...]).astype(BF16)
    per_step = h1_ref.shape[0] // tokens

    def sample(index, carry):
        rows = pl.ds(pl.multiple_of(index * tokens, tokens), tokens)
        kv_rows = pl.ds(pl.multiple_of((step * per_step + index) * SLOT, SLOT), SLOT)
        for pair in range(heads // 2):
            cols = pair * LANES
            out_ref[rows, cols:cols + LANES] = pair_forward(
                q_ref[rows, cols:cols + LANES], kv_ref[kv_rows, cols:cols + LANES],
                kv_ref[kv_rows, width + cols:width + cols + LANES], ctx_len)
        return carry

    lax.fori_loop(0, per_step, sample, 0)
    h2_ref[...] = h1_ref[...] + mm(out_ref[...], w_out_ref[...]) + rows_ref[7:8]


def normal_cdf(u):
    t = 1.0 / (1.0 + TAIL_P * jnp.abs(u))
    poly = TAIL[-1]
    for coef in TAIL[-2::-1]:
        poly = poly * t + coef
    bell = jnp.exp(u * u * -0.5)
    tail = bell * (t * poly)
    return jnp.where(u >= 0, 1.0 - tail, tail), bell


def ff_forward_kernel(chunk, h2_ref, w1a_ref, w1g_ref, w2_ref, b1a_ref, b1g_ref, rows_ref,
                      h3_ref, fa_ref, fg_ref, z_ref, norm_ref, acc_ref):
    step = pl.program_id(0)
    chunks = h2_ref.shape[0] // chunk

    @pl.when(step == 0)
    def _():
        def start(index, carry):
            rows = pl.ds(pl.multiple_of(index * chunk, chunk), chunk)
            hat, unused = normalize(h2_ref[rows])
            norm_ref[rows] = (hat * rows_ref[4:5] + rows_ref[5:6]).astype(BF16)
            acc_ref[rows] = jnp.zeros((chunk, h2_ref.shape[1]), F32)
            return carry

        lax.fori_loop(0, chunks, start, 0)

    def body(index, carry):
        rows = pl.ds(pl.multiple_of(index * chunk, chunk), chunk)
        norm3 = norm_ref[rows]
        gate = mm(norm3, w1g_ref[...]) + b1g_ref[...]
        cdf, bell = normal_cdf(gate)
        factor = gate * cdf
        value = mm(norm3, w1a_ref[...]) + b1a_ref[...]
        z = (value * factor).astype(BF16)
        z_ref[0, rows] = z
        fa_ref[0, rows] = factor
        fg_ref[0, rows] = value * (cdf + gate * bell * (2 * math.pi) ** -0.5)
        acc_ref[rows] += mm(z, w2_ref[...])
        return carry

    lax.fori_loop(0, chunks, body, 0)

    @pl.when(step == pl.num_programs(0) - 1)
    def _():
        h3_ref[...] = h2_ref[...] + acc_ref[...] + rows_ref[8:9]


def ff_backward_kernel(chunk, grad_ref, h2_ref, w1a_ref, w1g_ref, w2_ref, fa_ref, fg_ref, z_ref, rows_ref,
                       out_ref, d_w1a_ref, d_w1g_ref, d_w2_ref, d_b1_ref, d_rows_ref,
                       norm_t_ref, grad_bf_ref, du_ref, w1_ref, acc_ref):
    step = pl.program_id(0)
    chunks = h2_ref.shape[0] // chunk
    cols = fa_ref.shape[2]

    @pl.when(step == 0)
    def _():
        d_rows_ref[...] = jnp.zeros_like(d_rows_ref)

        def start(index, carry):
            rows = pl.ds(pl.multiple_of(index * chunk, chunk), chunk)
            hat, unused = normalize(h2_ref[rows])
            norm_t_ref[:, rows] = (hat * rows_ref[4:5] + rows_ref[5:6]).astype(BF16).T
            grad_bf_ref[rows] = grad_ref[rows].astype(BF16)
            d_rows_ref[8:9] += jnp.sum(grad_ref[rows], axis=0, keepdims=True)
            acc_ref[rows] = jnp.zeros((chunk, h2_ref.shape[1]), F32)
            return carry

        lax.fori_loop(0, chunks, start, 0)

    w1_ref[:, :cols] = w1a_ref[...]
    w1_ref[:, cols:] = w1g_ref[...]

    def body(index, sums):
        rows = pl.ds(pl.multiple_of(index * chunk, chunk), chunk)
        dz = mm_nt(grad_bf_ref[rows], w2_ref[...]).astype(BF16).astype(F32)
        du_a = dz * fa_ref[0, rows]
        du_g = dz * fg_ref[0, rows]
        du_ref[rows, :cols] = du_a.astype(BF16)
        du_ref[rows, cols:] = du_g.astype(BF16)
        acc_ref[rows] += mm_nt(du_ref[rows], w1_ref[...])
        return (sums[0] + jnp.sum(du_a, axis=0, keepdims=True), sums[1] + jnp.sum(du_g, axis=0, keepdims=True))

    zero = jnp.zeros((1, cols), F32)
    sum_a, sum_g = lax.fori_loop(0, chunks, body, (zero, zero))
    d_b1_ref[0, 0:1] = sum_a
    d_b1_ref[0, 1:2] = sum_g
    d_w1a_ref[...] = mm(norm_t_ref[...], du_ref[:, :cols])
    d_w1g_ref[...] = mm(norm_t_ref[...], du_ref[:, cols:])
    d_w2_ref[...] = mm_tn(z_ref[0], grad_bf_ref[...])

    @pl.when(step == pl.num_programs(0) - 1)
    def _():
        def finish(index, carry):
            rows = pl.ds(pl.multiple_of(index * chunk, chunk), chunk)
            d_res, d_gain, d_shift = norm_back(h2_ref[rows], acc_ref[rows], rows_ref[4:5])
            out_ref[rows] = grad_ref[rows] + d_res
            d_rows_ref[4:5] += d_gain
            d_rows_ref[5:6] += d_shift
            return carry

        lax.fori_loop(0, chunks, finish, 0)


def cross_backward_kernel(heads, tokens, ctx_len, row_steps, grad_ref, h1_ref, q_ref, out2_ref, kv_ref, context_ref,
                          w_q_ref, w_out_ref, rows_ref, out_ref, d_wq_ref, d_wout_ref, d_wkv_ref, d_rows_ref,
                          d_mix_ref, d_q_ref, d_kv_ref):
    width = heads * HEAD
    step = pl.program_id(0)
    pad = context_ref.shape[0] // (kv_ref.shape[0] // SLOT)
    per_step = h1_ref.shape[0] // tokens

    @pl.when(step == 0)
    def _():
        d_rows_ref[...] = jnp.zeros_like(d_rows_ref)
        d_wq_ref[...] = jnp.zeros_like(d_wq_ref)
        d_wout_ref[...] = jnp.zeros_like(d_wout_ref)

    @pl.when(step < row_steps)
    def _():
        grad = grad_ref[...]
        grad_bf = grad.astype(BF16)
        d_rows_ref[7:8] += jnp.sum(grad, axis=0, keepdims=True)
        d_wout_ref[...] += mm_tn(out2_ref[...], grad_bf)
        d_mix_ref[...] = mm_nt(grad_bf, w_out_ref[...]).astype(BF16)

        def sample(index, carry):
            rows = pl.ds(pl.multiple_of(index * tokens, tokens), tokens)
            kv_rows = pl.ds(pl.multiple_of((step * per_step + index) * SLOT, SLOT), SLOT)
            d_kv_rows = pl.ds(pl.multiple_of((step * per_step + index) * pad, pad), pad)
            for pair in range(heads // 2):
                cols = pair * LANES
                d_query, d_keys, d_values = pair_backward(
                    q_ref[rows, cols:cols + LANES], kv_ref[kv_rows, cols:cols + LANES],
                    kv_ref[kv_rows, width + cols:width + cols + LANES], d_mix_ref[rows, cols:cols + LANES], ctx_len)
                d_q_ref[rows, cols:cols + LANES] = d_query
                d_kv_ref[d_kv_rows, cols:cols + LANES] = d_keys[:pad]
                d_kv_ref[d_kv_rows, width + cols:width + cols + LANES] = d_values[:pad]
            return carry

        lax.fori_loop(0, per_step, sample, 0)
        h1 = h1_ref[...]
        hat, unused = normalize(h1)
        norm2 = (hat * rows_ref[2:3] + rows_ref[3:4]).astype(BF16)
        d_wq_ref[...] += mm_tn(norm2, d_q_ref[...])
        d_res, d_gain, d_shift = norm_back(h1, mm_nt(d_q_ref[...], w_q_ref[...]), rows_ref[2:3])
        out_ref[...] = grad + d_res
        d_rows_ref[2:3] += d_gain
        d_rows_ref[3:4] += d_shift

    @pl.when(step >= row_steps)
    def _():
        cols = d_wkv_ref.shape[1]
        start = pl.multiple_of((step - row_steps) * cols, cols)
        d_wkv_ref[...] = mm_tn(context_ref[...], d_kv_ref[:, pl.ds(start, cols)])


def self_backward_kernel(heads, tokens, row_steps, grad_ref, h_ref, qkv_ref, out1_ref, w_qkv_ref, w_out_ref, rows_ref,
                         out_ref, d_wqkv_ref, d_wout_ref, d_rows_ref, d_mix_ref, d_qkv_ref, norm_t_ref):
    width = heads * HEAD
    step = pl.program_id(0)
    block = h_ref.shape[0]

    @pl.when(step == 0)
    def _():
        d_rows_ref[...] = jnp.zeros_like(d_rows_ref)
        d_wout_ref[...] = jnp.zeros_like(d_wout_ref)

    @pl.when(step < row_steps)
    def _():
        grad = grad_ref[...]
        grad_bf = grad.astype(BF16)
        d_rows_ref[6:7] += jnp.sum(grad, axis=0, keepdims=True)
        d_wout_ref[...] += mm_tn(out1_ref[...], grad_bf)
        d_mix_ref[...] = mm_nt(grad_bf, w_out_ref[...]).astype(BF16)
        base = pl.multiple_of(step * block, block)

        def sample(index, carry):
            rows = pl.ds(pl.multiple_of(index * tokens, tokens), tokens)
            d_rows = pl.ds(pl.multiple_of(base + index * tokens, tokens), tokens)
            for pair in range(heads // 2):
                cols = pair * LANES
                d_query, d_keys, d_values = pair_backward(
                    qkv_ref[rows, cols:cols + LANES], qkv_ref[rows, width + cols:width + cols + LANES],
                    qkv_ref[rows, 2 * width + cols:2 * width + cols + LANES], d_mix_ref[rows, cols:cols + LANES], tokens)
                d_qkv_ref[d_rows, cols:cols + LANES] = d_query
                d_qkv_ref[d_rows, width + cols:width + cols + LANES] = d_keys
                d_qkv_ref[d_rows, 2 * width + cols:2 * width + cols + LANES] = d_values
            return carry

        lax.fori_loop(0, block // tokens, sample, 0)
        h = h_ref[...].astype(F32)
        hat, unused = normalize(h)
        norm_t_ref[:, pl.ds(base, block)] = (hat * rows_ref[0:1] + rows_ref[1:2]).astype(BF16).T
        d_norm = mm_nt(d_qkv_ref[pl.ds(base, block)], w_qkv_ref[...])
        d_res, d_gain, d_shift = norm_back(h, d_norm, rows_ref[0:1])
        out_ref[...] = (grad + d_res).astype(out_ref.dtype)
        d_rows_ref[0:1] += d_gain
        d_rows_ref[1:2] += d_shift

    @pl.when(step >= row_steps)
    def _():
        cols = d_wqkv_ref.shape[1]
        start = pl.multiple_of((step - row_steps) * cols, cols)
        d_wqkv_ref[...] = mm(norm_t_ref[...], d_qkv_ref[:, pl.ds(start, cols)])


def whole(shape):
    return pl.BlockSpec(shape, lambda step: (0,) * len(shape))


def params(**extra):
    return pltpu.CompilerParams(dimension_semantics=('arbitrary',), vmem_limit_bytes=62 * 1024 * 1024, **extra)


def cost(flops, moved):
    return pl.CostEstimate(flops=int(flops), bytes_accessed=int(moved), transcendentals=0)


def self_forward(h, w_qkv, w_out, rows, tokens):
    total, width = h.shape
    heads = width // HEAD
    row = lambda cols: pl.BlockSpec((PAIR_ROWS, cols), lambda step: (step, 0))
    return pl.pallas_call(
        lambda *refs: self_forward_kernel(heads, tokens, *refs),
        grid=(total // PAIR_ROWS,),
        in_specs=[row(width), whole(w_qkv.shape), whole(w_out.shape), whole(rows.shape)],
        out_specs=[row(width), row(3 * width), row(width)],
        out_shape=[jax.ShapeDtypeStruct((total, width), F32), jax.ShapeDtypeStruct((total, 3 * width), BF16),
                   jax.ShapeDtypeStruct((total, width), BF16)],
        compiler_params=params(), cost_estimate=cost(total * width * width * 10, 20e6), name='self_forward',
    )(h, w_qkv, w_out, rows)


def cross_forward(h1, context, w_q, w_kv, w_out, rows, tokens, ctx_len, samples):
    total, width = h1.shape
    heads = width // HEAD
    row = lambda cols: pl.BlockSpec((PAIR_ROWS, cols), lambda step: (step, 0))
    return pl.pallas_call(
        lambda *refs: cross_forward_kernel(heads, tokens, ctx_len, *refs),
        grid=(total // PAIR_ROWS,),
        in_specs=[row(width), whole(context.shape), whole(w_q.shape), whole(w_kv.shape), whole(w_out.shape),
                  whole(rows.shape)],
        out_specs=[row(width), row(width), whole((samples * SLOT, 2 * width)), row(width)],
        out_shape=[jax.ShapeDtypeStruct((total, width), F32), jax.ShapeDtypeStruct((total, width), BF16),
                   jax.ShapeDtypeStruct((samples * SLOT, 2 * width), BF16), jax.ShapeDtypeStruct((total, width), BF16)],
        compiler_params=params(), cost_estimate=cost(total * width * width * 8, 20e6), name='cross_forward',
    )(h1, context, w_q, w_kv, w_out, rows)


def ff_forward(h2, w1, w2, b1, rows, chunk):
    total, width = h2.shape
    inner = w2.shape[0]
    steps = inner // FF_COLS
    saved = pl.BlockSpec((1, total, FF_COLS), lambda step: (step, 0, 0))
    return pl.pallas_call(
        lambda *refs: ff_forward_kernel(chunk, *refs),
        grid=(steps,),
        in_specs=[whole(h2.shape), pl.BlockSpec((width, FF_COLS), lambda step: (0, step)),
                  pl.BlockSpec((width, FF_COLS), lambda step: (0, step + steps)),
                  pl.BlockSpec((FF_COLS, width), lambda step: (step, 0)),
                  pl.BlockSpec((1, FF_COLS), lambda step: (0, step)),
                  pl.BlockSpec((1, FF_COLS), lambda step: (0, step + steps)), whole(rows.shape)],
        out_specs=[whole(h2.shape), saved, saved, saved],
        out_shape=[jax.ShapeDtypeStruct((total, width), F32), jax.ShapeDtypeStruct((steps, total, FF_COLS), F32),
                   jax.ShapeDtypeStruct((steps, total, FF_COLS), F32), jax.ShapeDtypeStruct((steps, total, FF_COLS), BF16)],
        scratch_shapes=[pltpu.VMEM((total, width), BF16), pltpu.VMEM((total, width), F32)],
        compiler_params=params(), cost_estimate=cost(total * width * inner * 6, 60e6), name='ff_forward',
    )(h2, w1, w1, w2, b1, b1, rows)


def ff_backward(grad, h2, w1, w2, fa, fg, z, rows, chunk):
    total, width = h2.shape
    inner = w2.shape[0]
    steps = inner // FF_COLS
    saved = pl.BlockSpec((1, total, FF_COLS), lambda step: (step, 0, 0))
    column = pl.BlockSpec((width, FF_COLS), lambda step: (0, step))
    once = lambda shape: pl.BlockSpec(shape, lambda step: (0,) * len(shape), pipeline_mode=pl.Buffered(1))
    return pl.pallas_call(
        lambda *refs: ff_backward_kernel(chunk, *refs),
        grid=(steps,),
        in_specs=[once(grad.shape), once(h2.shape), column,
                  pl.BlockSpec((width, FF_COLS), lambda step: (0, step + steps)),
                  pl.BlockSpec((FF_COLS, width), lambda step: (step, 0)), saved, saved, saved, whole(rows.shape)],
        out_specs=[whole(h2.shape), column, column, pl.BlockSpec((FF_COLS, width), lambda step: (step, 0)),
                   pl.BlockSpec((1, 8, FF_COLS), lambda step: (step, 0, 0)), whole(rows.shape)],
        out_shape=[jax.ShapeDtypeStruct((total, width), F32), jax.ShapeDtypeStruct((width, inner), F32),
                   jax.ShapeDtypeStruct((width, inner), F32), jax.ShapeDtypeStruct((inner, width), F32),
                   jax.ShapeDtypeStruct((steps, 8, FF_COLS), F32), jax.ShapeDtypeStruct(rows.shape, F32)],
        scratch_shapes=[pltpu.VMEM((width, total), BF16), pltpu.VMEM((total, width), BF16),
                        pltpu.VMEM((total, 2 * FF_COLS), BF16), pltpu.VMEM((width, 2 * FF_COLS), BF16),
                        pltpu.VMEM((total, width), F32)],
        compiler_params=params(), cost_estimate=cost(total * width * inner * 12, 80e6), name='ff_backward',
    )(grad, h2, w1, w1, w2, fa, fg, z, rows)


def cross_backward(grad, h1, q, out2, kv, context, w_q, w_out, rows, tokens, ctx_len):
    total, width = h1.shape
    heads = width // HEAD
    row_steps = total // PAIR_ROWS
    kv_cols = 256
    extra = 2 * width // kv_cols
    row = lambda cols: pl.BlockSpec((PAIR_ROWS, cols), lambda step: (jnp.minimum(step, row_steps - 1), 0))
    return pl.pallas_call(
        lambda *refs: cross_backward_kernel(heads, tokens, ctx_len, row_steps, *refs),
        grid=(row_steps + extra,),
        in_specs=[row(width), row(width), row(width), row(width), whole(kv.shape), whole(context.shape),
                  whole(w_q.shape), whole(w_out.shape), whole(rows.shape)],
        out_specs=[row(width), whole(w_q.shape), whole(w_out.shape),
                   pl.BlockSpec((context.shape[1], kv_cols), lambda step: (0, jnp.maximum(step - row_steps, 0))),
                   whole(rows.shape)],
        out_shape=[jax.ShapeDtypeStruct((total, width), F32), jax.ShapeDtypeStruct(w_q.shape, F32),
                   jax.ShapeDtypeStruct(w_out.shape, F32), jax.ShapeDtypeStruct((context.shape[1], 2 * width), F32),
                   jax.ShapeDtypeStruct(rows.shape, F32)],
        scratch_shapes=[pltpu.VMEM((PAIR_ROWS, width), BF16), pltpu.VMEM((PAIR_ROWS, width), BF16),
                        pltpu.VMEM((context.shape[0], 2 * width), BF16)],
        compiler_params=params(), cost_estimate=cost(total * width * width * 16, 40e6), name='cross_backward',
    )(grad, h1, q, out2, kv, context, w_q, w_out, rows)


def self_backward(grad, h, qkv, out1, w_qkv, w_out, rows, tokens, out_dtype):
    total, width = h.shape
    heads = width // HEAD
    row_steps = total // PAIR_ROWS
    cols = 384
    extra = 3 * width // cols
    row = lambda cols: pl.BlockSpec((PAIR_ROWS, cols), lambda step: (jnp.minimum(step, row_steps - 1), 0))
    return pl.pallas_call(
        lambda *refs: self_backward_kernel(heads, tokens, row_steps, *refs),
        grid=(row_steps + extra,),
        in_specs=[row(width), row(width), row(3 * width), row(width), whole(w_qkv.shape), whole(w_out.shape),
                  whole(rows.shape)],
        out_specs=[row(width), pl.BlockSpec((width, cols), lambda step: (0, jnp.maximum(step - row_steps, 0))),
                   whole(w_out.shape), whole(rows.shape)],
        out_shape=[jax.ShapeDtypeStruct((total, width), out_dtype), jax.ShapeDtypeStruct(w_qkv.shape, F32),
                   jax.ShapeDtypeStruct(w_out.shape, F32), jax.ShapeDtypeStruct(rows.shape, F32)],
        scratch_shapes=[pltpu.VMEM((PAIR_ROWS, width), BF16), pltpu.VMEM((total, 3 * width), BF16),
                        pltpu.VMEM((width, total), BF16)],
        compiler_params=params(), cost_estimate=cost(total * width * width * 24, 40e6), name='self_backward',
    )(grad, h, qkv, out1, w_qkv, w_out, rows)


def gather(local):
    return lax.all_gather(local, AXIS, axis=0, tiled=True)


def scatter(grad, total):
    return lax.psum_scatter(grad, AXIS, scatter_dimension=0, tiled=True) / total


def solution(mesh):
    n_dev = mesh.shape[AXIS]

    def local(tokens_x, context, cot_out, *shards):
        samples, tokens, width = tokens_x.shape
        ctx_len, ctx_width = context.shape[1:]
        blocks = shards[0].shape[0]
        total = samples * n_dev
        chunk = PAIR_ROWS
        shapes = weight_shapes(width, ctx_width)
        pieces = [[shard[layer].reshape(shape[0] // n_dev, shape[1]) for shard, shape in zip(shards[:7], shapes[:7])]
                  for layer in range(blocks)]
        vecs = lax.all_gather(shards[7].reshape(1, blocks, -1), AXIS, axis=0, tiled=True)
        vecs = jnp.swapaxes(vecs, 0, 1).reshape(blocks, -1).astype(F32)
        pad = -(-ctx_len // 16) * 16
        ctx_rows = jnp.pad(context, ((0, 0), (0, pad - ctx_len), (0, 0))).reshape(samples * pad, ctx_width)
        h = tokens_x.reshape(samples * tokens, width)
        saved = []
        for layer in range(blocks):
            w_qkv, w_out, w_q2, w_kv2, w_out2, w_ff1, w_ff2 = pieces[layer]
            w_qkv = gather(w_qkv)
            small = gather(jnp.concatenate([w_out, w_q2, w_out2], axis=1))
            w_out, w_q2, w_out2 = (small[:, index * width:(index + 1) * width] for index in range(3))
            w_kv2, w_ff1, w_ff2 = gather(w_kv2), gather(w_ff1), gather(w_ff2)
            rows = jnp.pad(vecs[layer, :9 * width].reshape(9, width), ((0, 7), (0, 0)))
            b1 = vecs[layer, 9 * width:17 * width].reshape(1, 8 * width)
            h1, qkv, out1 = self_forward(h, w_qkv, w_out, rows, tokens)
            h2, q, kv, out2 = cross_forward(h1, ctx_rows, w_q2, w_kv2, w_out2, rows, tokens, ctx_len, samples)
            h3, fa, fg, z = ff_forward(h2, w_ff1, w_ff2, b1, rows, chunk)
            saved.append((h, h1, h2, qkv, out1, q, kv, out2, fa, fg, z, w_qkv, w_out, w_q2, w_out2, w_ff1, w_ff2, rows))
            h = h3
        out_tokens = h.astype(BF16).reshape(tokens_x.shape)
        grad = cot_out.reshape(samples * tokens, width).astype(F32)
        results, vec_grads = [None] * blocks, [None] * blocks
        for layer in reversed(range(blocks)):
            h, h1, h2, qkv, out1, q, kv, out2, fa, fg, z, w_qkv, w_out, w_q2, w_out2, w_ff1, w_ff2, rows = saved[layer]
            grad, d_w1a, d_w1g, d_w2, d_b1, d_rows3 = ff_backward(grad, h2, w_ff1, w_ff2, fa, fg, z, rows, chunk)
            g_ff1 = jnp.concatenate([scatter(d_w1a, total), scatter(d_w1g, total)], axis=1)
            g_ff2 = scatter(d_w2, total)
            grad, d_wq, d_wout2, d_wkv, d_rows2 = cross_backward(grad, h1, q, out2, kv, ctx_rows, w_q2, w_out2, rows,
                                                                 tokens, ctx_len)
            g_q2, g_out2, g_kv2 = scatter(d_wq, total), scatter(d_wout2, total), scatter(d_wkv, total)
            grad, d_wqkv, d_wout, d_rows1 = self_backward(grad, h, qkv, out1, w_qkv, w_out, rows, tokens,
                                                          BF16 if layer == 0 else F32)
            g_qkv, g_out = scatter(d_wqkv, total), scatter(d_wout, total)
            d_rows = (d_rows1 + d_rows2 + d_rows3)[:9].reshape(-1)
            d_b1 = jnp.swapaxes(d_b1[:, :2], 0, 1).reshape(-1)
            vec_grads[layer] = jnp.concatenate([d_rows, d_b1])
            results[layer] = [g_qkv, g_out, g_q2, g_kv2, g_out2, g_ff1, g_ff2]
        vec = jnp.stack(vec_grads).reshape(blocks, n_dev, -1)
        vec = lax.psum_scatter(vec, AXIS, scatter_dimension=1, tiled=False) / total
        stacked = [jnp.stack([result[index].reshape(-1) for result in results]) for index in range(7)]
        return tuple([out_tokens, grad.reshape(tokens_x.shape)] + stacked + [vec])

    param_spec = P(None, AXIS)
    in_specs = (P(AXIS), P(AXIS), P(AXIS)) + (param_spec,) * 8
    out_specs = (P(AXIS), P(AXIS)) + (param_spec,) * 8
    return jax.shard_map(local, mesh=mesh, in_specs=in_specs, out_specs=out_specs, check_vma=False)
```

time: 2980 us -> 1980 us (0.66)
  other arithmetic: 1090 us -> 36.5 us
  waiting for transfers between devices: 762 us -> 1360 us
  matrix products: 510 us -> 0 us
  Pallas kernels: 0 us -> 493 us
  local copies, waits for them, and re-layouts: 362 us -> 50.3 us
  blocking collectives: 226 us -> 14.5 us
    all_gather x14 -> x0, other arithmetic: 861 us -> none  [gather_block(): whole = lax.all_gather(shard, AXIS, axis=0, tiled=True)]
    reduce_scatter x0 -> x8, waiting for transfers between devices: none -> 665 us  [scatter(): return lax.psum_scatter(grad, AXIS, scatter_dimension=0, tiled=True) / total]
    dot_general x64 -> x0, matrix products: 510 us -> none  [the longest x12 148 us: project_back(): jnp.einsum('bte,de->btd', grads, weight, preferred_element_type=jnp.float32)]
    pallas_call x0 -> x12, Pallas kernels: none -> 493 us  [the longest x2 133 us: ff_backward(): pl.pallas_call(lambda *refs: ff_backward_kernel(chunk, *refs), grid=(step...]
    unnamed x18 -> x36, waiting for transfers between devices: 762 us -> 523 us
    reshape x38 -> x4, local copies, waits for them, and re-layouts: 197 us -> 0.03 us  [the longest x2 0.01 us: local(): d_b1 = jnp.swapaxes(d_b1[:, :2], 0, 1).reshape(-1)]
    all_gather x12 -> x1, blocking collectives: 190 us -> 14.5 us  [local(): lax.all_gather(shards[7].reshape(1, blocks, -1), AXIS, axis=0, tiled=True)]
    all_gather x14 -> x10, waiting for transfers between devices: 0.07 us -> 172 us  [gather(): return lax.all_gather(local, AXIS, axis=0, tiled=True)]
  transfers between devices with their start and end apart: 16 -> 27, of which waited for: 1 -> 24; matrix products, arithmetic and copies ran while one was open for 60% -> 4% of each run, Pallas kernels for 0% -> 7%
where the time goes in v2:
time: 1980 us; the launch traced here: 1970 us
  waiting for transfers between devices  1360 us (69%)
  Pallas kernels  493 us (25%)
  local copies, waits for them, and re-layouts  50.3 us (3%)
  other arithmetic  36.5 us (2%)
    reduce_scatter x8, waiting for transfers between devices, scatter(): return lax.psum_scatter(grad, AXIS, scatter_dimension=0, tiled=True) / total  665 us
    unnamed x36, waiting for transfers between devices  523 us
    all_gather x10, waiting for transfers between devices, gather(): return lax.all_gather(local, AXIS, axis=0, tiled=True)  172 us
    pallas_call x2, Pallas kernels, ff_backward(): pl.pallas_call(lambda *refs: ff_backward_kernel(chunk, *refs), grid=(step...  133 us
    pallas_call x2, Pallas kernels, ff_forward(): pl.pallas_call(lambda *refs: ff_forward_kernel(chunk, *refs), grid=(steps...  97.8 us
    pallas_call x2, Pallas kernels, self_backward(): pl.pallas_call(lambda *refs: self_backward_kernel(heads, tokens, row_step...  89.4 us
    pallas_call x2, Pallas kernels, cross_backward(): pl.pallas_call(lambda *refs: cross_backward_kernel(heads, tokens, ctx_len...  81.6 us
    pallas_call x2, Pallas kernels, self_forward(): pl.pallas_call(lambda *refs: self_forward_kernel(heads, tokens, *refs), g...  49.3 us
  transfers between devices with their start and end apart: 27, of which 24 were waited for; matrix products, arithmetic and copies ran while one was open for 4% of the time, Pallas kernels for 7%

profile of v2, /device:TPU:0, one launch (start us, length us, event | category | flops | bytes accessed | tf_op | source)
XLA Modules:
  0.0 1971.9 jit_solution(17052488706170694611)
XLA Ops:
  184.6 45.4 %all-gather.19.cloned.1.call-done.refs_1_.refs_2_.refs_3_ = bf16[640,5120]{1,0:T(8,128)(2,1)} async-done(((bf16[40,5120]{1,0:T(8,128)(2,1)}), bf16[640,5120]{1,0:T(8,128)(2,1)}) %all-gather.19.cloned.1.call-update) | async-done | bytes 6553616 | tf_op jit(solution)/shard_map/all_gather | solution.py:501
  230.0 48.8 %ff_forward.2 = (f32[1536,640]{1,0:T(8,128)}, f32[10,1536,256]{2,1,0:T(8,128)}, f32[10,1536,256]{2,1,0:T(8,128)}, bf16[10,1536,256]{2,1,0:T(8,128)(2,1)}) custom-call(f32[1536,640]{1,0:T(8,128)} %get-tuple-element.63.refs_0_.refs_1_, bf16[640,5120]{1,0:T(8,128)(2,1)} %all-gather.19.cloned.1.call-done.refs_1_.refs_2_.refs_3_, ...), custom_call_target="tpu_custom_call" | custom-call | flops 15099494400 | bytes 60000000 | tf_op jit(solution)/shard_map/ff_forward/pallas_call | solution.py:413
  337.1 45.4 %all-gather.29.cloned.1.call-done.refs_1_.refs_2_.refs_3_ = bf16[640,5120]{1,0:T(8,128)(2,1)} async-done(((bf16[40,5120]{1,0:T(8,128)(2,1)}), bf16[640,5120]{1,0:T(8,128)(2,1)}) %all-gather.29.cloned.1.call-update) | async-done | bytes 6553616 | tf_op jit(solution)/shard_map/all_gather | solution.py:501
  382.5 49.0 %ff_forward.3 = (f32[1536,640]{1,0:T(8,128)}, f32[10,1536,256]{2,1,0:T(8,128)}, f32[10,1536,256]{2,1,0:T(8,128)}, bf16[10,1536,256]{2,1,0:T(8,128)(2,1)}) custom-call(f32[1536,640]{1,0:T(8,128)} %get-tuple-element.66.refs_0_.refs_1_, bf16[640,5120]{1,0:T(8,128)(2,1)} %all-gather.29.cloned.1.call-done.refs_1_.refs_2_.refs_3_, ...), custom_call_target="tpu_custom_call" | custom-call | flops 15099494400 | bytes 60000000 | tf_op jit(solution)/shard_map/ff_forward/pallas_call | solution.py:413
  431.5 66.5 %ff_backward.2 = (f32[1536,640]{1,0:T(8,128)}, f32[640,2560]{1,0:T(8,128)}, f32[640,2560]{1,0:T(8,128)}, f32[2560,640]{1,0:T(8,128)}, f32[10,8,256]{2,1,0:T(8,128)}, /*index=5*/f32[16,640]{1,0:T(8,128)}) custom-call(f32[1536,640]{1,0:T(8,128)} %bitcast_convert_fusion.refs_0_, f32[1536,640]{1,0:T(8,128)} %get-tuple-element.66.refs_0_.refs_1_, ...), custom_call_target="tpu_custom_call" | custom-call | flops 30198988800 | bytes 80000000 | tf_op jit(solution)/shard_map/ff_backward/pallas_call | solution.py:436
  539.7 45.1 %self_backward.2 = (f32[1536,640]{1,0:T(8,128)}, f32[640,1920]{1,0:T(8,128)}, f32[640,640]{1,0:T(8,128)}, f32[16,640]{1,0:T(8,128)}) custom-call(f32[1536,640]{1,0:T(8,128)} %get-tuple-element.75.refs_0_, f32[1536,640]{1,0:T(8,128)} %get-tuple-element.64.refs_0_.refs_1_, bf16[1536,1920]{1,0:T(8,128)(2,1)} %get-tuple-element.76.refs_2_, ...), custom_call_target="tpu_custom_call" | custom-call | flops 15099494400 | bytes 40000000 | tf_op jit(solution)/shard_map/self_backward/pallas_call | solution.py:485
  585.8 66.3 %ff_backward.3 = (f32[1536,640]{1,0:T(8,128)}, f32[640,2560]{1,0:T(8,128)}, f32[640,2560]{1,0:T(8,128)}, f32[2560,640]{1,0:T(8,128)}, f32[10,8,256]{2,1,0:T(8,128)}, /*index=5*/f32[16,640]{1,0:T(8,128)}) custom-call(f32[1536,640]{1,0:T(8,128)} %get-tuple-element.78.refs_0_, f32[1536,640]{1,0:T(8,128)} %get-tuple-element.63.refs_0_.refs_1_, ...), custom_call_target="tpu_custom_call" | custom-call | flops 30198988800 | bytes 80000000 | tf_op jit(solution)/shard_map/ff_backward/pallas_call | solution.py:436
  753.6 51.4 %all-reduce.14.cloned.1.call-done = f32[2,16,680]{2,0,1:T(2,128)} async-done(((f32[2,16,680]{2,0,1:T(2,128)}), f32[2,16,680]{2,0,1:T(2,128)}) %all-reduce.14.cloned.1.call-update) | async-done | bytes 87056
  806.3 56.0 %reduce-scatter.61.cloned.1.call-done = f32[40,640]{1,0:T(8,128)} async-done(((f32[640,640]{1,0:T(8,128)}), f32[40,640]{1,0:T(8,128)}) %reduce-scatter.61.cloned.1.call-update) | async-done | bytes 102416
  863.3 56.3 %reduce-scatter.59.cloned.1.call-done = f32[40,640]{1,0:T(8,128)} async-done(((f32[640,640]{1,0:T(8,128)}), f32[40,640]{1,0:T(8,128)}) %reduce-scatter.59.cloned.1.call-update) | async-done | bytes 102416
  920.7 56.7 %reduce-scatter.65.cloned.1.call-done = f32[40,640]{1,0:T(8,128)} async-done(((f32[640,640]{1,0:T(8,128)}), f32[40,640]{1,0:T(8,128)}) %reduce-scatter.65.cloned.1.call-update) | async-done | bytes 102416
  978.4 56.1 %reduce-scatter.63.cloned.1.call-done = f32[40,640]{1,0:T(8,128)} async-done(((f32[640,640]{1,0:T(8,128)}), f32[40,640]{1,0:T(8,128)}) %reduce-scatter.63.cloned.1.call-update) | async-done | bytes 102416
  1035.5 56.1 %reduce-scatter.69.cloned.1.call-done = f32[40,640]{1,0:T(8,128)} async-done(((f32[640,640]{1,0:T(8,128)}), f32[40,640]{1,0:T(8,128)}) %reduce-scatter.69.cloned.1.call-update) | async-done | bytes 102416
  1092.5 56.1 %reduce-scatter.67.cloned.1.call-done = f32[40,640]{1,0:T(8,128)} async-done(((f32[640,640]{1,0:T(8,128)}), f32[40,640]{1,0:T(8,128)}) %reduce-scatter.67.cloned.1.call-update) | async-done | bytes 102416
  1151.6 60.8 %reduce-scatter.57.cloned.1.call-done = f32[40,1920]{1,0:T(8,128)} async-done(((f32[640,1920]{1,0:T(8,128)}), f32[40,1920]{1,0:T(8,128)}) %reduce-scatter.57.cloned.1.call-update) | async-done | bytes 307216
  1213.7 64.4 %reduce-scatter.55.cloned.1.call-done = f32[40,1920]{1,0:T(8,128)} async-done(((f32[640,1920]{1,0:T(8,128)}), f32[40,1920]{1,0:T(8,128)}) %reduce-scatter.55.cloned.1.call-update) | async-done | bytes 307216
  1280.8 73.7 %reduce-scatter.49.cloned.1.call-done = f32[40,2560]{1,0:T(8,128)} async-done(((f32[640,2560]{1,0:T(8,128)}), f32[40,2560]{1,0:T(8,128)}) %reduce-scatter.49.cloned.1.call-update) | async-done | bytes 409616 | tf_op jit(solution)/shard_map/reduce_scatter | solution.py:505
  1355.6 74.4 %reduce-scatter.47.cloned.1.call-done = f32[40,2560]{1,0:T(8,128)} async-done(((f32[640,2560]{1,0:T(8,128)}), f32[40,2560]{1,0:T(8,128)}) %reduce-scatter.47.cloned.1.call-update) | async-done | bytes 409616 | tf_op jit(solution)/shard_map/reduce_scatter | solution.py:505
  1431.9 73.5 %reduce-scatter.45.cloned.1.call-done = f32[40,2560]{1,0:T(8,128)} async-done(((f32[640,2560]{1,0:T(8,128)}), f32[40,2560]{1,0:T(8,128)}) %reduce-scatter.45.cloned.1.call-update) | async-done | bytes 409616 | tf_op jit(solution)/shard_map/reduce_scatter | solution.py:505
  1506.5 74.4 %reduce-scatter.43.cloned.1.call-done = f32[40,2560]{1,0:T(8,128)} async-done(((f32[640,2560]{1,0:T(8,128)}), f32[40,2560]{1,0:T(8,128)}) %reduce-scatter.43.cloned.1.call-update) | async-done | bytes 409616 | tf_op jit(solution)/shard_map/reduce_scatter | solution.py:505
  1582.8 73.3 %reduce-scatter.53.cloned.1.call-done = f32[160,640]{1,0:T(8,128)} async-done(((f32[2560,640]{1,0:T(8,128)}), f32[160,640]{1,0:T(8,128)}) %reduce-scatter.53.cloned.1.call-update) | async-done | bytes 409616 | tf_op jit(solution)/shard_map/reduce_scatter | solution.py:505
  1657.6 74.0 %reduce-scatter.51.cloned.1.call-done = f32[160,640]{1,0:T(8,128)} async-done(((f32[2560,640]{1,0:T(8,128)}), f32[160,640]{1,0:T(8,128)}) %reduce-scatter.51.cloned.1.call-update) | async-done | bytes 409616 | tf_op jit(solution)/shard_map/reduce_scatter | solution.py:505
  1737.1 109.4 %reduce-scatter.41.cloned.1.call-done = f32[128,1280]{1,0:T(8,128)} async-done(((f32[2048,1280]{1,0:T(8,128)}), f32[128,1280]{1,0:T(8,128)}) %reduce-scatter.41.cloned.1.call-update) | async-done | bytes 655376 | tf_op jit(solution)/shard_map/reduce_scatter | solution.py:505
  1848.3 112.4 %reduce-scatter.39.cloned.1.call-done = f32[128,1280]{1,0:T(8,128)} async-done(((f32[2048,1280]{1,0:T(8,128)}), f32[128,1280]{1,0:T(8,128)}) %reduce-scatter.39.cloned.1.call-update) | async-done | bytes 655376 | tf_op jit(solution)/shard_map/reduce_scatter | solution.py:505
  (181 shorter events, 411.0 us)
Async XLA Ops:
  17.5 132.4 %all-gather.17.cloned.1.call-start = ((), (), s32[]{:S(2)}) async-start(), calls=%async_computation.18 | async-start | bytes 5570560 | tf_op jit(solution)/shard_map/all_gather | solution.py:501
  25.6 158.9 %all-gather.21.cloned.1.call-start = ((), (), s32[]{:S(2)}) async-start(), calls=%async_computation.20 | async-start | bytes 3481600 | tf_op jit(solution)/shard_map/all_gather | solution.py:501
  28.7 201.2 %all-gather.19.cloned.1.call-start = ((), (), s32[]{:S(2)}) async-start(), calls=%async_computation.19 | async-start | bytes 6963200 | tf_op jit(solution)/shard_map/all_gather | solution.py:501
  38.6 240.1 %all-gather.23.cloned.1.call-start = ((), (), s32[]{:S(2)}) async-start(), calls=%async_computation.21 | async-start | bytes 2611200 | tf_op jit(solution)/shard_map/all_gather | solution.py:501
  39.6 263.8 %all-gather.27.cloned.1.call-start = ((), (), s32[]{:S(2)}) async-start(), calls=%async_computation.23 | async-start | bytes 5570560 | tf_op jit(solution)/shard_map/all_gather | solution.py:501
  40.7 296.4 %all-gather.31.cloned.1.call-start = ((), (), s32[]{:S(2)}) async-start(), calls=%async_computation.25 | async-start | bytes 3481600 | tf_op jit(solution)/shard_map/all_gather | solution.py:501
  41.7 340.8 %all-gather.29.cloned.1.call-start = ((), (), s32[]{:S(2)}) async-start(), calls=%async_computation.24 | async-start | bytes 6963200 | tf_op jit(solution)/shard_map/all_gather | solution.py:501
  42.7 762.3 %all-reduce.14.cloned.1.call-start = ((), (), s32[]{:S(2)}) async-start(), calls=%async_computation.34 | async-start | bytes 196608
  740.0 122.3 %reduce-scatter.61.cloned.1.call-start = ((), (), s32[]{:S(2)}) async-start(), calls=%async_computation.38 | async-start | bytes 1740800
  740.5 179.1 %reduce-scatter.59.cloned.1.call-start = ((), (), s32[]{:S(2)}) async-start(), calls=%async_computation.37 | async-start | bytes 1740800
  741.3 236.1 %reduce-scatter.65.cloned.1.call-start = ((), (), s32[]{:S(2)}) async-start(), calls=%async_computation.40 | async-start | bytes 1740800
  741.9 292.6 %reduce-scatter.63.cloned.1.call-start = ((), (), s32[]{:S(2)}) async-start(), calls=%async_computation.39 | async-start | bytes 1740800
  742.5 349.1 %reduce-scatter.69.cloned.1.call-start = ((), (), s32[]{:S(2)}) async-start(), calls=%async_computation.42 | async-start | bytes 1740800
  743.0 405.6 %reduce-scatter.67.cloned.1.call-start = ((), (), s32[]{:S(2)}) async-start(), calls=%async_computation.41 | async-start | bytes 1740800
  743.6 468.8 %reduce-scatter.57.cloned.1.call-start = ((), (), s32[]{:S(2)}) async-start(), calls=%async_computation.36 | async-start | bytes 5222400
  744.2 533.9 %reduce-scatter.55.cloned.1.call-start = ((), (), s32[]{:S(2)}) async-start(), calls=%async_computation.35 | async-start | bytes 5222400
  744.9 609.6 %reduce-scatter.49.cloned.1.call-start = ((), (), s32[]{:S(2)}) async-start(), calls=%async_computation.31 | async-start | bytes 6963200 | tf_op jit(solution)/shard_map/reduce_scatter | solution.py:505
  745.5 684.5 %reduce-scatter.47.cloned.1.call-start = ((), (), s32[]{:S(2)}) async-start(), calls=%async_computation.30 | async-start | bytes 6963200 | tf_op jit(solution)/shard_map/reduce_scatter | solution.py:505
  746.3 759.2 %reduce-scatter.45.cloned.1.call-start = ((), (), s32[]{:S(2)}) async-start(), calls=%async_computation.29 | async-start | bytes 6963200 | tf_op jit(solution)/shard_map/reduce_scatter | solution.py:505
  747.0 833.9 %reduce-scatter.43.cloned.1.call-start = ((), (), s32[]{:S(2)}) async-start(), calls=%async_computation.28 | async-start | bytes 6963200 | tf_op jit(solution)/shard_map/reduce_scatter | solution.py:505
  747.8 908.4 %reduce-scatter.53.cloned.1.call-start = ((), (), s32[]{:S(2)}) async-start(), calls=%async_computation.33 | async-start | bytes 6963200 | tf_op jit(solution)/shard_map/reduce_scatter | solution.py:505
  748.3 983.3 %reduce-scatter.51.cloned.1.call-start = ((), (), s32[]{:S(2)}) async-start(), calls=%async_computation.32 | async-start | bytes 6963200 | tf_op jit(solution)/shard_map/reduce_scatter | solution.py:505
  749.1 1097.4 %reduce-scatter.41.cloned.1.call-start = ((), (), s32[]{:S(2)}) async-start(), calls=%async_computation.27 | async-start | bytes 11141120 | tf_op jit(solution)/shard_map/reduce_scatter | solution.py:505
  749.7 1211.1 %reduce-scatter.39.cloned.1.call-start = ((), (), s32[]{:S(2)}) async-start(), calls=%async_computation.26 | async-start | bytes 11141120 | tf_op jit(solution)/shard_map/reduce_scatter | solution.py:505
  (13 other events, 476.2 us)
Sparse Core Ops, SparseCore 0:
  12.9 32.1 all-gather.14
  111.5 38.3 all-gather.16
  152.6 31.9 all-gather.20
  187.2 42.6 all-gather.18
  263.8 38.3 all-gather.26
  305.0 32.0 all-gather.30
  339.8 42.6 all-gather.28
  740.1 64.8 all-reduce.13
  807.1 55.1 reduce-scatter.60
  864.6 55.0 reduce-scatter.58
  922.3 54.9 reduce-scatter.64
  979.5 54.9 reduce-scatter.62
  1036.6 54.9 reduce-scatter.68
  1093.6 54.9 reduce-scatter.66
  1153.0 59.3 reduce-scatter.56
  1216.9 61.1 reduce-scatter.54
  1280.2 74.2 reduce-scatter.48
  1356.8 73.1 reduce-scatter.46
  1432.3 73.1 reduce-scatter.44
  1507.7 73.1 reduce-scatter.42
  1583.0 73.1 reduce-scatter.52
  1658.4 73.1 reduce-scatter.50
  1733.7 112.7 reduce-scatter.40
  1848.6 112.0 reduce-scatter.38
  (3 shorter events, 87.7 us)

commit v3 on v2

v3 whole, which is shorter than its diff:
```python
import functools
import math
from typing import Any, NamedTuple
import jax
import jax.numpy as jnp
from jax import lax
from jax.experimental import pallas as pl
from jax.experimental.pallas import tpu as pltpu
from jax.sharding import PartitionSpec as P

AXIS = 'fsdp'
HEAD = 64
EPS = 1e-5
F32 = jnp.float32
BF16 = jnp.bfloat16
LANES = 128
SLOT = 128
PAIR_ROWS = 512
FF_COLS = 256

TAIL_P = 0.265
TAIL = (0.10574158579953814, 0.10524628753634038, 0.10270369607548423, 0.0603023517537824, 0.13797880111692826,
        -0.11640058407079061, 0.2178489286936914, -0.1442454807654402, 0.03082441619112092)


def weight_shapes(width, ctx_width):
    return ((width, 3 * width), (width, width), (width, width), (ctx_width, 2 * width),
            (width, width), (width, 8 * width), (4 * width, width), (17 * width,))


def mm(lhs, rhs):
    return jnp.dot(lhs, rhs, preferred_element_type=F32)


def mm_nt(lhs, rhs):
    return lax.dot_general(lhs, rhs, (((1,), (1,)), ((), ())), preferred_element_type=F32)


def mm_tn(lhs, rhs):
    return lax.dot_general(lhs, rhs, (((0,), (0,)), ((), ())), preferred_element_type=F32)


def normalize(x):
    centered = x - jnp.mean(x, axis=-1, keepdims=True)
    scale = lax.rsqrt(jnp.mean(centered * centered, axis=-1, keepdims=True) + EPS)
    return centered * scale, scale


def norm_back(x, d_norm, gain):
    hat, scale = normalize(x)
    d_hat = d_norm * gain
    pulled = d_hat - jnp.mean(d_hat, axis=-1, keepdims=True) - hat * jnp.mean(d_hat * hat, axis=-1, keepdims=True)
    return pulled * scale, jnp.sum(d_norm * hat, axis=0, keepdims=True), jnp.sum(d_norm, axis=0, keepdims=True)


def low_half(rows):
    return lax.broadcasted_iota(jnp.int32, (rows, LANES), 1) < HEAD


def head_stack(pair, low):
    zero = jnp.zeros_like(pair)
    return jnp.concatenate([jnp.where(low, pair, zero), jnp.where(low, zero, pair)], axis=0)


def head_unstack(stacked, low):
    half = stacked.shape[0] // 2
    return jnp.where(low, stacked[:half], stacked[half:])


def softmax_halves(scores, valid):
    half = scores.shape[1] // 2
    parts = []
    for index in range(2):
        part = scores[:, index * half:(index + 1) * half]
        if valid < half:
            part = jnp.where(lax.broadcasted_iota(jnp.int32, part.shape, 1) < valid, part, -jnp.inf)
        part = jnp.exp(part - jnp.max(part, axis=-1, keepdims=True))
        parts.append(part * (1.0 / jnp.sum(part, axis=-1, keepdims=True)))
    return parts


def pair_forward(query, keys, values, valid):
    low = low_half(keys.shape[0])
    scores = mm_nt(query * BF16(HEAD ** -0.5), head_stack(keys, low))
    probs = jnp.concatenate([part.astype(BF16) for part in softmax_halves(scores, valid)], axis=1)
    return mm(probs, head_stack(values, low)).astype(BF16)


def pair_backward(query, keys, values, d_out, valid):
    low = low_half(keys.shape[0])
    half = keys.shape[0]
    query = query * BF16(HEAD ** -0.5)
    key_stack = head_stack(keys, low)
    value_stack = head_stack(values, low)
    parts = softmax_halves(mm_nt(query, key_stack), valid)
    probs = jnp.concatenate([part.astype(BF16) for part in parts], axis=1)
    d_values = head_unstack(mm_tn(probs, d_out), low).astype(BF16)
    d_probs = mm_nt(d_out, value_stack)
    d_scores = []
    for index in range(2):
        part, d_part = parts[index], d_probs[:, index * half:(index + 1) * half]
        d_scores.append((part * (d_part - jnp.sum(part * d_part, axis=-1, keepdims=True))).astype(BF16))
    d_scores = jnp.concatenate(d_scores, axis=1)
    d_query = (mm(d_scores, key_stack) * HEAD ** -0.5).astype(BF16)
    d_keys = head_unstack(mm_tn(d_scores, query), low).astype(BF16)
    return d_query, d_keys, d_values


def self_forward_kernel(heads, tokens, h_ref, w_qkv_ref, w_out_ref, rows_ref, h1_ref, qkv_ref, out_ref):
    width = heads * HEAD
    hat, unused = normalize(h_ref[...].astype(F32))
    norm1 = (hat * rows_ref[0:1] + rows_ref[1:2]).astype(BF16)
    qkv_ref[...] = mm(norm1, w_qkv_ref[...]).astype(BF16)

    def sample(index, carry):
        rows = pl.ds(pl.multiple_of(index * tokens, tokens), tokens)
        for pair in range(heads // 2):
            cols = pair * LANES
            out_ref[rows, cols:cols + LANES] = pair_forward(
                qkv_ref[rows, cols:cols + LANES], qkv_ref[rows, width + cols:width + cols + LANES],
                qkv_ref[rows, 2 * width + cols:2 * width + cols + LANES], tokens)
        return carry

    lax.fori_loop(0, h_ref.shape[0] // tokens, sample, 0)
    h1_ref[...] = h_ref[...].astype(F32) + mm(out_ref[...], w_out_ref[...]) + rows_ref[6:7]


def cross_forward_kernel(heads, tokens, ctx_len, h1_ref, context_ref, w_q_ref, w_kv_ref, w_out_ref, rows_ref,
                         h2_ref, q_ref, kv_ref, out_ref):
    width = heads * HEAD
    samples = kv_ref.shape[0] // SLOT
    pad = context_ref.shape[0] // samples
    step = pl.program_id(0)

    @pl.when(step == 0)
    def _():
        kv = mm(context_ref[...], w_kv_ref[...]).astype(BF16)
        for index in range(samples):
            kv_ref[index * SLOT:index * SLOT + pad] = kv[index * pad:(index + 1) * pad]
            kv_ref[index * SLOT + pad:(index + 1) * SLOT] = jnp.zeros((SLOT - pad, 2 * width), BF16)

    hat, unused = normalize(h1_ref[...])
    norm2 = (hat * rows_ref[2:3] + rows_ref[3:4]).astype(BF16)
    q_ref[...] = mm(norm2, w_q_ref[...]).astype(BF16)
    per_step = h1_ref.shape[0] // tokens

    def sample(index, carry):
        rows = pl.ds(pl.multiple_of(index * tokens, tokens), tokens)
        kv_rows = pl.ds(pl.multiple_of((step * per_step + index) * SLOT, SLOT), SLOT)
        for pair in range(heads // 2):
            cols = pair * LANES
            out_ref[rows, cols:cols + LANES] = pair_forward(
                q_ref[rows, cols:cols + LANES], kv_ref[kv_rows, cols:cols + LANES],
                kv_ref[kv_rows, width + cols:width + cols + LANES], ctx_len)
        return carry

    lax.fori_loop(0, per_step, sample, 0)
    h2_ref[...] = h1_ref[...] + mm(out_ref[...], w_out_ref[...]) + rows_ref[7:8]


def normal_cdf(u):
    t = 1.0 / (1.0 + TAIL_P * jnp.abs(u))
    poly = TAIL[-1]
    for coef in TAIL[-2::-1]:
        poly = poly * t + coef
    bell = jnp.exp(u * u * -0.5)
    tail = bell * (t * poly)
    return jnp.where(u >= 0, 1.0 - tail, tail), bell


def ff_forward_kernel(chunk, h2_ref, w1a_ref, w1g_ref, w2_ref, b1a_ref, b1g_ref, rows_ref,
                      h3_ref, fa_ref, fg_ref, z_ref, norm_ref, acc_ref):
    step = pl.program_id(0)
    chunks = h2_ref.shape[0] // chunk

    @pl.when(step == 0)
    def _():
        def start(index, carry):
            rows = pl.ds(pl.multiple_of(index * chunk, chunk), chunk)
            hat, unused = normalize(h2_ref[rows])
            norm_ref[rows] = (hat * rows_ref[4:5] + rows_ref[5:6]).astype(BF16)
            acc_ref[rows] = jnp.zeros((chunk, h2_ref.shape[1]), F32)
            return carry

        lax.fori_loop(0, chunks, start, 0)

    def body(index, carry):
        rows = pl.ds(pl.multiple_of(index * chunk, chunk), chunk)
        norm3 = norm_ref[rows]
        gate = mm(norm3, w1g_ref[...]) + b1g_ref[...]
        cdf, bell = normal_cdf(gate)
        factor = gate * cdf
        value = mm(norm3, w1a_ref[...]) + b1a_ref[...]
        z = (value * factor).astype(BF16)
        z_ref[0, rows] = z
        fa_ref[0, rows] = factor
        fg_ref[0, rows] = value * (cdf + gate * bell * (2 * math.pi) ** -0.5)
        acc_ref[rows] += mm(z, w2_ref[...])
        return carry

    lax.fori_loop(0, chunks, body, 0)

    @pl.when(step == pl.num_programs(0) - 1)
    def _():
        h3_ref[...] = h2_ref[...] + acc_ref[...] + rows_ref[8:9]


def whole(shape):
    return pl.BlockSpec(shape, lambda step: (0,) * len(shape))


def params(**extra):
    return pltpu.CompilerParams(dimension_semantics=('arbitrary',), vmem_limit_bytes=62 * 1024 * 1024, **extra)


def cost(flops, moved):
    return pl.CostEstimate(flops=int(flops), bytes_accessed=int(moved), transcendentals=0)


def self_forward(h, w_qkv, w_out, rows, tokens):
    total, width = h.shape
    heads = width // HEAD
    row = lambda cols: pl.BlockSpec((PAIR_ROWS, cols), lambda step: (step, 0))
    return pl.pallas_call(
        lambda *refs: self_forward_kernel(heads, tokens, *refs),
        grid=(total // PAIR_ROWS,),
        in_specs=[row(width), whole(w_qkv.shape), whole(w_out.shape), whole(rows.shape)],
        out_specs=[row(width), row(3 * width), row(width)],
        out_shape=[jax.ShapeDtypeStruct((total, width), F32), jax.ShapeDtypeStruct((total, 3 * width), BF16),
                   jax.ShapeDtypeStruct((total, width), BF16)],
        compiler_params=params(), cost_estimate=cost(total * width * width * 10, 20e6), name='self_forward',
    )(h, w_qkv, w_out, rows)


def cross_forward(h1, context, w_q, w_kv, w_out, rows, tokens, ctx_len, samples):
    total, width = h1.shape
    heads = width // HEAD
    row = lambda cols: pl.BlockSpec((PAIR_ROWS, cols), lambda step: (step, 0))
    return pl.pallas_call(
        lambda *refs: cross_forward_kernel(heads, tokens, ctx_len, *refs),
        grid=(total // PAIR_ROWS,),
        in_specs=[row(width), whole(context.shape), whole(w_q.shape), whole(w_kv.shape), whole(w_out.shape),
                  whole(rows.shape)],
        out_specs=[row(width), row(width), whole((samples * SLOT, 2 * width)), row(width)],
        out_shape=[jax.ShapeDtypeStruct((total, width), F32), jax.ShapeDtypeStruct((total, width), BF16),
                   jax.ShapeDtypeStruct((samples * SLOT, 2 * width), BF16), jax.ShapeDtypeStruct((total, width), BF16)],
        compiler_params=params(), cost_estimate=cost(total * width * width * 8, 20e6), name='cross_forward',
    )(h1, context, w_q, w_kv, w_out, rows)


def ff_forward(h2, w1, w2, b1, rows, chunk):
    total, width = h2.shape
    inner = w2.shape[0]
    steps = inner // FF_COLS
    saved = pl.BlockSpec((1, total, FF_COLS), lambda step: (step, 0, 0))
    return pl.pallas_call(
        lambda *refs: ff_forward_kernel(chunk, *refs),
        grid=(steps,),
        in_specs=[whole(h2.shape), pl.BlockSpec((width, FF_COLS), lambda step: (0, step)),
                  pl.BlockSpec((width, FF_COLS), lambda step: (0, step + steps)),
                  pl.BlockSpec((FF_COLS, width), lambda step: (step, 0)),
                  pl.BlockSpec((1, FF_COLS), lambda step: (0, step)),
                  pl.BlockSpec((1, FF_COLS), lambda step: (0, step + steps)), whole(rows.shape)],
        out_specs=[whole(h2.shape), saved, saved, saved],
        out_shape=[jax.ShapeDtypeStruct((total, width), F32), jax.ShapeDtypeStruct((steps, total, FF_COLS), F32),
                   jax.ShapeDtypeStruct((steps, total, FF_COLS), F32), jax.ShapeDtypeStruct((steps, total, FF_COLS), BF16)],
        scratch_shapes=[pltpu.VMEM((total, width), BF16), pltpu.VMEM((total, width), F32)],
        compiler_params=params(), cost_estimate=cost(total * width * inner * 6, 60e6), name='ff_forward',
    )(h2, w1, w1, w2, b1, b1, rows)


UNIT = 80
MACRO = 3 * UNIT
SLOTS = 3
STREAMS = 2
STAGES = 4
ORDERS = ((2, 1, 0), (1, 0, 2), (0, 2, 1))
MESH = pl.DeviceIdType.MESH


class Place:
    def __init__(self):
        me = lax.axis_index(AXIS)
        self.bits = [lax.rem(lax.div(me, weight), 2) for weight in (8, 4, 2, 1)]
        self.others = [1 - bit for bit in self.bits]
        self.devices = [(me + (1 - 2 * bit) * weight,) for bit, weight in zip(self.bits, (8, 4, 2, 1))]

    def entry_barrier(self):
        barrier = pltpu.get_barrier_semaphore()
        for device in self.devices:
            pl.semaphore_signal(barrier, inc=1, device_id=device, device_id_type=MESH)
        pl.semaphore_wait(barrier, 4)


def pick(ref, lead, dim, value):
    return ref.at[(lead,) + (slice(None),) * dim + (value,)]


class At(NamedTuple):
    stream: Any
    index: Any
    row: Any


class Reducer:
    def __init__(self, place, macros, scale, grads, out, refs):
        self.place, self.macros, self.scale, self.grads, self.out = place, macros, scale, grads, out
        self.own, self.held = refs[0], refs[1:1 + STAGES]
        self.result, self.send, self.recv, self.load, self.store = refs[1 + STAGES:]

    @staticmethod
    def scratch():
        held = [pltpu.VMEM((STREAMS * SLOTS * 3,) + (2,) * (3 - stage) + (UNIT, LANES), F32) for stage in range(STAGES)]
        sems = [pltpu.SemaphoreType.DMA((STREAMS, 3, STAGES)), pltpu.SemaphoreType.DMA((STREAMS * SLOTS * 3, STAGES)),
                pltpu.SemaphoreType.DMA((STREAMS, 3)), pltpu.SemaphoreType.DMA((STREAMS,))]
        return [pltpu.VMEM((STREAMS * 3, 2, 2, 2, UNIT, LANES), F32)] + held + [
            pltpu.VMEM((STREAMS, MACRO, LANES), F32)] + sems

    def axis(self, color, stage):
        return 3 if stage == 0 else ORDERS[color][stage - 1]

    def dim(self, color, stage):
        gone = ORDERS[color][:stage - 1]
        return sum(1 for axis in range(ORDERS[color][stage - 1]) if axis not in gone)

    def copy(self, at, color, stage):
        axis = self.axis(color, stage)
        other = self.place.others[axis]
        index = at.index + color
        if stage == 0:
            source = self.grads.at[:, :, :, other, pl.ds(at.row + color * UNIT, UNIT)]
        else:
            source = pick(self.held[stage - 1], index, self.dim(color, stage), other)
        return pltpu.make_async_remote_copy(
            src_ref=source, dst_ref=self.held[stage].at[index], send_sem=self.send.at[at.stream, color, stage],
            recv_sem=self.recv.at[index, stage], device_id=self.place.devices[axis], device_id_type=MESH)

    def own_copy(self, at, color):
        return pltpu.make_async_copy(self.grads.at[:, :, :, self.place.bits[3], pl.ds(at.row + color * UNIT, UNIT)],
                                     self.own.at[at.stream * 3 + color], self.load.at[at.stream, color])

    def out_copy(self, stream, row):
        return pltpu.make_async_copy(self.result.at[stream], self.out.at[pl.ds(row, MACRO)], self.store.at[stream])

    def add(self, at, color, stage):
        index = at.index + color
        if stage == 0:
            self.held[0][index] += self.own[at.stream * 3 + color]
            return
        mine = self.held[stage - 1][(index,) + (slice(None),) * self.dim(color, stage)
                                    + (self.place.bits[self.axis(color, stage)],)]
        if stage < STAGES - 1:
            self.held[stage][index] += mine
        else:
            self.result[at.stream, color * UNIT:(color + 1) * UNIT] = (self.held[stage][index] + mine) * self.scale

    def step(self, t):
        stream, tau = lax.rem(t, STREAMS), lax.div(t, STREAMS)

        def when_live(local, body):
            @pl.when((local >= 0) & (local * STREAMS + stream < self.macros))
            def _():
                body(At(stream, (stream * SLOTS + lax.rem(local, SLOTS)) * 3,
                        pl.multiple_of((local * STREAMS + stream) * MACRO, 8)))

        def take(stage, at):
            for color in range(3):
                copy = self.copy(at, color, stage)
                copy.wait_send()
                copy.wait_recv()
                if stage == 0:
                    self.own_copy(at, color).wait()
            if stage == STAGES - 1:
                @pl.when(tau > STAGES)
                def _():
                    self.out_copy(stream, pl.multiple_of(at.row - STREAMS * MACRO, 8)).wait()
            for color in range(3):
                self.add(at, color, stage)
            if stage == STAGES - 1:
                self.out_copy(stream, at.row).start()

        def give(stage, at):
            for color in range(3):
                self.copy(at, color, stage).start()
                if stage == 0:
                    self.own_copy(at, color).start()

        for stage in reversed(range(STAGES)):
            when_live(tau - 1 - stage, functools.partial(take, stage))
        for stage in range(STAGES):
            when_live(tau - stage, functools.partial(give, stage))

    def run(self, start, count):
        lax.fori_loop(0, count, lambda index, carry: (self.step(start + index), carry)[1], 0)

    def finish(self, start):
        self.run(start, self.macros + STREAMS * STAGES - start)
        for stream in range(STREAMS):
            last = (self.macros - 1 - stream) // STREAMS * STREAMS + stream
            self.out_copy(stream, last * MACRO).wait()


def view(values, *lead):
    return values.reshape((2, 2, 2, 2) + lead + (LANES,))


def put_tiles(stage, values, first=0):
    rows = values.shape[0] // 16
    for tile in range(values.shape[1] // LANES):
        at = first + tile * rows
        stage[:, :, :, :, at:at + rows] = view(values[:, tile * LANES:(tile + 1) * LANES], rows)


class Layout:
    def __init__(self, width, ctx_width, blocks):
        unit = width // 16 * (width // LANES)
        self.ff1, self.ff2 = 0, 8 * unit
        self.kv2 = 12 * unit
        self.q2 = self.kv2 + ctx_width // 16 * (2 * width // LANES)
        self.out2 = self.q2 + unit
        self.qkv = self.out2 + unit
        self.out = self.qkv + 3 * unit
        self.block = self.out + unit
        self.vec = blocks * self.block
        self.vec_rows = -(-17 * width // 16 // LANES // 8) * 8
        used = self.vec + blocks * self.vec_rows
        self.macros = -(-used // MACRO)
        self.pad = self.macros * MACRO - used
        self.rows = self.macros * MACRO


NAMES = ('h', 'h1', 'h2', 'qkv', 'out1', 'q', 'kv', 'out2', 'fa', 'fg', 'z', 'w_qkv', 'w_out', 'w_q2', 'w_out2', 'w_ff1',
         'w_ff2', 'rows')


def backward_kernel(cfg, *refs):
    tokens, ctx_len, width, blocks, layout, total, plan = cfg
    heads = width // HEAD
    cot_ref, context_ref = refs[:2]
    saved = [dict(zip(NAMES, refs[2 + layer * len(NAMES):])) for layer in range(blocks)]
    refs = refs[2 + blocks * len(NAMES):]
    gx_ref, grads_ref, out_ref = refs[:3]
    grad_ref, hidden_ref, rows_ref, d_rows_ref, vec_ref, in_sems = refs[3:9]
    place = Place()
    reducer = Reducer(place, layout.macros, 1.0 / total, grads_ref, out_ref, refs[9:])
    count = grad_ref.shape[0]
    chunk = PAIR_ROWS
    chunks = count // chunk
    phases = [(layer, kind) for layer in reversed(range(blocks)) for kind in ('h2', 'h1', 'h')]

    def hidden_copy(index):
        layer, kind = phases[index]
        return pltpu.make_async_copy(saved[layer][kind], hidden_ref.at[index % 2], in_sems.at[index % 2])

    def rows_copy(layer):
        return pltpu.make_async_copy(saved[layer]['rows'], rows_ref.at[layer], in_sems.at[2 + layer])

    def base(layer):
        return (blocks - 1 - layer) * layout.block

    def region(row, size):
        return grads_ref.at[:, :, :, :, pl.ds(pl.multiple_of(row, 8), size)]

    def each_chunk(body):
        def one(index, carry):
            body(pl.ds(pl.multiple_of(index * chunk, chunk), chunk))
            return carry
        lax.fori_loop(0, chunks, one, 0)

    def ff_phase(layer, index, first):
        hidden = hidden_ref.at[index % 2]
        rows = rows_ref.at[layer]
        d_rows = d_rows_ref.at[layer]
        vec = vec_ref.at[layer]
        src = saved[layer]
        inner = src['w_ff2'].shape[0]
        steps = inner // FF_COLS
        start, lag, limit = first

        def scoped(norm_t, grad_bf, du, w1, acc, stage1, stage2, sem1, sem2):
            def begin(at):
                hat, unused = normalize(hidden[at])
                norm_t[:, at] = (hat * rows[4:5] + rows[5:6]).astype(BF16).T
                grad_bf[at] = grad_ref[at].astype(BF16)
                d_rows[8:9] += jnp.sum(grad_ref[at], axis=0, keepdims=True)
                acc[at] = jnp.zeros((chunk, width), F32)

            each_chunk(begin)

            def copy1(step):
                return pltpu.make_async_copy(stage1, region(base(layer) + layout.ff1 + step * 160, 160), sem1)

            def copy2(step, part):
                block = step * 8 + part
                shard = lax.div(block, 5)
                row = pl.multiple_of(base(layer) + layout.ff2 + lax.rem(block, 5) * 160, 8)
                bits = [lax.rem(lax.div(shard, weight), 2) for weight in (8, 4, 2, 1)]
                return pltpu.make_async_copy(stage2.at[part], grads_ref.at[(*bits, pl.ds(row, 160))], sem2.at[part])

            def wait(step):
                copy1(step).wait()
                for part in range(8):
                    copy2(step, part).wait()

            def body(idx, w1a, w1g, w2, fa, fg, z):
                step = idx.index[0]
                w1[:, :FF_COLS] = w1a[...]
                w1[:, FF_COLS:] = w1g[...]

                def part(number, sums):
                    at = pl.ds(pl.multiple_of(number * chunk, chunk), chunk)
                    dz = mm_nt(grad_bf[at], w2[...]).astype(BF16).astype(F32)
                    du_a = dz * fa[0, at]
                    du_g = dz * fg[0, at]
                    du[at, :FF_COLS] = du_a.astype(BF16)
                    du[at, FF_COLS:] = du_g.astype(BF16)
                    acc[at] += mm_nt(du[at], w1[...])
                    return (sums[0] + jnp.sum(du_a, axis=0, keepdims=True), sums[1] + jnp.sum(du_g, axis=0, keepdims=True))

                zero = jnp.zeros((1, FF_COLS), F32)
                sums = lax.fori_loop(0, chunks, part, (zero, zero))
                for half in range(2):
                    for tile in range(2):
                        row = 9 * width // LANES + half * (inner // LANES) + 2 * step + tile
                        vec[pl.ds(row, 1)] = sums[half][:, tile * LANES:(tile + 1) * LANES]

                @pl.when(step > 0)
                def _():
                    wait(step - 1)

                if limit > 0:
                    @pl.when((step >= lag) & (step < lag + limit))
                    def _():
                        reducer.step(start + step - lag)

                put_tiles(stage1, mm(norm_t[...], du[:, :FF_COLS]))
                put_tiles(stage1, mm(norm_t[...], du[:, FF_COLS:]), 80)
                d_w2 = mm_tn(z[0], grad_bf[...])
                for tile in range(width // LANES):
                    stage2[:, tile * 32:(tile + 1) * 32] = d_w2[:, tile * LANES:(tile + 1) * LANES].reshape(8, 32, LANES)
                copy1(step).start()
                for number in range(8):
                    copy2(step, number).start()

            column = pl.BlockSpec((width, FF_COLS), lambda step: (0, step))
            kept = pl.BlockSpec((1, count, FF_COLS), lambda step: (step, 0, 0))
            pltpu.emit_pipeline(
                body, grid=(steps,),
                in_specs=[column, pl.BlockSpec((width, FF_COLS), lambda step: (0, step + steps)),
                          pl.BlockSpec((FF_COLS, width), lambda step: (step, 0)), kept, kept, kept],
                _explicit_indices=True,
            )(src['w_ff1'], src['w_ff1'], src['w_ff2'], src['fa'], src['fg'], src['z'])

            def finish(at):
                d_res, d_gain, d_shift = norm_back(hidden[at], acc[at], rows[4:5])
                grad_ref[at] += d_res
                d_rows[4:5] += d_gain
                d_rows[5:6] += d_shift

            each_chunk(finish)
            wait(steps - 1)

        pl.run_scoped(scoped, pltpu.VMEM((width, count), BF16), pltpu.VMEM((count, width), BF16),
                      pltpu.VMEM((count, 2 * FF_COLS), BF16), pltpu.VMEM((width, 2 * FF_COLS), BF16),
                      pltpu.VMEM((count, width), F32), pltpu.VMEM((2, 2, 2, 2, 160, LANES), F32),
                      pltpu.VMEM((8, 160, LANES), F32), pltpu.SemaphoreType.DMA, pltpu.SemaphoreType.DMA((8,)))

    def attention_phase(layer, index, first, cross):
        hidden = hidden_ref.at[index % 2]
        rows = rows_ref.at[layer]
        d_rows = d_rows_ref.at[layer]
        src = saved[layer]
        steps = count // PAIR_ROWS
        per_step = PAIR_ROWS // tokens
        start, in_samples, in_tails = first
        gain, shift, bias = (2, 3, 7) if cross else (0, 1, 6)
        samples = count // tokens
        pad = context_ref.shape[0] // samples
        kv_rows_all = context_ref.shape[0] if cross else count

        def scoped(d_mix, d_q, d_kv, norm_t, d_wq, d_wout, stage, stage_out, sem, sem_out, context, kv, ctx_sems):
            if cross:
                loads = [pltpu.make_async_copy(context_ref, context, ctx_sems.at[0]),
                         pltpu.make_async_copy(src['kv'], kv, ctx_sems.at[1])]
                for copy in loads:
                    copy.start()
                d_wq[...] = jnp.zeros_like(d_wq)
                for copy in loads:
                    copy.wait()
            d_wout[...] = jnp.zeros_like(d_wout)

            def body(idx, qkv, mixed, w_in, w_out):
                step = idx.index[0]
                at_rows = pl.ds(pl.multiple_of(step * PAIR_ROWS, PAIR_ROWS), PAIR_ROWS)
                grad_bf = grad_ref[at_rows].astype(BF16)
                d_rows[bias:bias + 1] += jnp.sum(grad_ref[at_rows], axis=0, keepdims=True)
                d_wout[...] += mm_tn(mixed[...], grad_bf)
                d_mix[...] = mm_nt(grad_bf, w_out[...]).astype(BF16)

                def sample(number, carry):
                    at = pl.ds(pl.multiple_of(number * tokens, tokens), tokens)
                    sample_index = step * per_step + number
                    if cross:
                        kv_at = pl.ds(pl.multiple_of(sample_index * SLOT, SLOT), SLOT)
                        d_kv_at = pl.ds(pl.multiple_of(sample_index * pad, pad), pad)
                        d_q_at = at
                    else:
                        d_q_at = pl.ds(pl.multiple_of(sample_index * tokens, tokens), tokens)
                    for pair in range(heads // 2):
                        cols = slice(pair * LANES, (pair + 1) * LANES)
                        k_cols = slice(width + pair * LANES, width + (pair + 1) * LANES)
                        v_cols = slice(2 * width + pair * LANES, 2 * width + (pair + 1) * LANES)
                        if cross:
                            d_query, d_keys, d_values = pair_backward(qkv[at, cols], kv[kv_at, cols], kv[kv_at, k_cols],
                                                                      d_mix[at, cols], ctx_len)
                            d_kv[d_kv_at, cols] = d_keys[:pad]
                            d_kv[d_kv_at, k_cols] = d_values[:pad]
                        else:
                            d_query, d_keys, d_values = pair_backward(qkv[at, cols], qkv[at, k_cols], qkv[at, v_cols],
                                                                      d_mix[at, cols], tokens)
                            d_q[d_q_at, k_cols] = d_keys
                            d_q[d_q_at, v_cols] = d_values
                        d_q[d_q_at, cols] = d_query
                    @pl.when(sample_index < in_samples)
                    def _():
                        reducer.step(start + sample_index)

                    return carry

                lax.fori_loop(0, per_step, sample, 0)
                hat, unused = normalize(hidden[at_rows])
                norm = (hat * rows[gain:gain + 1] + rows[shift:shift + 1]).astype(BF16)
                if cross:
                    d_wq[...] += mm_tn(norm, d_q[...])
                    d_norm = mm_nt(d_q[...], w_in[...])
                else:
                    norm_t[:, at_rows] = norm.T
                    d_norm = mm_nt(d_q[at_rows], w_in[...])
                d_res, d_gain, d_shift = norm_back(hidden[at_rows], d_norm, rows[gain:gain + 1])
                grad_ref[at_rows] += d_res
                d_rows[gain:gain + 1] += d_gain
                d_rows[shift:shift + 1] += d_shift

            w_in, w_out = ('w_q2', 'w_out2') if cross else ('w_qkv', 'w_out')
            block = lambda ref: pl.BlockSpec((PAIR_ROWS, ref.shape[1]), lambda step: (step, 0))
            full = lambda ref: pl.BlockSpec(ref.shape, lambda step: (0, 0))
            operands = [src['q' if cross else 'qkv'], src['out2' if cross else 'out1'], src[w_in], src[w_out]]
            pltpu.emit_pipeline(
                body, grid=(steps,), in_specs=[block(operands[0]), block(operands[1]), full(operands[2]), full(operands[3])],
                _explicit_indices=True,
            )(*operands)
            where = base(layer) + (layout.out2 if cross else layout.out)
            size = width // 16 * (width // LANES)
            if cross:
                put_tiles(stage_out, d_wq[...])
                put_tiles(stage_out, d_wout[...], size)
                copy_out = pltpu.make_async_copy(stage_out, region(base(layer) + layout.q2, 2 * size), sem_out)
            else:
                put_tiles(stage_out, d_wout[...])
                copy_out = pltpu.make_async_copy(stage_out, region(where, size), sem_out)
            copy_out.start()
            rows_each = stage.shape[4]
            cols_each = stage.shape[4] // ((context_ref.shape[1] if cross else width) // 16) * LANES
            tails = (2 if cross else 3) * width // cols_each
            first_row = base(layer) + (layout.kv2 if cross else layout.qkv)

            def copy_tail(step):
                return pltpu.make_async_copy(stage, region(first_row + step * rows_each, rows_each), sem)

            def tail(step, carry):
                cols = pl.ds(pl.multiple_of(step * cols_each, cols_each), cols_each)
                result = mm_tn(context[...], d_kv[:, cols]) if cross else mm(norm_t[...], d_q[:, cols])

                @pl.when(step > 0)
                def _():
                    copy_tail(step - 1).wait()

                put_tiles(stage, result)
                copy_tail(step).start()
                if in_tails:
                    @pl.when(step < in_tails)
                    def _():
                        reducer.step(start + in_samples + step)

                return carry

            lax.fori_loop(0, tails, tail, 0)
            copy_tail(tails - 1).wait()
            copy_out.wait()

        small = pltpu.VMEM((8, LANES), BF16)
        size = width // 16 * (width // LANES)
        if cross:
            ctx_width = context_ref.shape[1]
            pl.run_scoped(scoped, pltpu.VMEM((PAIR_ROWS, width), BF16), pltpu.VMEM((PAIR_ROWS, width), BF16),
                          pltpu.VMEM((kv_rows_all, 2 * width), BF16), small, pltpu.VMEM((width, width), F32),
                          pltpu.VMEM((width, width), F32), pltpu.VMEM((2, 2, 2, 2, ctx_width // 16 * 2, LANES), F32),
                          pltpu.VMEM((2, 2, 2, 2, 2 * size, LANES), F32), pltpu.SemaphoreType.DMA,
                          pltpu.SemaphoreType.DMA, pltpu.VMEM(context_ref.shape, BF16),
                          pltpu.VMEM(src['kv'].shape, BF16), pltpu.SemaphoreType.DMA((2,)))
        else:
            pl.run_scoped(scoped, pltpu.VMEM((PAIR_ROWS, width), BF16), pltpu.VMEM((count, 3 * width), BF16), small,
                          pltpu.VMEM((width, count), BF16), small, pltpu.VMEM((width, width), F32),
                          pltpu.VMEM((2, 2, 2, 2, width // 16 * 3, LANES), F32),
                          pltpu.VMEM((2, 2, 2, 2, size, LANES), F32), pltpu.SemaphoreType.DMA,
                          pltpu.SemaphoreType.DMA, small, small, pltpu.SemaphoreType.DMA((2,)))

    place.entry_barrier()
    hidden_copy(0).start()
    for layer in range(blocks):
        rows_copy(layer).start()
    d_rows_ref[...] = jnp.zeros_like(d_rows_ref)
    vec_ref[...] = jnp.zeros_like(vec_ref)

    def load_cot(cot, sem):
        copy = pltpu.make_async_copy(cot_ref, cot, sem)
        copy.start()
        copy.wait()
        each_chunk(lambda at: grad_ref.__setitem__(at, cot[at].astype(F32)))

    pl.run_scoped(load_cot, pltpu.VMEM(cot_ref.shape, BF16), pltpu.SemaphoreType.DMA)
    for layer in range(blocks):
        rows_copy(layer).wait()
    for index, (layer, kind) in enumerate(phases):
        hidden_copy(index).wait()
        if index + 1 < len(phases):
            hidden_copy(index + 1).start()
        if kind == 'h2':
            ff_phase(layer, index, plan[index])
        else:
            attention_phase(layer, index, plan[index], kind == 'h1')

    def finish(stage, sem, image, sem_image):
        def cast(at):
            image[at] = grad_ref[at].astype(BF16)

        each_chunk(cast)
        copy_image = pltpu.make_async_copy(image, gx_ref, sem_image)
        copy_image.start()
        per_device = 17 * width // 16
        stage[...] = jnp.zeros_like(stage)
        for layer in range(blocks):
            vec = vec_ref.at[layer]
            for row in range(9):
                for tile in range(width // LANES):
                    at = row * (width // LANES) + tile
                    vec[at:at + 1] = d_rows_ref[layer, row:row + 1, tile * LANES:(tile + 1) * LANES]
            lane = lax.broadcasted_iota(jnp.int32, (8, LANES), 1)
            for shard in range(16):
                row, off = divmod(shard * per_device, LANES)
                here, after = vec[row:row + 8], vec[row + 1:row + 9]
                if off:
                    here = jnp.where(lane < LANES - off, pltpu.roll(here, LANES - off, 1), pltpu.roll(after, LANES - off, 1))
                stage[shard // 8, shard // 4 % 2, shard // 2 % 2, shard % 2,
                      layer * layout.vec_rows:(layer + 1) * layout.vec_rows] = here
        copy = pltpu.make_async_copy(stage, region(layout.vec, stage.shape[4]), sem)
        copy.start()
        copy.wait()
        reducer.finish(plan[-1])
        copy_image.wait()

    pl.run_scoped(finish, pltpu.VMEM((2, 2, 2, 2, blocks * layout.vec_rows + layout.pad, LANES), F32),
                  pltpu.SemaphoreType.DMA, pltpu.VMEM(cot_ref.shape, BF16), pltpu.SemaphoreType.DMA)


def backward(cot, context, saved, tokens, ctx_len, total):
    count, width = cot.shape
    blocks = len(saved)
    layout = Layout(width, context.shape[1], blocks)
    cfg = (tokens, ctx_len, width, blocks, layout, total, PLAN)
    operands = [cot, context]
    for block in saved:
        operands += [block[name] for name in NAMES]
    any_spec = pl.BlockSpec(memory_space=pl.ANY)
    shape = saved[0]['rows'].shape
    gx, unused, out = pl.pallas_call(
        lambda *refs: backward_kernel(cfg, *refs),
        in_specs=[any_spec] * len(operands), out_specs=[any_spec] * 3,
        out_shape=[jax.ShapeDtypeStruct((count, width), BF16),
                   jax.ShapeDtypeStruct((2, 2, 2, 2, layout.rows, LANES), F32),
                   jax.ShapeDtypeStruct((layout.rows, LANES), F32)],
        scratch_shapes=[pltpu.VMEM((count, width), F32), pltpu.VMEM((2, count, width), F32),
                        pltpu.VMEM((blocks,) + shape, F32), pltpu.VMEM((blocks,) + shape, F32),
                        pltpu.VMEM((blocks, 96, LANES), F32), pltpu.SemaphoreType.DMA((2 + blocks,))] + Reducer.scratch(),
        compiler_params=pltpu.CompilerParams(collective_id=0, has_side_effects=True, vmem_limit_bytes=63 * 1024 * 1024),
        cost_estimate=cost(110e9, 300e6), name='backward',
    )(*operands)
    return gx, out, layout


PLAN = [(0, 4, 6), (6, 4, 0), (10, 6, 1), (17, 0, 8), (25, 5, 0), (30, 6, 1), 37]


def gather(local):
    return lax.all_gather(local, AXIS, axis=0, tiled=True)


def ungrad(out, layout, layer, blocks, width, ctx_width):
    rows = out[(blocks - 1 - layer) * layout.block:(blocks - layer) * layout.block]
    part = width // 16
    tiles = width // LANES
    inner = 4 * width

    def square(first, count):
        return rows[first:first + count * tiles * part].reshape(count * tiles, part, LANES).swapaxes(0, 1).reshape(-1)

    ff1 = rows[:layout.ff2].reshape(inner // FF_COLS, 2, FF_COLS // LANES, part, LANES)
    ff1 = ff1.transpose(3, 1, 0, 2, 4).reshape(-1)
    ff2 = rows[layout.ff2:layout.kv2].reshape(inner // 16 // 32, tiles, 32, LANES).transpose(0, 2, 1, 3).reshape(-1)
    kv2 = rows[layout.kv2:layout.q2].reshape(2 * tiles, ctx_width // 16, LANES).swapaxes(0, 1).reshape(-1)
    return [square(layout.qkv, 3), square(layout.out, 1), square(layout.q2, 1), kv2, square(layout.out2, 1), ff1, ff2]


def solution(mesh):
    n_dev = mesh.shape[AXIS]

    def local(tokens_x, context, cot_out, *shards):
        samples, tokens, width = tokens_x.shape
        ctx_len, ctx_width = context.shape[1:]
        blocks = shards[0].shape[0]
        total = samples * n_dev
        chunk = PAIR_ROWS
        shapes = weight_shapes(width, ctx_width)
        pieces = [[shard[layer].reshape(shape[0] // n_dev, shape[1]) for shard, shape in zip(shards[:7], shapes[:7])]
                  for layer in range(blocks)]
        vecs = lax.all_gather(shards[7].reshape(1, blocks, -1), AXIS, axis=0, tiled=True)
        vecs = jnp.swapaxes(vecs, 0, 1).reshape(blocks, -1).astype(F32)
        pad = -(-ctx_len // 16) * 16
        ctx_rows = jnp.pad(context, ((0, 0), (0, pad - ctx_len), (0, 0))).reshape(samples * pad, ctx_width)
        h = tokens_x.reshape(samples * tokens, width).astype(F32)
        saved = []
        for layer in range(blocks):
            w_qkv, w_out, w_q2, w_kv2, w_out2, w_ff1, w_ff2 = pieces[layer]
            small = gather(jnp.concatenate([w_qkv, w_out, w_q2, w_out2], axis=1))
            w_qkv = small[:, :3 * width]
            w_out, w_q2, w_out2 = (small[:, index * width:(index + 1) * width] for index in range(3, 6))
            w_kv2, w_ff1, w_ff2 = gather(w_kv2), gather(w_ff1), gather(w_ff2)
            rows = jnp.pad(vecs[layer, :9 * width].reshape(9, width), ((0, 7), (0, 0)))
            b1 = vecs[layer, 9 * width:17 * width].reshape(1, 8 * width)
            h1, qkv, out1 = self_forward(h, w_qkv, w_out, rows, tokens)
            h2, q, kv, out2 = cross_forward(h1, ctx_rows, w_q2, w_kv2, w_out2, rows, tokens, ctx_len, samples)
            h3, fa, fg, z = ff_forward(h2, w_ff1, w_ff2, b1, rows, chunk)
            saved.append(dict(zip(NAMES, (h, h1, h2, qkv, out1, q, kv, out2, fa, fg, z, w_qkv, w_out, w_q2, w_out2, w_ff1,
                                          w_ff2, rows))))
            h = h3
        out_tokens = h.astype(BF16).reshape(tokens_x.shape)
        gx, out, layout = backward(cot_out.reshape(samples * tokens, width), ctx_rows, saved, tokens, ctx_len, total)
        results = [ungrad(out, layout, layer, blocks, width, ctx_width) for layer in range(blocks)]
        stacked = [jnp.stack([result[index] for result in results]) for index in range(7)]
        vec = out[layout.vec:layout.vec + blocks * layout.vec_rows].reshape(blocks, -1)[:, :17 * width // n_dev]
        return tuple([out_tokens, gx.reshape(tokens_x.shape)] + stacked + [vec])

    param_spec = P(None, AXIS)
    in_specs = (P(AXIS), P(AXIS), P(AXIS)) + (param_spec,) * 8
    out_specs = (P(AXIS), P(AXIS)) + (param_spec,) * 8
    return jax.shard_map(local, mesh=mesh, in_specs=in_specs, out_specs=out_specs, check_vma=False)
```

time: 1980 us -> 823 us (0.42)
  waiting for transfers between devices: 1360 us -> 121 us
  Pallas kernels: 493 us -> 566 us
  local copies, waits for them, and re-layouts: 50.3 us -> 78.9 us
    reduce_scatter x8 -> x0, waiting for transfers between devices: 665 us -> none  [scatter(): return lax.psum_scatter(grad, AXIS, scatter_dimension=0, tiled=True) / total]
    unnamed x36 -> x8, waiting for transfers between devices: 523 us -> 0.13 us
    pallas_call x6 -> x1, Pallas kernels: 304 us -> 377 us  [backward(): pl.pallas_call(lambda *refs: backward_kernel(cfg, *refs), in_specs=[any_s...]
    all_gather x10 -> x8, waiting for transfers between devices: 172 us -> 121 us  [gather(): return lax.all_gather(local, AXIS, axis=0, tiled=True)]
  transfers between devices with their start and end apart: 27 -> 8, of which waited for: 24 -> 5; matrix products, arithmetic and copies ran while one was open for 4% -> 5% of each run, Pallas kernels for 7% -> 17%
where the time goes in v3:
time: 823 us; the launch traced here: 814 us
  Pallas kernels  566 us (69%)
  waiting for transfers between devices  121 us (15%)
  local copies, waits for them, and re-layouts  78.9 us (10%)
  other arithmetic  17.9 us (2%)
  between operations  14.9 us (2%)
  blocking collectives  14.5 us (2%)
    pallas_call x1, Pallas kernels, backward(): pl.pallas_call(lambda *refs: backward_kernel(cfg, *refs), in_specs=[any_s...  377 us
    all_gather x8, waiting for transfers between devices, gather(): return lax.all_gather(local, AXIS, axis=0, tiled=True)  121 us
    pallas_call x2, Pallas kernels, ff_forward(): pl.pallas_call(lambda *refs: ff_forward_kernel(chunk, *refs), grid=(steps...  97.6 us
    pallas_call x2, Pallas kernels, self_forward(): pl.pallas_call(lambda *refs: self_forward_kernel(heads, tokens, *refs), g...  49.5 us
    pallas_call x2, Pallas kernels, cross_forward(): pl.pallas_call(lambda *refs: cross_forward_kernel(heads, tokens, ctx_len,...  42.3 us
    slice x7, local copies, waits for them, and re-layouts, local(): shard[layer].reshape(shape[0] // n_dev, shape[1])  26.6 us
  transfers between devices with their start and end apart: 8, of which 5 were waited for; matrix products, arithmetic and copies ran while one was open for 5% of the time, Pallas kernels for 17%

profile of v3, /device:TPU:0, one launch (start us, length us, event | category | flops | bytes accessed | tf_op | source)
XLA Modules:
  0.0 813.5 jit_solution(5263937401103873901)
XLA Ops:
  12.1 2.8 slice_reduce_fusion.6
  17.2 6.9 slice_reduce_fusion.2
  25.3 2.8 slice_reduce_fusion.4
  29.3 9.4 %slice_reduce_fusion = (bf16[204800]{0:T(1024)(128)(2,1)S(1)}, bf16[204800]{0:T(1024)(128)(2,1)}) fusion(bf16[2,204800]{1,0:T(2,128)(2,1)S(1)} %copy-done.3), kind=kLoop, calls=%fused_computation.6 | loop fusion | bytes 1638400 | tf_op jit(solution)/shard_map/slice | solution.py:824
  44.7 14.5 %all-gather.1 = bf16[16,2,680]{2,1,0:T(2,128)(2,1)S(1)} all-gather(bf16[1,2,680]{2,1,0:T(2,128)(2,1)S(1)} %bitcast.99), channel_id=2, replica_groups=mesh['fsdp'=16] {'fsdp'}, dimensions={0}, use_global_device_ids=true | all-gather | bytes 46240 | tf_op jit(solution)/shard_map/all_gather | solution.py:826
  62.3 2.3 bitcast_convert_fusion.refs_0_.refs_2_
  65.2 3.3 slice.184.refs_1_.refs_13_
  68.5 27.9 %all-gather.19.cloned.1.call-done = bf16[640,3840]{1,0:T(8,128)(2,1)} async-done(((bf16[40,3840]{1,0:T(8,128)(2,1)}), bf16[640,3840]{1,0:T(8,128)(2,1)}) %all-gather.19.cloned.1.call-update) | async-done | bytes 4915216 | tf_op jit(solution)/shard_map/all_gather | solution.py:795
  96.4 3.5 slice.190.refs_1_.refs_31_
  104.3 24.8 %self_forward.2 = (f32[1536,640]{1,0:T(8,128)}, bf16[1536,1920]{1,0:T(8,128)(2,1)}, bf16[1536,640]{1,0:T(8,128)(2,1)}) custom-call(f32[1536,640]{1,0:T(8,128)} %bitcast_convert_fusion.refs_0_.refs_2_, bf16[640,1920]{1,0:T(8,128)(2,1)} %slice.184.refs_1_.refs_13_, bf16[640,640]{1,0:T(8,128)(2,1)} %get-tuple-element.93.refs_2_.refs_14_, ...), custom_call_target="tpu_custom_call" | custom-call | flops 6291456000 | bytes 20000000 | tf_op jit(solution)/shard_map/self_forward/pallas_call | solution.py:224
  129.1 7.9 all-gather.13.cloned.1.call-done.refs_3_
  137.1 21.1 %cross_forward.2 = (f32[1536,640]{1,0:T(8,128)}, bf16[1536,640]{1,0:T(8,128)(2,1)}, bf16[768,1280]{1,0:T(8,128)(2,1)}, bf16[1536,640]{1,0:T(8,128)(2,1)}) custom-call(f32[1536,640]{1,0:T(8,128)} %get-tuple-element.34.refs_0_.refs_3_, bf16[480,2048]{1,0:T(8,128)(2,1)} %bitcast.77, bf16[640,640]{1,0:T(8,128)(2,1)} %get-tuple-element.92.refs_2_.refs_15_, ...), custom_call_target="tpu_custom_call" | custom-call | flops 5033164800 | bytes 20000000 | tf_op jit(solution)/shard_map/cross_forward/pallas_call | solution.py:239
  158.2 13.6 %all-gather.17.cloned.1.call-done.refs_3_.refs_18_ = bf16[2560,640]{1,0:T(8,128)(2,1)} async-done(((bf16[160,640]{1,0:T(8,128)(2,1)}), bf16[2560,640]{1,0:T(8,128)(2,1)}) %all-gather.17.cloned.1.call-update) | async-done | bytes 3276816 | tf_op jit(solution)/shard_map/all_gather | solution.py:795
  171.8 44.8 %all-gather.15.cloned.1.call-done.refs_1_.refs_2_.refs_17_ = bf16[640,5120]{1,0:T(8,128)(2,1)} async-done(((bf16[40,5120]{1,0:T(8,128)(2,1)}), bf16[640,5120]{1,0:T(8,128)(2,1)}) %all-gather.15.cloned.1.call-update) | async-done | bytes 6553616 | tf_op jit(solution)/shard_map/all_gather | solution.py:795
  216.6 48.8 %ff_forward.2 = (f32[1536,640]{1,0:T(8,128)}, f32[10,1536,256]{2,1,0:T(8,128)}, f32[10,1536,256]{2,1,0:T(8,128)}, bf16[10,1536,256]{2,1,0:T(8,128)(2,1)}) custom-call(f32[1536,640]{1,0:T(8,128)} %get-tuple-element.35.refs_0_.refs_4_, bf16[640,5120]{1,0:T(8,128)(2,1)} %all-gather.15.cloned.1.call-done.refs_1_.refs_2_.refs_17_, ...), custom_call_target="tpu_custom_call" | custom-call | flops 15099494400 | bytes 60000000 | tf_op jit(solution)/shard_map/ff_forward/pallas_call | solution.py:256
  265.3 24.6 %self_forward.3 = (f32[1536,640]{1,0:T(8,128)}, bf16[1536,1920]{1,0:T(8,128)(2,1)}, bf16[1536,640]{1,0:T(8,128)(2,1)}) custom-call(f32[1536,640]{1,0:T(8,128)} %get-tuple-element.36.refs_0_.refs_20_, bf16[640,1920]{1,0:T(8,128)(2,1)} %slice.190.refs_1_.refs_31_, bf16[640,640]{1,0:T(8,128)(2,1)} %get-tuple-element.90.refs_2_.refs_32_, ...), custom_call_target="tpu_custom_call" | custom-call | flops 6291456000 | bytes 20000000 | tf_op jit(solution)/shard_map/self_forward/pallas_call | solution.py:224
  290.0 21.1 %cross_forward.3 = (f32[1536,640]{1,0:T(8,128)}, bf16[1536,640]{1,0:T(8,128)(2,1)}, bf16[768,1280]{1,0:T(8,128)(2,1)}, bf16[1536,640]{1,0:T(8,128)(2,1)}) custom-call(f32[1536,640]{1,0:T(8,128)} %get-tuple-element.37.refs_0_.refs_21_, bf16[480,2048]{1,0:T(8,128)(2,1)} %bitcast.78, bf16[640,640]{1,0:T(8,128)(2,1)} %get-tuple-element.89.refs_2_.refs_33_, ...), custom_call_target="tpu_custom_call" | custom-call | flops 5033164800 | bytes 20000000 | tf_op jit(solution)/shard_map/cross_forward/pallas_call | solution.py:239
  311.1 26.4 %all-gather.23.cloned.1.call-done.refs_1_.refs_2_.refs_35_ = bf16[640,5120]{1,0:T(8,128)(2,1)} async-done(((bf16[40,5120]{1,0:T(8,128)(2,1)}), bf16[640,5120]{1,0:T(8,128)(2,1)}) %all-gather.23.cloned.1.call-update) | async-done | bytes 6553616 | tf_op jit(solution)/shard_map/all_gather | solution.py:795
  337.5 48.9 %ff_forward.3 = (f32[1536,640]{1,0:T(8,128)}, f32[10,1536,256]{2,1,0:T(8,128)}, f32[10,1536,256]{2,1,0:T(8,128)}, bf16[10,1536,256]{2,1,0:T(8,128)(2,1)}) custom-call(f32[1536,640]{1,0:T(8,128)} %get-tuple-element.38.refs_0_.refs_22_, bf16[640,5120]{1,0:T(8,128)(2,1)} %all-gather.23.cloned.1.call-done.refs_1_.refs_2_.refs_35_, ...), custom_call_target="tpu_custom_call" | custom-call | flops 15099494400 | bytes 60000000 | tf_op jit(solution)/shard_map/ff_forward/pallas_call | solution.py:256
  386.4 376.7 %backward.1 = (bf16[1536,640]{1,0:T(8,128)(2,1)}, f32[2,2,2,2,9840,128]{5,4,3,2,1,0:T(8,128)}, f32[9840,128]{1,0:T(8,128)}) custom-call(bf16[1536,640]{1,0:T(8,128)(2,1)} %bitcast.100, bf16[480,2048]{1,0:T(8,128)(2,1)} %bitcast.79, f32[1536,640]{1,0:T(8,128)} %bitcast_convert_fusion.refs_0_.refs_2_, f32[1536,640]{1,0:T(8,128)} %get-tuple-element.34.refs_0_.refs_3_, ...), custom_call_target="tpu_custom_call" | custom-call | flops 109999996928 | bytes 300000000 | tf_op jit(solution)/shard_map/backward/pallas_call | solution.py:776
  766.1 2.4 fusion.3
  792.4 2.4 pad_maximum_fusion.3
  794.8 3.2 pad_maximum_fusion.1
  799.8 2.4 pad_maximum_fusion
  (122 shorter events, 56.0 us)
Async XLA Ops:
  7.2 10.0 %copy-start.5 = (bf16[2,163840]{1,0:T(2,128)(2,1)S(1)}, bf16[2,163840]{1,0:T(2,128)(2,1)}, u32[]{:S(2)}) copy-start(bf16[2,163840]{1,0:T(2,128)(2,1)} %param.17) | copy-start | bytes 1966084
  7.2 18.1 %copy-start.9 = (bf16[2,102400]{1,0:T(2,128)(2,1)S(1)}, bf16[2,102400]{1,0:T(2,128)(2,1)}, u32[]{:S(2)}) copy-start(bf16[2,102400]{1,0:T(2,128)(2,1)} %param.20) | copy-start | bytes 1228804
  7.2 58.1 %all-gather.11.cloned.1.call-start = ((), (), s32[]{:S(2)}) async-start(), calls=%async_computation | async-start | bytes 5222400 | tf_op jit(solution)/shard_map/all_gather | solution.py:795
  14.9 14.3 %copy-start.3 = (bf16[2,204800]{1,0:T(2,128)(2,1)S(1)}, bf16[2,204800]{1,0:T(2,128)(2,1)}, u32[]{:S(2)}) copy-start(bf16[2,204800]{1,0:T(2,128)(2,1)} %param.19) | copy-start | bytes 2457604
  15.9 80.5 %all-gather.19.cloned.1.call-start = ((), (), s32[]{:S(2)}) async-start(), calls=%async_computation.4 | async-start | bytes 5222400 | tf_op jit(solution)/shard_map/all_gather | solution.py:795
  17.1 119.9 %all-gather.13.cloned.1.call-start = ((), (), s32[]{:S(2)}) async-start(), calls=%async_computation.1 | async-start | bytes 5570560 | tf_op jit(solution)/shard_map/all_gather | solution.py:795
  25.2 19.4 %copy-start.16 = (bf16[2,680]{1,0:T(2,128)(2,1)S(1)}, bf16[2,680]{1,0:T(2,128)(2,1)}, u32[]{:S(2)}) copy-start(bf16[2,680]{1,0:T(2,128)(2,1)} %param.21) | copy-start | bytes 8164
  25.3 146.5 %all-gather.17.cloned.1.call-start = ((), (), s32[]{:S(2)}) async-start(), calls=%async_computation.3 | async-start | bytes 3481600 | tf_op jit(solution)/shard_map/all_gather | solution.py:795
  29.0 31.8 %copy-start.6 = (bf16[6,77,2048]{2,1,0:T(8,128)(2,1)S(1)}, bf16[6,77,2048]{2,1,0:T(8,128)(2,1)}, u32[]{:S(2)}) copy-start(bf16[6,77,2048]{2,1,0:T(8,128)(2,1)} %param.12) | copy-start | bytes 5677060
  29.0 187.6 %all-gather.15.cloned.1.call-start = ((), (), s32[]{:S(2)}) async-start(), calls=%async_computation.2 | async-start | bytes 6963200 | tf_op jit(solution)/shard_map/all_gather | solution.py:795
  40.6 249.3 %all-gather.21.cloned.1.call-start = ((), (), s32[]{:S(2)}) async-start(), calls=%async_computation.5 | async-start | bytes 5570560 | tf_op jit(solution)/shard_map/all_gather | solution.py:795
  41.8 269.3 %all-gather.25.cloned.1.call-start = ((), (), s32[]{:S(2)}) async-start(), calls=%async_computation.7 | async-start | bytes 3481600 | tf_op jit(solution)/shard_map/all_gather | solution.py:795
  43.7 293.9 %all-gather.23.cloned.1.call-start = ((), (), s32[]{:S(2)}) async-start(), calls=%async_computation.6 | async-start | bytes 6963200 | tf_op jit(solution)/shard_map/all_gather | solution.py:795
  96.4 3.6 copy-start
  96.4 6.4 copy-start.1
  766.1 6.6 copy-start.2
  784.4 6.7 copy-start.10
  788.2 6.6 copy-start.4
  791.7 10.5 %copy-start.11 = (f32[1,102400]{1,0:T(1,128)S(1)}, f32[1,102400]{1,0:T(1,128)}, u32[]{:S(2)}) copy-start(f32[1,102400]{1,0:T(1,128)} %stack_reshape.55) | copy-start | bytes 1228804
  794.8 9.0 %copy-start.12 = (f32[1,25600]{1,0:T(1,128)S(1)}, f32[1,25600]{1,0:T(1,128)}, u32[]{:S(2)}) copy-start(f32[1,25600]{1,0:T(1,128)} %stack_reshape.45) | copy-start | bytes 307204
  794.8 9.0 %copy-start.13 = (f32[1,25600]{1,0:T(1,128)S(1)}, f32[1,25600]{1,0:T(1,128)}, u32[]{:S(2)}) copy-start(f32[1,25600]{1,0:T(1,128)} %stack_reshape.44) | copy-start | bytes 307204
  794.8 9.0 %copy-start.14 = (f32[1,25600]{1,0:T(1,128)S(1)}, f32[1,25600]{1,0:T(1,128)}, u32[]{:S(2)}) copy-start(f32[1,25600]{1,0:T(1,128)} %stack_reshape.47) | copy-start | bytes 307204
  794.8 9.0 %copy-start.15 = (f32[1,25600]{1,0:T(1,128)S(1)}, f32[1,25600]{1,0:T(1,128)}, u32[]{:S(2)}) copy-start(f32[1,25600]{1,0:T(1,128)} %stack_reshape.46) | copy-start | bytes 307204
  794.8 10.1 %copy-start.8 = (bf16[1536,640]{1,0:T(8,128)(2,1)S(1)}, bf16[1536,640]{1,0:T(8,128)(2,1)}, u32[]{:S(2)}) copy-start(bf16[1536,640]{1,0:T(8,128)(2,1)} %get-tuple-element.56) | copy-start | bytes 5898244
  (1 other events, 2.7 us)
Sparse Core Ops, SparseCore 0:
  16.0 40.1 all-gather.10
  59.1 37.2 all-gather.18
  98.6 38.3 all-gather.12
  139.7 32.0 all-gather.16
  173.9 42.6 all-gather.14
  218.7 38.3 all-gather.20
  259.9 32.0 all-gather.24
  294.8 42.6 all-gather.22

commit v4 on v3

v4 whole, which is shorter than its diff:
```python
import functools
import math
from typing import Any, NamedTuple
import jax
import jax.numpy as jnp
from jax import lax
from jax.experimental import pallas as pl
from jax.experimental.pallas import tpu as pltpu
from jax.sharding import PartitionSpec as P

AXIS = 'fsdp'
HEAD = 64
EPS = 1e-5
SHARDS = 16
CUBE = (2, 2, 2, 2)
WEIGHT = (8, 4, 2, 1)
CHIP_WEIGHT = WEIGHT[1:]
CHIPS = 8
SUB = 8
FULL = slice(None)
SELF_ROWS, CROSS_ROWS = (0, 1, 6), (2, 3, 7)
F32 = jnp.float32
BF16 = jnp.bfloat16
LANES = 128
VMEM_BYTES = 63 * 2 ** 20
BELL = (2 * math.pi) ** -0.5
SLOT = LANES
PAIR_ROWS = 512
FF_COLS = 256

TAIL_P = 0.265
TAIL = (0.10574158579953814, 0.10524628753634038, 0.10270369607548423, 0.0603023517537824, 0.13797880111692826,
        -0.11640058407079061, 0.2178489286936914, -0.1442454807654402, 0.03082441619112092)


def mm(lhs, rhs):
    return jnp.dot(lhs, rhs, preferred_element_type=F32)


def mm_nt(lhs, rhs):
    return lax.dot_general(lhs, rhs, (((1,), (1,)), ((), ())), preferred_element_type=F32)


def mm_tn(lhs, rhs):
    return lax.dot_general(lhs, rhs, (((0,), (0,)), ((), ())), preferred_element_type=F32)


pipeline = functools.partial(pltpu.emit_pipeline, _explicit_indices=True)


def lane_mean(x):
    return jnp.mean(x, axis=-1, keepdims=True)


def lane_sum(x):
    return jnp.sum(x, axis=-1, keepdims=True)


def row_sum(x):
    return jnp.sum(x, axis=0, keepdims=True)


def line(ref, index):
    return ref[index:index + 1]


def add_line(ref, index, values):
    ref[index:index + 1] += values


def span(index, size):
    return pl.ds(pl.multiple_of(index * size, size), size)


def lanes(tile):
    return slice(tile * LANES, (tile + 1) * LANES)


def repeat(count, body):
    def one(index, carry):
        body(index)
        return carry

    lax.fori_loop(0, count, one, 0)


def normalize(x):
    centered = x - lane_mean(x)
    scale = lax.rsqrt(lane_mean(centered * centered) + EPS)
    return centered * scale, scale


def norm_back(x, d_norm, gain):
    hat, scale = normalize(x)
    d_hat = d_norm * gain
    pulled = d_hat - lane_mean(d_hat) - hat * lane_mean(d_hat * hat)
    return pulled * scale, row_sum(d_norm * hat), row_sum(d_norm)


def low_half(rows):
    return lax.broadcasted_iota(jnp.int32, (rows, LANES), 1) < HEAD


def head_stack(pair, low):
    zero = jnp.zeros_like(pair)
    return jnp.concatenate([jnp.where(low, pair, zero), jnp.where(low, zero, pair)], axis=0)


def head_unstack(stacked, low):
    half = stacked.shape[0] // 2
    return jnp.where(low, stacked[:half], stacked[half:])


def softmax_halves(scores, valid):
    half = scores.shape[1] // 2
    parts = []
    for index in range(2):
        part = scores[:, index * half:(index + 1) * half]
        if valid < half:
            part = jnp.where(lax.broadcasted_iota(jnp.int32, part.shape, 1) < valid, part, -jnp.inf)
        part = jnp.exp(part - jnp.max(part, axis=-1, keepdims=True))
        parts.append(part * (1.0 / lane_sum(part)))
    return parts


def pair_forward(query, keys, values, valid):
    low = low_half(keys.shape[0])
    scores = mm_nt(query * BF16(HEAD ** -0.5), head_stack(keys, low))
    probs = jnp.concatenate([part.astype(BF16) for part in softmax_halves(scores, valid)], axis=1)
    return mm(probs, head_stack(values, low)).astype(BF16)


def pair_backward(query, keys, values, d_out, valid):
    low = low_half(keys.shape[0])
    half = keys.shape[0]
    query = query * BF16(HEAD ** -0.5)
    key_stack = head_stack(keys, low)
    value_stack = head_stack(values, low)
    parts = softmax_halves(mm_nt(query, key_stack), valid)
    probs = jnp.concatenate([part.astype(BF16) for part in parts], axis=1)
    d_values = head_unstack(mm_tn(probs, d_out), low).astype(BF16)
    d_probs = mm_nt(d_out, value_stack)
    d_scores = []
    for index in range(2):
        part, d_part = parts[index], d_probs[:, index * half:(index + 1) * half]
        d_scores.append((part * (d_part - lane_sum(part * d_part))).astype(BF16))
    d_scores = jnp.concatenate(d_scores, axis=1)
    d_query = (mm(d_scores, key_stack) * HEAD ** -0.5).astype(BF16)
    d_keys = head_unstack(mm_tn(d_scores, query), low).astype(BF16)
    return d_query, d_keys, d_values


def normal_cdf(u):
    t = 1.0 / (1.0 + TAIL_P * jnp.abs(u))
    poly = TAIL[-1]
    for coef in TAIL[-2::-1]:
        poly = poly * t + coef
    bell = jnp.exp(u * u * -0.5)
    tail = bell * (t * poly)
    return jnp.where(u >= 0, 1.0 - tail, tail), bell


UNIT = 80
COLORS = 3
MACRO = COLORS * UNIT
SLOTS = 3
STREAMS = 2
STAGES = 4
CORE = 3
ORDERS = ((2, 1, 0), (1, 0, 2), (0, 2, 1))
MESH = pl.DeviceIdType.MESH


def bits_of(device):
    return [lax.rem(lax.div(device, weight), 2) for weight in WEIGHT]


class Place:
    def __init__(self):
        me = lax.axis_index(AXIS)
        self.bits = bits_of(me)
        self.others = [1 - bit for bit in self.bits]
        self.devices = [(me + (other - bit) * weight,) for bit, other, weight in zip(self.bits, self.others, WEIGHT)]

    def rows_of(self, ref, first, rows):
        half = ref.shape[CORE] // 2
        return pl.ds(pl.multiple_of(self.bits[CORE] * half + first, SUB), rows)

    def own(self, ref):
        return ref.at[(*self.bits[:CORE], self.rows_of(ref, 0, ref.shape[CORE] // 2))]

    def entry_barrier(self):
        barrier = pltpu.get_barrier_semaphore()
        for device in self.devices:
            pl.semaphore_signal(barrier, inc=1, device_id=device, device_id_type=MESH)
        pl.semaphore_wait(barrier, 4)


def pick(ref, lead, dim, value):
    return ref.at[(lead,) + (FULL,) * dim + (value,)]


class At(NamedTuple):
    stream: Any
    index: Any
    row: Any


class Reducer:
    def __init__(self, place, macros, scale, grads, out, refs):
        self.place, self.macros, self.scale, self.grads, self.out = place, macros, scale, grads, out
        self.own, self.held = refs[0], refs[1:1 + STAGES]
        self.send, self.recv, self.load = refs[1 + STAGES:]

    @staticmethod
    def scratch():
        held = [pltpu.VMEM((STREAMS * SLOTS * COLORS,) + (2,) * (3 - stage) + (UNIT, LANES), F32) for stage in range(STAGES)]
        sems = [pltpu.SemaphoreType.DMA((STREAMS, COLORS, STAGES)), pltpu.SemaphoreType.DMA((STREAMS * SLOTS * COLORS, STAGES)),
                pltpu.SemaphoreType.DMA((STREAMS, COLORS))]
        return [pltpu.VMEM((STREAMS * COLORS, *CUBE[1:], UNIT, LANES), F32)] + held + sems

    def axis(self, color, stage):
        return CORE if stage == 0 else ORDERS[color][stage - 1]

    def dim(self, color, stage):
        gone = ORDERS[color][:stage - 1]
        return sum(1 for axis in range(ORDERS[color][stage - 1]) if axis not in gone)

    def copy(self, at, color, stage):
        axis = self.axis(color, stage)
        other = self.place.others[axis]
        index = at.index + color
        if stage == 0:
            source = self.grads.at[:, :, :, other, pl.ds(at.row + color * UNIT, UNIT)]
        else:
            source = pick(self.held[stage - 1], index, self.dim(color, stage), other)
        return pltpu.make_async_remote_copy(
            src_ref=source, dst_ref=self.held[stage].at[index], send_sem=self.send.at[at.stream, color, stage],
            recv_sem=self.recv.at[index, stage], device_id=self.place.devices[axis], device_id_type=MESH)

    def own_copy(self, at, color):
        return pltpu.make_async_copy(self.grads.at[:, :, :, self.place.bits[CORE], pl.ds(at.row + color * UNIT, UNIT)],
                                     self.own.at[at.stream * COLORS + color], self.load.at[at.stream, color])

    def add(self, at, color, stage):
        index = at.index + color
        if stage == 0:
            self.held[0][index] += self.own[at.stream * COLORS + color]
            return
        mine = self.held[stage - 1][(index,) + (FULL,) * self.dim(color, stage)
                                    + (self.place.bits[self.axis(color, stage)],)]
        if stage < STAGES - 1:
            self.held[stage][index] += mine
        else:
            self.out[pl.ds(at.row + color * UNIT, UNIT)] = (self.held[stage][index] + mine) * self.scale

    def step(self, t):
        stream, tau = lax.rem(t, STREAMS), lax.div(t, STREAMS)

        def when_live(local, body):
            @pl.when((local >= 0) & (local * STREAMS + stream < self.macros))
            def _():
                body(At(stream, (stream * SLOTS + lax.rem(local, SLOTS)) * COLORS,
                        pl.multiple_of((local * STREAMS + stream) * MACRO, SUB)))

        def take(stage, at):
            for color in range(COLORS):
                copy = self.copy(at, color, stage)
                copy.wait_send()
                copy.wait_recv()
                if stage == 0:
                    self.own_copy(at, color).wait()
            for color in range(COLORS):
                self.add(at, color, stage)

        def give(stage, at):
            for color in range(COLORS):
                self.copy(at, color, stage).start()
                if stage == 0:
                    self.own_copy(at, color).start()

        for stage in reversed(range(STAGES)):
            when_live(tau - 1 - stage, functools.partial(take, stage))
        for stage in range(STAGES):
            when_live(tau - stage, functools.partial(give, stage))


class Piece(NamedTuple):
    ref: Any
    first: Any
    rows: Any
    cols: Any
    color: int
    number: int


class Gatherer:
    def __init__(self, place, macros, send, recv):
        self.place, self.macros, self.send, self.recv = place, [], send, recv
        number = 0
        for macro in macros:
            pieces = []
            for ref, color, first, rows, cols in macro:
                pieces.append(Piece(ref, first, rows, cols, color, number))
                number += 1
            self.macros.append(pieces)

    def copy(self, piece, stage):
        order = ORDERS[piece.color]
        index = [FULL if axis in order[:stage] else self.place.bits[axis] for axis in range(CORE)]
        block = piece.ref.at[(*index, self.place.rows_of(piece.ref, piece.first, piece.rows), piece.cols)]
        axis = order[stage] if stage < CORE else CORE
        return pltpu.make_async_remote_copy(
            src_ref=block, dst_ref=block, send_sem=self.send.at[piece.number, stage],
            recv_sem=self.recv.at[piece.number, stage], device_id=self.place.devices[axis], device_id_type=MESH)

    def step(self, t):
        for macro, pieces in enumerate(self.macros):
            stage = t - macro
            if stage in range(1, STAGES + 1):
                for piece in pieces:
                    copy = self.copy(piece, stage - 1)
                    copy.wait_send()
                    copy.wait_recv()
            if stage in range(STAGES):
                for piece in pieces:
                    self.copy(piece, stage).start()

    def beside(self, index, plan):
        first, count = plan
        for number in range(count):
            @pl.when(index == 2 * number + 1)
            def _(number=number):
                self.step(first + number)


def thirds(tiles):
    edges = [round(tiles * part / 3) * LANES for part in range(4)]
    return [slice(first, last) for first, last in zip(edges[:-1], edges[1:])]


FORWARD_PLAN = [(5, 3), (8, 3), (11, 5), (SHARDS, 2), (0, 0), (0, 0)]
MATS = ('qkv', 'out', 'q2', 'kv2', 'out2', 'ff1', 'ff2')
WEIGHTS = ('w_a', 'w_b', 'w_kv2', 'w_ff1', 'w_ff2')
KEPT = ('h', 'h1', 'h2', 'qkv', 'out1', 'q', 'kv', 'out2', 'fa', 'fg', 'z', 'rows')


def load(source, target, sem):
    copy = pltpu.make_async_copy(source, target, sem)
    copy.start()
    return copy


def fetch(source, cols, target, sems):
    def copy(shard):
        index = [lax.rem(lax.div(shard, weight), 2) for weight in CHIP_WEIGHT]
        return pltpu.make_async_copy(source.at[(*index, FULL, cols)], target.at[span(shard, source.shape[CORE])],
                                     sems.at[shard])

    repeat(CHIPS, lambda shard: copy(shard).start())
    return lambda: repeat(CHIPS, lambda shard: copy(shard).wait())


def macro_list(weights, vec):
    macros = []
    for block in weights:
        high = {name: block[name].shape[CORE] // 2 for name in WEIGHTS}
        cols = {name: thirds(block[name].shape[-1] // LANES) for name in ('w_a', 'w_b', 'w_kv2')}
        wide = block['w_ff1'].shape[-1] // 2

        def add(name, first, rows, cols):
            macros.append([(block[name], color, first, rows, part) for color, part in enumerate(cols)])

        add('w_a', 0, high['w_a'], cols['w_a'])
        for part in range(2):
            add('w_kv2', part * high['w_kv2'] // 2, high['w_kv2'] // 2, cols['w_kv2'])
        add('w_b', 0, high['w_b'], cols['w_b'])
        for part in range(2):
            add('w_ff1', 0, high['w_ff1'],
                [pl.ds(part * wide + third.start, third.stop - third.start) for third in thirds(wide // LANES)])
        tenth = high['w_ff2'] // 10
        macros.append([(block['w_ff2'], color, first * tenth, rows * tenth, FULL)
                       for color, (first, rows) in enumerate(((0, 3), (3, 4), (7, 3)))])
    macros[0].append((vec, 0, 0, vec.shape[CORE] // 2, FULL))
    return macros


def forward_kernel(cfg, *refs):
    tokens, width, blocks, per_vec = cfg
    heads = width // HEAD
    tiles = width // LANES
    tokens_ref, context_ref = refs[:2]
    raw_refs = refs[2:2 + len(MATS) + 1]
    refs = refs[2 + len(raw_refs):]
    kept = [dict(zip(KEPT, refs[layer * len(KEPT):])) for layer in range(blocks)]
    refs = refs[blocks * len(KEPT):]
    weights = [dict(zip(WEIGHTS, refs[layer * len(WEIGHTS):])) for layer in range(blocks)]
    refs = refs[blocks * len(WEIGHTS):]
    vec_all_ref, ctx_out_ref, tokens_out_ref, hidden, context, rows_ref, vec_ref, sems, send, recv = refs
    samples, ctx_len = context_ref.shape[:2]
    pad = context.shape[0] // samples
    count = tokens_ref.shape[0]
    chunk = PAIR_ROWS
    per_step = chunk // tokens
    place = Place()
    gatherer = Gatherer(place, macro_list(weights, vec_all_ref), send, recv)

    def each_chunk(body):
        repeat(count // chunk, lambda index: body(span(index, chunk)))

    def startup(image, wide, flat, vec_piece, raws, pieces, raw_sems, own_sems):
        first = [load(tokens_ref, image, sems.at[0]), load(context_ref, wide, sems.at[1])]
        loads = [load(source, target, raw_sems.at[index])
                 for index, (source, target) in enumerate(zip(raw_refs, raws))]

        def tile(layer, name, target, first_col):
            raw = raws[MATS.index(name)]
            total = raw.shape[0]
            flat[:total] = raw[:, layer].astype(F32)
            rows = target.shape[0]
            many = total // rows
            for index in range(many):
                at = first_col + index * LANES
                target[:, at:at + LANES] = flat[pl.ds(index, rows, stride=many)].astype(BF16)

        def own(layer, name):
            number = layer * len(WEIGHTS) + WEIGHTS.index(name)
            return load(pieces[number], place.own(weights[layer][name]), own_sems.at[number])

        def prepare(layer, name):
            target = pieces[layer * len(WEIGHTS) + WEIGHTS.index(name)]
            if name == 'w_a':
                tile(layer, 'qkv', target, 0)
                tile(layer, 'out', target, 3 * width)
            elif name == 'w_b':
                tile(layer, 'q2', target, 0)
                tile(layer, 'out2', target, width)
            else:
                tile(layer, name[2:], target, 0)
            return own(layer, name)

        for copy in loads:
            copy.wait()
        vec_piece[:] = jnp.zeros_like(vec_piece)
        for layer in range(blocks):
            flat[:per_vec] = raws[-1][:, layer].astype(F32)
            vec_piece[layer * SUB:layer * SUB + per_vec] = flat[:per_vec].astype(BF16)
        pending = [prepare(0, 'w_a'), load(vec_piece, place.own(vec_all_ref), sems.at[2])]
        place.entry_barrier()
        later = [[(0, 'w_kv2')], [(0, 'w_b'), (0, 'w_ff1'), (0, 'w_ff2')], [(1, 'w_a'), (1, 'w_kv2'), (1, 'w_b')],
                 [(1, 'w_ff1'), (1, 'w_ff2')]]
        for t, jobs in enumerate(later):
            for copy in pending:
                copy.wait()
            gatherer.step(t)
            pending = [prepare(layer, name) for layer, name in jobs if layer < blocks]
        for copy in first:
            copy.wait()
        each_chunk(lambda at: hidden.at[0].__setitem__(at, image[at].astype(F32)))
        context[:] = jnp.zeros_like(context)
        for sample in range(samples):
            context[sample * pad:sample * pad + ctx_len] = wide[sample]
        for copy in pending:
            copy.wait()
        gatherer.step(len(later))

    def raw_shape(index):
        return pltpu.VMEM(raw_refs[index].shape, BF16)

    pl.run_scoped(startup, pltpu.VMEM(tokens_ref.shape, BF16), pltpu.VMEM(context_ref.shape, BF16),
                  pltpu.VMEM((max(ref.shape[0] for ref in raw_refs), LANES), F32), pltpu.VMEM((blocks * SUB, LANES), BF16),
                  [raw_shape(index) for index in range(len(raw_refs))],
                  [pltpu.VMEM((block[name].shape[CORE] // 2, block[name].shape[-1]), BF16)
                   for block in weights for name in WEIGHTS],
                  pltpu.SemaphoreType.DMA((len(raw_refs),)), pltpu.SemaphoreType.DMA((blocks * len(WEIGHTS),)))
    ctx_copy = load(context, ctx_out_ref, sems.at[3])

    def unpack(parts, sem):
        load(vec_all_ref, parts, sem).wait()
        vec_ref[:] = jnp.zeros_like(vec_ref)
        rows_ref[:] = jnp.zeros_like(rows_ref)
        lane = lax.broadcasted_iota(jnp.int32, (SUB, LANES), 1)
        per_device = 17 * width // SHARDS
        for layer in range(blocks):
            vec = vec_ref.at[layer]
            for shard in range(SHARDS):
                chip, core = divmod(shard, 2)
                bits = [chip // weight % 2 for weight in CHIP_WEIGHT]
                part = parts[(*bits, pl.ds((core * blocks + layer) * SUB, SUB))].astype(F32)
                row, off = divmod(shard * per_device, LANES)
                if off:
                    part = pltpu.roll(part, off, 1)
                    vec[pl.ds(row + 1, SUB)] += jnp.where(lane < off, part, 0.0)
                vec[pl.ds(row, SUB)] += jnp.where(lane >= off, part, 0.0)
            for row in range(9):
                for tile in range(tiles):
                    rows_ref[layer, row:row + 1, lanes(tile)] = line(vec, row * tiles + tile)

    pl.run_scoped(unpack, pltpu.VMEM(vec_all_ref.shape, BF16), pltpu.SemaphoreType.DMA)
    rows_copies = [load(rows_ref.at[layer], kept[layer]['rows'], sems.at[4 + layer]) for layer in range(blocks)]

    def attention(layer, source, target, cross, plan):
        rows = rows_ref.at[layer]
        packed = weights[layer]['w_b' if cross else 'w_a']
        inner = packed.shape[-1] - width
        gain, shift, bias = CROSS_ROWS if cross else SELF_ROWS

        def scoped(w_in, w_out, w_kv, kv, in_sems):
            waits = [fetch(packed, pl.ds(0, inner), w_in, in_sems.at[0]), fetch(packed, pl.ds(inner, width), w_out, in_sems.at[1])]
            if cross:
                fetch(weights[layer]['w_kv2'], FULL, w_kv, in_sems.at[2])()
                fresh = mm(context[:], w_kv[:]).astype(BF16)
                for index in range(samples):
                    kv[index * SLOT:index * SLOT + pad] = fresh[index * pad:(index + 1) * pad]
                    kv[index * SLOT + pad:(index + 1) * SLOT] = jnp.zeros((SLOT - pad, 2 * width), BF16)
                kv_copy = load(kv, kept[layer]['kv'], in_sems.at[2, 0])
            for wait in waits:
                wait()

            def body(idx, qkv, mixed):
                step = idx.index[0]
                at_rows = span(step, chunk)
                hat, unused = normalize(source[at_rows])
                norm = (hat * line(rows, gain) + line(rows, shift)).astype(BF16)
                qkv[:] = mm(norm, w_in[:]).astype(BF16)

                def sample(number):
                    at = span(number, tokens)
                    index = step * per_step + number
                    for pair in range(heads // 2):
                        cols, k_cols, v_cols = (slice(part * width + pair * LANES, part * width + (pair + 1) * LANES)
                                                for part in range(COLORS))
                        if cross:
                            kv_at = span(index, SLOT)
                            mixed[at, cols] = pair_forward(qkv[at, cols], kv[kv_at, cols], kv[kv_at, k_cols], ctx_len)
                        else:
                            mixed[at, cols] = pair_forward(qkv[at, cols], qkv[at, k_cols], qkv[at, v_cols], tokens)
                    gatherer.beside(index, plan)

                repeat(per_step, sample)
                target[at_rows] = source[at_rows] + mm(mixed[:], w_out[:]) + line(rows, bias)

            block = lambda cols: pl.BlockSpec((chunk, cols), lambda step: (step, 0))
            pipeline(body, grid=(count // chunk,), out_specs=[block(inner), block(width)])(
                kept[layer]['q' if cross else 'qkv'], kept[layer]['out2' if cross else 'out1'])
            if cross:
                kv_copy.wait()

        small = pltpu.VMEM((SUB, LANES), BF16)
        pl.run_scoped(scoped, pltpu.VMEM((width, inner), BF16), pltpu.VMEM((width, width), BF16),
                      pltpu.VMEM((context_ref.shape[2], 2 * width), BF16) if cross else small,
                      pltpu.VMEM((samples * SLOT, 2 * width), BF16) if cross else small, pltpu.SemaphoreType.DMA((3, CHIPS)))

    def feed_forward(layer, source, target, plan):
        rows = rows_ref.at[layer]
        vec = vec_ref.at[layer]
        inner = weights[layer]['w_ff1'].shape[-1] // 2
        steps = inner // FF_COLS
        part = FF_COLS // LANES

        def scoped(norm, w1, w2, w_sems):
            waits = [fetch(weights[layer]['w_ff1'], FULL, w1, w_sems.at[0]), fetch(weights[layer]['w_ff2'], FULL, w2, w_sems.at[1])]

            def begin(at):
                hat, unused = normalize(source[at])
                norm[at] = (hat * line(rows, 4) + line(rows, 5)).astype(BF16)
                target[at] = source[at] + line(rows, SUB)

            each_chunk(begin)
            for wait in waits:
                wait()

            def body(idx, fa, fg, z):
                step = idx.index[0]
                cols, gate_cols = span(step, FF_COLS), span(step + steps, FF_COLS)

                def bias(half):
                    first = 9 * tiles + (half * steps + step) * part
                    return jnp.concatenate([vec[pl.ds(first + index, 1)] for index in range(part)], axis=1)

                bias_a, bias_g = bias(0), bias(1)

                def one(at):
                    gate = mm(norm[at], w1[:, gate_cols]) + bias_g
                    cdf, bell = normal_cdf(gate)
                    factor = gate * cdf
                    value = mm(norm[at], w1[:, cols]) + bias_a
                    z[at] = (value * factor).astype(BF16)
                    fa[at] = factor
                    fg[at] = value * (cdf + gate * bell * BELL)
                    target[at] += mm(z[at], w2[cols])

                each_chunk(one)
                gatherer.beside(step, plan)

            block = ff_block(count)
            pipeline(body, grid=(steps,), out_specs=[block, block, block])(
                kept[layer]['fa'], kept[layer]['fg'], kept[layer]['z'])

        pl.run_scoped(scoped, pltpu.VMEM((count, width), BF16), pltpu.VMEM((width, 2 * inner), BF16),
                      pltpu.VMEM((inner, width), BF16), pltpu.SemaphoreType.DMA((2, CHIPS)))

    phases = len(FORWARD_PLAN)
    saves = [load(hidden.at[0], kept[0]['h'], sems.at[6]), None]
    for phase in range(phases):
        layer, kind = divmod(phase, 3)
        source, target = hidden.at[phase % 2], hidden.at[(phase + 1) % 2]
        other = (phase + 1) % 2
        if saves[other] is not None:
            saves[other].wait()
        if kind < 2:
            attention(layer, source, target, kind == 1, FORWARD_PLAN[phase])
        else:
            feed_forward(layer, source, target, FORWARD_PLAN[phase])
        following = divmod(phase + 1, 3)
        saves[other] = None
        if phase + 1 < phases:
            saves[other] = load(target, kept[following[0]][KEPT[following[1]]], sems.at[6 + other])

    def finish(image):
        each_chunk(lambda at: image.__setitem__(at, hidden[phases % 2, at].astype(BF16)))
        load(image, tokens_out_ref, sems.at[0]).wait()

    pl.run_scoped(finish, pltpu.VMEM(tokens_ref.shape, BF16))
    for copy in [copy for copy in saves if copy is not None] + [ctx_copy] + rows_copies:
        copy.wait()


def settings(number):
    return dict(compiler_params=pltpu.CompilerParams(collective_id=number, has_side_effects=True,
                                                     vmem_limit_bytes=VMEM_BYTES),
                cost_estimate=pl.CostEstimate(flops=10 ** 11, bytes_accessed=10 ** 8, transcendentals=0))


def ff_block(count):
    return pl.BlockSpec((None, count, FF_COLS), lambda step: (step, 0, 0))


def any_specs(count):
    return [pl.BlockSpec(memory_space=pl.ANY)] * count


def forward(tokens_x, context, raws):
    samples, tokens, width = tokens_x.shape
    ctx_width = context.shape[2]
    blocks = raws[0].shape[1]
    count, inner = samples * tokens, 4 * width
    pad = -(-context.shape[1] // SHARDS) * SHARDS
    steps = inner // FF_COLS
    plain = jax.ShapeDtypeStruct((count, width), F32)
    half = jax.ShapeDtypeStruct((count, width), BF16)
    wide = jax.ShapeDtypeStruct((steps, count, FF_COLS), F32)
    kept = [plain, plain, plain, jax.ShapeDtypeStruct((count, 3 * width), BF16), half, half,
            jax.ShapeDtypeStruct((samples * SLOT, 2 * width), BF16), half, wide, wide,
            jax.ShapeDtypeStruct(wide.shape, BF16), jax.ShapeDtypeStruct((SHARDS, width), F32)]
    whole_of = lambda rows, cols: jax.ShapeDtypeStruct((*CUBE[:CORE], rows // CHIPS, cols), BF16)
    weights = [whole_of(width, 4 * width), whole_of(width, 2 * width), whole_of(ctx_width, 2 * width),
               whole_of(width, 2 * inner), whole_of(inner, width)]
    extra = [whole_of(SHARDS * blocks * SUB, LANES), jax.ShapeDtypeStruct((samples * pad, ctx_width), BF16), half]
    shapes = kept * blocks + weights * blocks + extra
    pieces = 1 + 3 * 7 * blocks
    outs = pl.pallas_call(
        functools.partial(forward_kernel, (tokens, width, blocks, raws[-1].shape[0])),
        in_specs=any_specs(2 + len(raws)), out_specs=any_specs(len(shapes)), out_shape=shapes,
        scratch_shapes=[pltpu.VMEM((2, count, width), F32), pltpu.VMEM((samples * pad, ctx_width), BF16),
                        pltpu.VMEM((blocks, SHARDS, width), F32), pltpu.VMEM((blocks, 96, LANES), F32),
                        pltpu.SemaphoreType.DMA((8,)), pltpu.SemaphoreType.DMA((pieces, STAGES)),
                        pltpu.SemaphoreType.DMA((pieces, STAGES))],
        name='forward', **settings(1),
    )(tokens_x.reshape(count, width), context, *raws)
    kept_of = [outs[layer * len(kept):(layer + 1) * len(kept)] for layer in range(blocks)]
    outs = outs[blocks * len(kept):]
    weights_of = [[whole.reshape(-1, whole.shape[-1]) for whole in outs[layer * len(weights):(layer + 1) * len(weights)]]
                  for layer in range(blocks)]
    saved = [dict(zip(KEPT + WEIGHTS, list(one) + list(two))) for one, two in zip(kept_of, weights_of)]
    return saved, outs[-2], outs[-1]


def view(values, *lead):
    return values.reshape(CUBE + lead + (LANES,))


def put_tiles(stage, values, first=0):
    rows = values.shape[0] // SHARDS
    for tile in range(values.shape[1] // LANES):
        at = first + tile * rows
        stage[:, :, :, :, at:at + rows] = view(values[:, lanes(tile)], rows)


class Layout:
    def __init__(self, width, ctx_width, blocks):
        unit = width // SHARDS * (width // LANES)
        self.ff1, self.ff2 = 0, 8 * unit
        self.kv2 = 12 * unit
        self.q2 = self.kv2 + ctx_width // SHARDS * (2 * width // LANES)
        self.out2 = self.q2 + unit
        self.qkv = self.out2 + unit
        self.out = self.qkv + 3 * unit
        self.block = self.out + unit
        self.vec = blocks * self.block
        self.vec_rows = -(-17 * width // SHARDS // LANES // SUB) * SUB
        used = self.vec + blocks * self.vec_rows
        self.macros = -(-used // MACRO)
        self.pad = self.macros * MACRO - used
        self.rows = self.macros * MACRO


NAMES = KEPT + WEIGHTS


def backward_kernel(cfg, *refs):
    tokens, ctx_len, width, blocks, layout, total, plan = cfg
    heads = width // HEAD
    cot_ref, context_ref = refs[:2]
    saved = [dict(zip(NAMES, refs[2 + layer * len(NAMES):])) for layer in range(blocks)]
    refs = refs[2 + blocks * len(NAMES):]
    gx_ref, grads_ref = refs[:2]
    out_refs, refs = refs[2:3 + len(MATS)], refs[3 + len(MATS):]
    grad_ref, hidden_ref, rows_ref, d_rows_ref, vec_ref, out_ref, in_sems = refs[:7]
    place = Place()
    reducer = Reducer(place, layout.macros, 1.0 / total, grads_ref, out_ref, refs[7:])
    count = grad_ref.shape[0]
    chunk = PAIR_ROWS
    chunks = count // chunk
    phases = [(layer, kind) for layer in reversed(range(blocks)) for kind in ('h2', 'h1', 'h')]

    def hidden_copy(index):
        layer, kind = phases[index]
        return pltpu.make_async_copy(saved[layer][kind], hidden_ref.at[index % 2], in_sems.at[index % 2])

    def rows_copy(layer):
        return pltpu.make_async_copy(saved[layer]['rows'], rows_ref.at[layer], in_sems.at[2 + layer])

    def base(layer):
        return (blocks - 1 - layer) * layout.block

    def region(row, size):
        return grads_ref.at[:, :, :, :, pl.ds(pl.multiple_of(row, SUB), size)]

    def each_chunk(body):
        def one(index, carry):
            body(span(index, chunk))
            return carry
        lax.fori_loop(0, chunks, one, 0)

    def ff_phase(layer, index, first):
        hidden = hidden_ref.at[index % 2]
        rows = rows_ref.at[layer]
        d_rows = d_rows_ref.at[layer]
        vec = vec_ref.at[layer]
        src = saved[layer]
        w1_all, w2_all = src['w_ff1'], src['w_ff2']
        inner = w2_all.shape[0]
        steps = inner // FF_COLS
        start, lag, limit = first

        def scoped(norm_t, grad_bf, du, w1, acc, stage1, stage2, sem1, sem2):
            def begin(at):
                hat, unused = normalize(hidden[at])
                norm_t[:, at] = (hat * line(rows, 4) + line(rows, 5)).astype(BF16).T
                grad_bf[at] = grad_ref[at].astype(BF16)
                add_line(d_rows, 8, row_sum(grad_ref[at]))
                acc[at] = jnp.zeros((chunk, width), F32)

            each_chunk(begin)

            def copy1(step):
                return pltpu.make_async_copy(stage1, region(base(layer) + layout.ff1 + step * 160, 160), sem1)

            def copy2(step, part):
                block = step * 8 + part
                shard = lax.div(block, 5)
                row = pl.multiple_of(base(layer) + layout.ff2 + lax.rem(block, 5) * 160, SUB)
                bits = bits_of(shard)
                return pltpu.make_async_copy(stage2.at[part], grads_ref.at[(*bits, pl.ds(row, 160))], sem2.at[part])

            def wait(step):
                copy1(step).wait()
                for part in range(8):
                    copy2(step, part).wait()

            def body(idx, w1a, w1g, w2, fa, fg, z):
                step = idx.index[0]
                w1[:, :FF_COLS] = w1a[:]
                w1[:, FF_COLS:] = w1g[:]

                def part(number, sums):
                    at = span(number, chunk)
                    dz = mm_nt(grad_bf[at], w2[:]).astype(BF16).astype(F32)
                    du_a = dz * fa[at]
                    du_g = dz * fg[at]
                    du[at, :FF_COLS] = du_a.astype(BF16)
                    du[at, FF_COLS:] = du_g.astype(BF16)
                    acc[at] += mm_nt(du[at], w1[:])
                    return (sums[0] + row_sum(du_a), sums[1] + row_sum(du_g))

                zero = jnp.zeros((1, FF_COLS), F32)
                sums = lax.fori_loop(0, chunks, part, (zero, zero))
                for half in range(2):
                    for tile in range(2):
                        row = 9 * width // LANES + half * (inner // LANES) + 2 * step + tile
                        vec[pl.ds(row, 1)] = sums[half][:, lanes(tile)]

                @pl.when(step > 0)
                def _():
                    wait(step - 1)

                if limit > 0:
                    @pl.when((step >= lag) & (step < lag + limit))
                    def _():
                        reducer.step(start + step - lag)

                put_tiles(stage1, mm(norm_t[:], du[:, :FF_COLS]))
                put_tiles(stage1, mm(norm_t[:], du[:, FF_COLS:]), 80)
                d_w2 = mm_tn(z[:], grad_bf[:])
                for tile in range(width // LANES):
                    stage2[:, tile * 32:(tile + 1) * 32] = d_w2[:, lanes(tile)].reshape(8, 32, LANES)
                copy1(step).start()
                for number in range(8):
                    copy2(step, number).start()

            column = pl.BlockSpec((width, FF_COLS), lambda step: (0, step))
            kept = ff_block(count)
            pipeline(
                body, grid=(steps,),
                in_specs=[column, pl.BlockSpec((width, FF_COLS), lambda step: (0, step + steps)),
                          pl.BlockSpec((FF_COLS, width), lambda step: (step, 0)), kept, kept, kept],
            )(w1_all, w1_all, w2_all, src['fa'], src['fg'], src['z'])

            def finish(at):
                d_res, d_gain, d_shift = norm_back(hidden[at], acc[at], line(rows, 4))
                grad_ref[at] += d_res
                add_line(d_rows, 4, d_gain)
                add_line(d_rows, 5, d_shift)

            each_chunk(finish)
            wait(steps - 1)

        pl.run_scoped(scoped, pltpu.VMEM((width, count), BF16), pltpu.VMEM((count, width), BF16),
                      pltpu.VMEM((count, 2 * FF_COLS), BF16), pltpu.VMEM((width, 2 * FF_COLS), BF16),
                      pltpu.VMEM((count, width), F32), pltpu.VMEM((*CUBE, 160, LANES), F32),
                      pltpu.VMEM((8, 160, LANES), F32), pltpu.SemaphoreType.DMA, pltpu.SemaphoreType.DMA((8,)))

    def attention_phase(layer, index, first, cross):
        hidden = hidden_ref.at[index % 2]
        rows = rows_ref.at[layer]
        d_rows = d_rows_ref.at[layer]
        src = saved[layer]
        packed = src['w_b' if cross else 'w_a']
        inner = packed.shape[1] - width
        steps = count // PAIR_ROWS
        per_step = PAIR_ROWS // tokens
        start, in_samples, in_tails = first
        gain, shift, bias = CROSS_ROWS if cross else SELF_ROWS
        samples = count // tokens
        pad = context_ref.shape[0] // samples
        kv_rows_all = context_ref.shape[0] if cross else count

        def scoped(d_mix, d_q, d_kv, norm_t, d_wq, d_wout, stage, stage_out, sem, sem_out, w_in, w_out, in_sems_, context, kv, ctx_sems):
            if cross:
                loads = [pltpu.make_async_copy(context_ref, context, ctx_sems.at[0]),
                         pltpu.make_async_copy(src['kv'], kv, ctx_sems.at[1])]
                for copy in loads:
                    copy.start()
                d_wq[:] = jnp.zeros_like(d_wq)
                for copy in loads:
                    copy.wait()
            d_wout[:] = jnp.zeros_like(d_wout)
            for copy in [load(packed.at[:, pl.ds(0, inner)], w_in, in_sems_.at[0]),
                         load(packed.at[:, pl.ds(inner, width)], w_out, in_sems_.at[1])]:
                copy.wait()

            def body(idx, qkv, mixed):
                step = idx.index[0]
                at_rows = span(step, PAIR_ROWS)
                grad_bf = grad_ref[at_rows].astype(BF16)
                add_line(d_rows, bias, row_sum(grad_ref[at_rows]))
                d_wout[:] += mm_tn(mixed[:], grad_bf)
                d_mix[:] = mm_nt(grad_bf, w_out[:]).astype(BF16)

                def sample(number, carry):
                    at = span(number, tokens)
                    sample_index = step * per_step + number
                    if cross:
                        kv_at = span(sample_index, SLOT)
                        d_kv_at = span(sample_index, pad)
                        d_q_at = at
                    else:
                        d_q_at = span(sample_index, tokens)
                    for pair in range(heads // 2):
                        cols = lanes(pair)
                        k_cols = slice(width + pair * LANES, width + (pair + 1) * LANES)
                        v_cols = slice(2 * width + pair * LANES, 2 * width + (pair + 1) * LANES)
                        if cross:
                            d_query, d_keys, d_values = pair_backward(qkv[at, cols], kv[kv_at, cols], kv[kv_at, k_cols],
                                                                      d_mix[at, cols], ctx_len)
                            d_kv[d_kv_at, cols] = d_keys[:pad]
                            d_kv[d_kv_at, k_cols] = d_values[:pad]
                        else:
                            d_query, d_keys, d_values = pair_backward(qkv[at, cols], qkv[at, k_cols], qkv[at, v_cols],
                                                                      d_mix[at, cols], tokens)
                            d_q[d_q_at, k_cols] = d_keys
                            d_q[d_q_at, v_cols] = d_values
                        d_q[d_q_at, cols] = d_query
                    @pl.when(sample_index < in_samples)
                    def _():
                        reducer.step(start + sample_index)

                    return carry

                lax.fori_loop(0, per_step, sample, 0)
                hat, unused = normalize(hidden[at_rows])
                norm = (hat * line(rows, gain) + line(rows, shift)).astype(BF16)
                if cross:
                    d_wq[:] += mm_tn(norm, d_q[:])
                    d_norm = mm_nt(d_q[:], w_in[:])
                else:
                    norm_t[:, at_rows] = norm.T
                    d_norm = mm_nt(d_q[at_rows], w_in[:])
                d_res, d_gain, d_shift = norm_back(hidden[at_rows], d_norm, line(rows, gain))
                grad_ref[at_rows] += d_res
                add_line(d_rows, gain, d_gain)
                add_line(d_rows, shift, d_shift)

            block = lambda ref: pl.BlockSpec((PAIR_ROWS, ref.shape[1]), lambda step: (step, 0))
            operands = [src['q' if cross else 'qkv'], src['out2' if cross else 'out1']]
            pipeline(
                body, grid=(steps,), in_specs=[block(operands[0]), block(operands[1])],
            )(*operands)
            where = base(layer) + (layout.out2 if cross else layout.out)
            size = width // SHARDS * (width // LANES)
            if cross:
                put_tiles(stage_out, d_wq[:])
                put_tiles(stage_out, d_wout[:], size)
                copy_out = pltpu.make_async_copy(stage_out, region(base(layer) + layout.q2, 2 * size), sem_out)
            else:
                put_tiles(stage_out, d_wout[:])
                copy_out = pltpu.make_async_copy(stage_out, region(where, size), sem_out)
            copy_out.start()
            rows_each = stage.shape[4]
            cols_each = stage.shape[4] // ((context_ref.shape[1] if cross else width) // SHARDS) * LANES
            tails = (2 if cross else 3) * width // cols_each
            first_row = base(layer) + (layout.kv2 if cross else layout.qkv)

            def copy_tail(step):
                return pltpu.make_async_copy(stage, region(first_row + step * rows_each, rows_each), sem)

            def tail(step, carry):
                cols = span(step, cols_each)
                result = mm_tn(context[:], d_kv[:, cols]) if cross else mm(norm_t[:], d_q[:, cols])

                @pl.when(step > 0)
                def _():
                    copy_tail(step - 1).wait()

                put_tiles(stage, result)
                copy_tail(step).start()
                if in_tails:
                    @pl.when(step < in_tails)
                    def _():
                        reducer.step(start + in_samples + step)

                return carry

            lax.fori_loop(0, tails, tail, 0)
            copy_tail(tails - 1).wait()
            copy_out.wait()

        small = pltpu.VMEM((SUB, LANES), BF16)
        w_scratch = [pltpu.VMEM((width, inner), BF16), pltpu.VMEM((width, width), BF16), pltpu.SemaphoreType.DMA((2,))]
        size = width // SHARDS * (width // LANES)
        if cross:
            ctx_width = context_ref.shape[1]
            pl.run_scoped(scoped, pltpu.VMEM((PAIR_ROWS, width), BF16), pltpu.VMEM((PAIR_ROWS, width), BF16),
                          pltpu.VMEM((kv_rows_all, 2 * width), BF16), small, pltpu.VMEM((width, width), F32),
                          pltpu.VMEM((width, width), F32), pltpu.VMEM((*CUBE, ctx_width // SHARDS * 2, LANES), F32),
                          pltpu.VMEM((*CUBE, 2 * size, LANES), F32), pltpu.SemaphoreType.DMA,
                          pltpu.SemaphoreType.DMA, *w_scratch, pltpu.VMEM(context_ref.shape, BF16),
                          pltpu.VMEM(src['kv'].shape, BF16), pltpu.SemaphoreType.DMA((2,)))
        else:
            pl.run_scoped(scoped, pltpu.VMEM((PAIR_ROWS, width), BF16), pltpu.VMEM((count, 3 * width), BF16), small,
                          pltpu.VMEM((width, count), BF16), small, pltpu.VMEM((width, width), F32),
                          pltpu.VMEM((*CUBE, width // SHARDS * 3, LANES), F32),
                          pltpu.VMEM((*CUBE, size, LANES), F32), pltpu.SemaphoreType.DMA,
                          pltpu.SemaphoreType.DMA, *w_scratch, small, small, pltpu.SemaphoreType.DMA((2,)))

    place.entry_barrier()
    hidden_copy(0).start()
    for layer in range(blocks):
        rows_copy(layer).start()
    d_rows_ref[:] = jnp.zeros_like(d_rows_ref)
    vec_ref[:] = jnp.zeros_like(vec_ref)

    def load_cot(cot, sem):
        copy = pltpu.make_async_copy(cot_ref, cot, sem)
        copy.start()
        copy.wait()
        each_chunk(lambda at: grad_ref.__setitem__(at, cot[at].astype(F32)))

    pl.run_scoped(load_cot, pltpu.VMEM(cot_ref.shape, BF16), pltpu.SemaphoreType.DMA)
    for layer in range(blocks):
        rows_copy(layer).wait()
    for index, (layer, kind) in enumerate(phases):
        hidden_copy(index).wait()
        if index + 1 < len(phases):
            hidden_copy(index + 1).start()
        if kind == 'h2':
            ff_phase(layer, index, plan[index])
        else:
            attention_phase(layer, index, plan[index], kind == 'h1')

    def finish(stage, sem, image, sem_image, vec_out, images, out_sems):
        def cast(at):
            image[at] = grad_ref[at].astype(BF16)

        each_chunk(cast)
        copy_image = pltpu.make_async_copy(image, gx_ref, sem_image)
        copy_image.start()
        per_device = 17 * width // SHARDS
        stage[:] = jnp.zeros_like(stage)
        for layer in range(blocks):
            vec = vec_ref.at[layer]
            for row in range(9):
                for tile in range(width // LANES):
                    at = row * (width // LANES) + tile
                    vec[at:at + 1] = d_rows_ref[layer, row:row + 1, lanes(tile)]
            lane = lax.broadcasted_iota(jnp.int32, (SUB, LANES), 1)
            for shard in range(SHARDS):
                row, off = divmod(shard * per_device, LANES)
                here, after = vec[pl.ds(row, SUB)], vec[pl.ds(row + 1, SUB)]
                if off:
                    here = jnp.where(lane < LANES - off, pltpu.roll(here, LANES - off, 1), pltpu.roll(after, LANES - off, 1))
                bits = [shard // weight % 2 for weight in WEIGHT]
                stage[(*bits, pl.ds(layer * layout.vec_rows, layout.vec_rows))] = here
        copy = pltpu.make_async_copy(stage, region(layout.vec, stage.shape[4]), sem)
        copy.start()
        copy.wait()

        def convert(layer, name):
            target = images[MATS.index(name)]
            first = base(layer) + getattr(layout, name)
            part = width // SHARDS
            total = target.shape[0]
            many = total // (context_ref.shape[1] // SHARDS if name == 'kv2' else part)

            def put(tile, size, stride, row):
                target[pl.ds(tile, size, stride=stride), layer] = out_ref[row:row + size]

            if name == 'ff1':
                for index in range(many):
                    half, at = divmod(index, many // 2)
                    step, tile = divmod(at, 2)
                    put(index, part, many, first + step * 160 + half * 80 + tile * part)
            elif name == 'ff2':
                tiles = width // LANES
                for block in range(total // 160):
                    for tile in range(tiles):
                        put(block * 160 + tile, 32, tiles, first + block * 160 + tile * 32)
            else:
                for index in range(many):
                    put(index, total // many, many, first + index * (total // many))

        jobs = [(blocks - 1, name) for name in MATS] + [(0, name) for name in ('ff1', 'ff2', '', 'kv2', 'q2', 'out2')]

        def tail(index):
            reducer.step(plan[-1] + index)
            for number, (layer, name) in enumerate(jobs):
                if name:
                    @pl.when(index == min(number, layout.macros + STREAMS * STAGES - plan[-1] - 1))
                    def _(layer=layer, name=name):
                        convert(layer, name)

        repeat(layout.macros + STREAMS * STAGES - plan[-1], tail)
        convert(0, 'qkv')
        convert(0, 'out')
        copies = [load(source, target, out_sems.at[number])
                  for number, (source, target) in enumerate(zip(images, out_refs))]
        for layer in range(blocks):
            for row in range(-(-per_device // LANES)):
                at = layout.vec + layer * layout.vec_rows + row
                size = min(LANES, per_device - row * LANES)
                vec_out[layer:layer + 1, row * LANES:row * LANES + size] = line(out_ref, at)[:, :size]
        load(vec_out, out_refs[-1], sem).wait()
        for copy in copies:
            copy.wait()
        copy_image.wait()

    pl.run_scoped(finish, pltpu.VMEM((*CUBE, blocks * layout.vec_rows + layout.pad, LANES), F32),
                  pltpu.SemaphoreType.DMA, pltpu.VMEM(cot_ref.shape, BF16), pltpu.SemaphoreType.DMA,
                  pltpu.VMEM(out_refs[-1].shape, F32), [pltpu.VMEM(ref.shape, F32) for ref in out_refs[:-1]],
                  pltpu.SemaphoreType.DMA((len(MATS),)))


def backward(cot, context, saved, tokens, ctx_len, total, out_shapes):
    count, width = cot.shape
    blocks = len(saved)
    layout = Layout(width, context.shape[1], blocks)
    cfg = (tokens, ctx_len, width, blocks, layout, total, PLAN)
    operands = [cot, context]
    for block in saved:
        operands += [block[name] for name in NAMES]
    shape = saved[0]['rows'].shape
    outs = pl.pallas_call(
        functools.partial(backward_kernel, cfg),
        in_specs=any_specs(len(operands)), out_specs=any_specs(3 + len(MATS)),
        out_shape=[jax.ShapeDtypeStruct((count, width), BF16),
                   jax.ShapeDtypeStruct((*CUBE, layout.rows, LANES), F32)]
        + [jax.ShapeDtypeStruct(shape, F32) for shape in out_shapes],
        scratch_shapes=[pltpu.VMEM((count, width), F32), pltpu.VMEM((2, count, width), F32),
                        pltpu.VMEM((blocks,) + shape, F32), pltpu.VMEM((blocks,) + shape, F32),
                        pltpu.VMEM((blocks, 96, LANES), F32), pltpu.VMEM((layout.rows, LANES), F32),
                        pltpu.SemaphoreType.DMA((2 + blocks,))] + Reducer.scratch(),
        name='backward', **settings(0),
    )(*operands)
    return outs[0], outs[2:]


PLAN = [(0, 4, 6), (6, 4, 0), (10, 6, 1), (17, 0, SUB), (25, 5, 0), (30, 6, 1), 37]


def solution(mesh):
    n_dev = mesh.shape[AXIS]

    def local(tokens_x, context, cot_out, *shards):
        samples, tokens, width = tokens_x.shape
        blocks = shards[0].shape[0]
        spare = -shards[-1].shape[1] % LANES
        padded = shards[:-1] + (jnp.pad(shards[-1], ((0, 0), (0, spare))),)
        raws = [shard.reshape(blocks, -1, LANES).swapaxes(0, 1) for shard in padded]
        saved, ctx_rows, out_tokens = forward(tokens_x, context, raws)
        out_shapes = [raw.shape for raw in raws[:-1]] + [shards[-1].shape]
        grad_x, grads = backward(cot_out.reshape(samples * tokens, width), ctx_rows, saved, tokens, context.shape[1],
                                 samples * n_dev, out_shapes)
        grads = [grad.swapaxes(0, 1).reshape(blocks, -1) for grad in grads[:-1]] + [grads[-1]]
        return (out_tokens.reshape(tokens_x.shape), grad_x.reshape(tokens_x.shape), *grads)

    param_spec = P(None, AXIS)
    in_specs = (P(AXIS), P(AXIS), P(AXIS)) + (param_spec,) * 8
    out_specs = (P(AXIS), P(AXIS)) + (param_spec,) * 8
    return jax.shard_map(local, mesh=mesh, in_specs=in_specs, out_specs=out_specs, check_vma=False)
```

time: 823 us -> 651 us (0.79)
  waiting for transfers between devices: 121 us -> 0 us
  local copies, waits for them, and re-layouts: 78.9 us -> 12.3 us
  Pallas kernels: 566 us -> 630 us
  other arithmetic: 17.9 us -> 0 us
  blocking collectives: 14.5 us -> 0 us
  between operations: 14.9 us -> 1.13 us
    all_gather x8 -> x0, waiting for transfers between devices: 121 us -> none  [gather(): return lax.all_gather(local, AXIS, axis=0, tiled=True)]
    pallas_call x7 -> x2, Pallas kernels: 566 us -> 630 us  [the longest x1 375 us: backward(): pl.pallas_call(functools.partial(backward_kernel, cfg), in_specs=any_spec...]
    slice x20 -> x0, local copies, waits for them, and re-layouts: 47.3 us -> none  [the longest x7 26.6 us: local(): shard[layer].reshape(shape[0] // n_dev, shape[1])]
    another operation x28 -> x0, local copies, waits for them, and re-layouts: 19.5 us -> none  [the longest x12 11.1 us: local(): jnp.stack([result[index] for result in results])]
    all_gather x1 -> x0, blocking collectives: 14.5 us -> none  [local(): lax.all_gather(shards[7].reshape(1, blocks, -1), AXIS, axis=0, tiled=True)]
    another operation x6 -> x0, other arithmetic: 12.5 us -> none  [local(): jnp.stack([result[index] for result in results])]
    unnamed x35 -> x28, local copies, waits for them, and re-layouts: 2.74 us -> 11 us
  transfers between devices with their start and end apart: 8 -> 0, of which waited for: 5 -> 0; matrix products, arithmetic and copies ran while one was open for 5% -> 0% of each run, Pallas kernels for 17% -> 0%
where the time goes in v4:
time: 651 us; the launch traced here: 644 us
  Pallas kernels  630 us (97%)
  local copies, waits for them, and re-layouts  12.3 us (2%)
    pallas_call x1, Pallas kernels, backward(): pl.pallas_call(functools.partial(backward_kernel, cfg), in_specs=any_spec...  375 us
    pallas_call x1, Pallas kernels, forward(): pl.pallas_call(functools.partial(forward_kernel, (tokens, width, blocks,...  255 us

profile of v4, /device:TPU:0, one launch (start us, length us, event | category | flops | bytes accessed | tf_op | source)
XLA Modules:
  0.0 643.9 jit_solution(13809357927684099125)
XLA Ops:
  0.6 1.3 pad_bitcast_fusion.refs_9_
  1.9 255.3 %forward.1 = (f32[1536,640]{1,0:T(8,128)}, f32[1536,640]{1,0:T(8,128)}, f32[1536,640]{1,0:T(8,128)}, bf16[1536,1920]{1,0:T(8,128)(2,1)}, bf16[1536,640]{1,0:T(8,...) custom-call(bf16[1536,640]{1,0:T(8,128)(2,1)} %bitcast.69, ...), custom_call_target="tpu_custom_call" | custom-call | flops 99999997952 | bytes 100000000 | tf_op jit(solution)/shard_map/forward/pallas_call | solution.py:662
  257.2 375.2 %backward.1 = (bf16[1536,640]{1,0:T(8,128)(2,1)}, f32[2,2,2,2,9840,128]{5,4,3,2,1,0:T(8,128)}, f32[600,2,128]{2,1,0:T(2,128)}, f32[200,2,128]{2,1,0:T(2,128)}, f...) custom-call(bf16[1536,640]{1,0:T(8,128)(2,1)} %bitcast.70, ...), custom_call_target="tpu_custom_call" | custom-call | flops 99999997952 | bytes 100000000 | tf_op jit(solution)/shard_map/backward/pallas_call | solution.py:1103
  632.4 0.0 copy-start
  632.4 0.0 copy-start.4
  632.4 3.1 copy.31
  635.5 0.0 copy-done
  635.5 1.3 copy.32
  636.8 0.0 copy-done.4
  636.8 0.8 copy.33
  637.6 0.0 copy-done.7
  637.6 0.7 copy.34
  638.3 0.0 copy-done.6
  638.3 0.7 copy.35
  639.0 0.0 copy-done.2
  639.0 1.1 copy.36
  640.1 0.0 copy-done.5
  640.1 0.7 copy.37
  640.8 0.0 copy-done.1
  640.8 1.2 copy.38
  641.9 0.0 copy-done.3
  641.9 0.9 copy.39
  642.8 0.0 copy-done.8
  642.8 0.6 copy.40
  (7 shorter events, 0.0 us)
Async XLA Ops:
  632.4 3.2 copy-start
  632.4 4.4 copy-start.4
  635.5 2.1 copy-start.7
  635.5 2.8 copy-start.6
  635.5 3.5 copy-start.2
  636.8 3.3 copy-start.5
  636.8 3.9 copy-start.1
  638.3 3.6 copy-start.3
  640.1 2.7 copy-start.8

commit v5 on v4

--- a/solution.py
+++ b/solution.py
@@ -24,8 +24,9 @@
 LANES = 128
 VMEM_BYTES = 63 * 2 ** 20
 BELL = (2 * math.pi) ** -0.5
-SLOT = LANES
+LN_ROWS = 128
 PAIR_ROWS = 512
+FF_ROWS = 256
 FF_COLS = 256
 
 TAIL_P = 0.265
@@ -70,6 +71,10 @@
 
 def span(index, size):
     return pl.ds(pl.multiple_of(index * size, size), size)
+
+
+def pieces_of(first, size):
+    return [pl.ds(pl.multiple_of(first + piece * LN_ROWS, LN_ROWS), LN_ROWS) for piece in range(size // LN_ROWS)]
 
 
 def lanes(tile):
@@ -112,42 +117,62 @@
 
 
 def softmax_halves(scores, valid):
-    half = scores.shape[1] // 2
+    half = scores.shape[0] // 2
     parts = []
-    for index in range(2):
-        part = scores[:, index * half:(index + 1) * half]
+    for part in (scores[:half], scores[half:]):
         if valid < half:
-            part = jnp.where(lax.broadcasted_iota(jnp.int32, part.shape, 1) < valid, part, -jnp.inf)
-        part = jnp.exp(part - jnp.max(part, axis=-1, keepdims=True))
-        parts.append(part * (1.0 / lane_sum(part)))
+            part = jnp.where(lax.broadcasted_iota(jnp.int32, part.shape, 0) < valid, part, -jnp.inf)
+        part = jnp.exp(part - jnp.max(part, axis=0, keepdims=True))
+        parts.append(part * (1.0 / row_sum(part)))
     return parts
 
 
-def pair_forward(query, keys, values, valid):
+def stack_bf16(parts):
+    return jnp.concatenate([part.astype(BF16) for part in parts], axis=0)
+
+
+def rows_at(number):
+    return slice(number * FF_ROWS, (number + 1) * FF_ROWS)
+
+
+def ahead(count, first, second):
+    ready = first(0)
+    for index in range(count):
+        now = ready
+        if index + 1 < count:
+            ready = first(index + 1)
+        second(index, now)
+
+
+def scaled(query):
+    return query * BF16(HEAD ** -0.5)
+
+
+def pair_scores(query, keys):
+    return mm_nt(head_stack(keys, low_half(keys.shape[0])), scaled(query))
+
+
+def pair_forward(scores, values, valid):
+    probs = stack_bf16(softmax_halves(scores, valid))
+    return mm_tn(head_stack(values, low_half(values.shape[0])), probs).astype(BF16).T
+
+
+def pair_backward_scores(query, keys, values, d_out):
     low = low_half(keys.shape[0])
-    scores = mm_nt(query * BF16(HEAD ** -0.5), head_stack(keys, low))
-    probs = jnp.concatenate([part.astype(BF16) for part in softmax_halves(scores, valid)], axis=1)
-    return mm(probs, head_stack(values, low)).astype(BF16)
-
-
-def pair_backward(query, keys, values, d_out, valid):
+    return mm_nt(head_stack(keys, low), scaled(query)), mm_nt(head_stack(values, low), d_out)
+
+
+def pair_backward(scores, d_probs, query, keys, d_out, valid):
     low = low_half(keys.shape[0])
     half = keys.shape[0]
-    query = query * BF16(HEAD ** -0.5)
-    key_stack = head_stack(keys, low)
-    value_stack = head_stack(values, low)
-    parts = softmax_halves(mm_nt(query, key_stack), valid)
-    probs = jnp.concatenate([part.astype(BF16) for part in parts], axis=1)
-    d_values = head_unstack(mm_tn(probs, d_out), low).astype(BF16)
-    d_probs = mm_nt(d_out, value_stack)
+    parts = softmax_halves(scores, valid)
+    d_values = head_unstack(mm(stack_bf16(parts), d_out), low).astype(BF16)
     d_scores = []
-    for index in range(2):
-        part, d_part = parts[index], d_probs[:, index * half:(index + 1) * half]
-        d_scores.append((part * (d_part - lane_sum(part * d_part))).astype(BF16))
-    d_scores = jnp.concatenate(d_scores, axis=1)
-    d_query = (mm(d_scores, key_stack) * HEAD ** -0.5).astype(BF16)
-    d_keys = head_unstack(mm_tn(d_scores, query), low).astype(BF16)
-    return d_query, d_keys, d_values
+    for part, d_part in zip(parts, (d_probs[:half], d_probs[half:])):
+        d_scores.append(part * (d_part - row_sum(part * d_part)))
+    d_scores = stack_bf16(d_scores)
+    d_query = (mm_tn(head_stack(keys, low), d_scores) * HEAD ** -0.5).astype(BF16).T
+    return d_query, head_unstack(mm(d_scores, scaled(query)), low).astype(BF16), d_values
 
 
 def normal_cdf(u):
@@ -405,8 +430,8 @@
     place = Place()
     gatherer = Gatherer(place, macro_list(weights, vec_all_ref), send, recv)
 
-    def each_chunk(body):
-        repeat(count // chunk, lambda index: body(span(index, chunk)))
+    def each_piece(body):
+        repeat(count // chunk, lambda index: [body(at) for at in pieces_of(index * chunk, chunk)])
 
     def startup(image, wide, flat, vec_piece, raws, pieces, raw_sems, own_sems):
         first = [load(tokens_ref, image, sems.at[0]), load(context_ref, wide, sems.at[1])]
@@ -415,13 +440,12 @@
 
         def tile(layer, name, target, first_col):
             raw = raws[MATS.index(name)]
-            total = raw.shape[0]
-            flat[:total] = raw[:, layer].astype(F32)
+            flat[:raw.shape[0]] = raw[:].astype(F32)
             rows = target.shape[0]
-            many = total // rows
-            for index in range(many):
+            stride = raw.shape[0] // rows
+            for index in range(stride // blocks):
                 at = first_col + index * LANES
-                target[:, at:at + LANES] = flat[pl.ds(index, rows, stride=many)].astype(BF16)
+                target[:, at:at + LANES] = flat[pl.ds(index * blocks + layer, rows, stride=stride)].astype(BF16)
 
         def own(layer, name):
             number = layer * len(WEIGHTS) + WEIGHTS.index(name)
@@ -456,7 +480,7 @@
             pending = [prepare(layer, name) for layer, name in jobs if layer < blocks]
         for copy in first:
             copy.wait()
-        each_chunk(lambda at: hidden.at[0].__setitem__(at, image[at].astype(F32)))
+        each_piece(lambda at: hidden.at[0].__setitem__(at, image[at].astype(F32)))
         context[:] = jnp.zeros_like(context)
         for sample in range(samples):
             context[sample * pad:sample * pad + ctx_len] = wide[sample]
@@ -505,14 +529,11 @@
         inner = packed.shape[-1] - width
         gain, shift, bias = CROSS_ROWS if cross else SELF_ROWS
 
-        def scoped(w_in, w_out, w_kv, kv, in_sems):
+        def scoped(norm, w_in, w_out, w_kv, kv, in_sems):
             waits = [fetch(packed, pl.ds(0, inner), w_in, in_sems.at[0]), fetch(packed, pl.ds(inner, width), w_out, in_sems.at[1])]
             if cross:
                 fetch(weights[layer]['w_kv2'], FULL, w_kv, in_sems.at[2])()
-                fresh = mm(context[:], w_kv[:]).astype(BF16)
-                for index in range(samples):
-                    kv[index * SLOT:index * SLOT + pad] = fresh[index * pad:(index + 1) * pad]
-                    kv[index * SLOT + pad:(index + 1) * SLOT] = jnp.zeros((SLOT - pad, 2 * width), BF16)
+                kv[:] = mm(context[:], w_kv[:]).astype(BF16)
                 kv_copy = load(kv, kept[layer]['kv'], in_sems.at[2, 0])
             for wait in waits:
                 wait()
@@ -520,21 +541,25 @@
             def body(idx, qkv, mixed):
                 step = idx.index[0]
                 at_rows = span(step, chunk)
-                hat, unused = normalize(source[at_rows])
-                norm = (hat * line(rows, gain) + line(rows, shift)).astype(BF16)
-                qkv[:] = mm(norm, w_in[:]).astype(BF16)
+                for at, here in zip(pieces_of(step * chunk, chunk), pieces_of(0, chunk)):
+                    hat, unused = normalize(source[at])
+                    norm[here] = (hat * line(rows, gain) + line(rows, shift)).astype(BF16)
+                qkv[:] = mm(norm[:], w_in[:]).astype(BF16)
 
                 def sample(number):
                     at = span(number, tokens)
                     index = step * per_step + number
-                    for pair in range(heads // 2):
-                        cols, k_cols, v_cols = (slice(part * width + pair * LANES, part * width + (pair + 1) * LANES)
-                                                for part in range(COLORS))
-                        if cross:
-                            kv_at = span(index, SLOT)
-                            mixed[at, cols] = pair_forward(qkv[at, cols], kv[kv_at, cols], kv[kv_at, k_cols], ctx_len)
-                        else:
-                            mixed[at, cols] = pair_forward(qkv[at, cols], qkv[at, k_cols], qkv[at, v_cols], tokens)
+                    kv_at = span(index, pad) if cross else at
+                    k_ref, k_first, limit = (kv, 0, ctx_len) if cross else (qkv, width, tokens)
+
+                    def scores(pair):
+                        return pair_scores(qkv[at, lanes(pair)], k_ref[kv_at, lanes(pair + k_first // LANES)])
+
+                    def rest(pair, ready):
+                        values = k_ref[kv_at, lanes(pair + (k_first + width) // LANES)]
+                        mixed[at, lanes(pair)] = pair_forward(ready, values, limit)
+
+                    ahead(heads // 2, scores, rest)
                     gatherer.beside(index, plan)
 
                 repeat(per_step, sample)
@@ -547,9 +572,9 @@
                 kv_copy.wait()
 
         small = pltpu.VMEM((SUB, LANES), BF16)
-        pl.run_scoped(scoped, pltpu.VMEM((width, inner), BF16), pltpu.VMEM((width, width), BF16),
-                      pltpu.VMEM((context_ref.shape[2], 2 * width), BF16) if cross else small,
-                      pltpu.VMEM((samples * SLOT, 2 * width), BF16) if cross else small, pltpu.SemaphoreType.DMA((3, CHIPS)))
+        pl.run_scoped(scoped, pltpu.VMEM((chunk, width), BF16), pltpu.VMEM((width, inner), BF16),
+                      pltpu.VMEM((width, width), BF16), pltpu.VMEM((context_ref.shape[2], 2 * width), BF16) if cross else small,
+                      pltpu.VMEM((samples * pad, 2 * width), BF16) if cross else small, pltpu.SemaphoreType.DMA((3, CHIPS)))
 
     def feed_forward(layer, source, target, plan):
         rows = rows_ref.at[layer]
@@ -566,7 +591,7 @@
                 norm[at] = (hat * line(rows, 4) + line(rows, 5)).astype(BF16)
                 target[at] = source[at] + line(rows, SUB)
 
-            each_chunk(begin)
+            each_piece(begin)
             for wait in waits:
                 wait()
 
@@ -580,17 +605,21 @@
 
                 bias_a, bias_g = bias(0), bias(1)
 
-                def one(at):
-                    gate = mm(norm[at], w1[:, gate_cols]) + bias_g
+                def hidden_of(number):
+                    normed = norm[rows_at(number)]
+                    return mm(normed, w1[:, gate_cols]) + bias_g, mm(normed, w1[:, cols]) + bias_a
+
+                def rest(number, ready):
+                    at = rows_at(number)
+                    gate, value = ready
                     cdf, bell = normal_cdf(gate)
                     factor = gate * cdf
-                    value = mm(norm[at], w1[:, cols]) + bias_a
                     z[at] = (value * factor).astype(BF16)
                     fa[at] = factor
                     fg[at] = value * (cdf + gate * bell * BELL)
                     target[at] += mm(z[at], w2[cols])
 
-                each_chunk(one)
+                ahead(count // FF_ROWS, hidden_of, rest)
                 gatherer.beside(step, plan)
 
             block = ff_block(count)
@@ -618,7 +647,7 @@
             saves[other] = load(target, kept[following[0]][KEPT[following[1]]], sems.at[6 + other])
 
     def finish(image):
-        each_chunk(lambda at: image.__setitem__(at, hidden[phases % 2, at].astype(BF16)))
+        each_piece(lambda at: image.__setitem__(at, hidden[phases % 2, at].astype(BF16)))
         load(image, tokens_out_ref, sems.at[0]).wait()
 
     pl.run_scoped(finish, pltpu.VMEM(tokens_ref.shape, BF16))
@@ -640,10 +669,9 @@
     return [pl.BlockSpec(memory_space=pl.ANY)] * count
 
 
-def forward(tokens_x, context, raws):
+def forward(tokens_x, context, raws, blocks):
     samples, tokens, width = tokens_x.shape
     ctx_width = context.shape[2]
-    blocks = raws[0].shape[1]
     count, inner = samples * tokens, 4 * width
     pad = -(-context.shape[1] // SHARDS) * SHARDS
     steps = inner // FF_COLS
@@ -651,7 +679,7 @@
     half = jax.ShapeDtypeStruct((count, width), BF16)
     wide = jax.ShapeDtypeStruct((steps, count, FF_COLS), F32)
     kept = [plain, plain, plain, jax.ShapeDtypeStruct((count, 3 * width), BF16), half, half,
-            jax.ShapeDtypeStruct((samples * SLOT, 2 * width), BF16), half, wide, wide,
+            jax.ShapeDtypeStruct((samples * pad, 2 * width), BF16), half, wide, wide,
             jax.ShapeDtypeStruct(wide.shape, BF16), jax.ShapeDtypeStruct((SHARDS, width), F32)]
     whole_of = lambda rows, cols: jax.ShapeDtypeStruct((*CUBE[:CORE], rows // CHIPS, cols), BF16)
     weights = [whole_of(width, 4 * width), whole_of(width, 2 * width), whole_of(ctx_width, 2 * width),
@@ -714,8 +742,8 @@
     cot_ref, context_ref = refs[:2]
     saved = [dict(zip(NAMES, refs[2 + layer * len(NAMES):])) for layer in range(blocks)]
     refs = refs[2 + blocks * len(NAMES):]
-    gx_ref, grads_ref = refs[:2]
-    out_refs, refs = refs[2:3 + len(MATS)], refs[3 + len(MATS):]
+    gx_ref, grads_ref, sum_ref = refs[:3]
+    refs = refs[3:]
     grad_ref, hidden_ref, rows_ref, d_rows_ref, vec_ref, out_ref, in_sems = refs[:7]
     place = Place()
     reducer = Reducer(place, layout.macros, 1.0 / total, grads_ref, out_ref, refs[7:])
@@ -737,11 +765,8 @@
     def region(row, size):
         return grads_ref.at[:, :, :, :, pl.ds(pl.multiple_of(row, SUB), size)]
 
-    def each_chunk(body):
-        def one(index, carry):
-            body(span(index, chunk))
-            return carry
-        lax.fori_loop(0, chunks, one, 0)
+    def each_piece(body):
+        repeat(chunks, lambda index: [body(at) for at in pieces_of(index * chunk, chunk)])
 
     def ff_phase(layer, index, first):
         hidden = hidden_ref.at[index % 2]
@@ -760,9 +785,9 @@
                 norm_t[:, at] = (hat * line(rows, 4) + line(rows, 5)).astype(BF16).T
                 grad_bf[at] = grad_ref[at].astype(BF16)
                 add_line(d_rows, 8, row_sum(grad_ref[at]))
-                acc[at] = jnp.zeros((chunk, width), F32)
-
-            each_chunk(begin)
+                acc[at] = jnp.zeros((LN_ROWS, width), F32)
+
+            each_piece(begin)
 
             def copy1(step):
                 return pltpu.make_async_copy(stage1, region(base(layer) + layout.ff1 + step * 160, 160), sem1)
@@ -784,18 +809,20 @@
                 w1[:, :FF_COLS] = w1a[:]
                 w1[:, FF_COLS:] = w1g[:]
 
-                def part(number, sums):
-                    at = span(number, chunk)
-                    dz = mm_nt(grad_bf[at], w2[:]).astype(BF16).astype(F32)
-                    du_a = dz * fa[at]
-                    du_g = dz * fg[at]
-                    du[at, :FF_COLS] = du_a.astype(BF16)
-                    du[at, FF_COLS:] = du_g.astype(BF16)
+                sums = [jnp.zeros((1, FF_COLS), F32)] * 2
+
+                def d_gated(number):
+                    return mm_nt(grad_bf[rows_at(number)], w2[:]).astype(BF16).astype(F32)
+
+                def rest(number, dz):
+                    at = rows_at(number)
+                    for half, factor in enumerate((fa, fg)):
+                        part = dz * factor[at]
+                        du[at, half * FF_COLS:(half + 1) * FF_COLS] = part.astype(BF16)
+                        sums[half] += row_sum(part)
                     acc[at] += mm_nt(du[at], w1[:])
-                    return (sums[0] + row_sum(du_a), sums[1] + row_sum(du_g))
-
-                zero = jnp.zeros((1, FF_COLS), F32)
-                sums = lax.fori_loop(0, chunks, part, (zero, zero))
+
+                ahead(count // FF_ROWS, d_gated, rest)
                 for half in range(2):
                     for tile in range(2):
                         row = 9 * width // LANES + half * (inner // LANES) + 2 * step + tile
@@ -805,10 +832,14 @@
                 def _():
                     wait(step - 1)
 
-                if limit > 0:
-                    @pl.when((step >= lag) & (step < lag + limit))
+                if lag:
+                    @pl.when((step >= lag) & (lax.rem(step, 3) != 1))
                     def _():
-                        reducer.step(start + step - lag)
+                        reducer.step(start + lax.div(2 * (step - 1), 3))
+                else:
+                    @pl.when((step < limit) | (step == steps - 1))
+                    def _():
+                        reducer.step(start + jnp.minimum(step, limit))
 
                 put_tiles(stage1, mm(norm_t[:], du[:, :FF_COLS]))
                 put_tiles(stage1, mm(norm_t[:], du[:, FF_COLS:]), 80)
@@ -833,7 +864,7 @@
                 add_line(d_rows, 4, d_gain)
                 add_line(d_rows, 5, d_shift)
 
-            each_chunk(finish)
+            each_piece(finish)
             wait(steps - 1)
 
         pl.run_scoped(scoped, pltpu.VMEM((width, count), BF16), pltpu.VMEM((count, width), BF16),
@@ -882,26 +913,28 @@
                     at = span(number, tokens)
                     sample_index = step * per_step + number
                     if cross:
-                        kv_at = span(sample_index, SLOT)
-                        d_kv_at = span(sample_index, pad)
-                        d_q_at = at
+                        kv_at, d_q_at, k_ref, d_k_ref, k_first, limit = span(sample_index, pad), at, kv, d_kv, 0, ctx_len
                     else:
-                        d_q_at = span(sample_index, tokens)
-                    for pair in range(heads // 2):
-                        cols = lanes(pair)
-                        k_cols = slice(width + pair * LANES, width + (pair + 1) * LANES)
-                        v_cols = slice(2 * width + pair * LANES, 2 * width + (pair + 1) * LANES)
-                        if cross:
-                            d_query, d_keys, d_values = pair_backward(qkv[at, cols], kv[kv_at, cols], kv[kv_at, k_cols],
-                                                                      d_mix[at, cols], ctx_len)
-                            d_kv[d_kv_at, cols] = d_keys[:pad]
-                            d_kv[d_kv_at, k_cols] = d_values[:pad]
-                        else:
-                            d_query, d_keys, d_values = pair_backward(qkv[at, cols], qkv[at, k_cols], qkv[at, v_cols],
-                                                                      d_mix[at, cols], tokens)
-                            d_q[d_q_at, k_cols] = d_keys
-                            d_q[d_q_at, v_cols] = d_values
-                        d_q[d_q_at, cols] = d_query
+                        kv_at, d_q_at = at, span(sample_index, tokens)
+                        k_ref, d_k_ref, k_first, limit = qkv, d_q, width, tokens
+                    d_k_at = kv_at if cross else d_q_at
+
+                    def operands(pair):
+                        k_cols, v_cols = (lanes(pair + (k_first + more) // LANES) for more in (0, width))
+                        return qkv[at, lanes(pair)], k_ref[kv_at, k_cols], k_ref[kv_at, v_cols], d_mix[at, lanes(pair)]
+
+                    def scores(pair):
+                        return pair_backward_scores(*operands(pair))
+
+                    def rest(pair, ready):
+                        query, keys, values, d_out = operands(pair)
+                        d_query, d_keys, d_values = pair_backward(*ready, query, keys, d_out, limit)
+                        d_q[d_q_at, lanes(pair)] = d_query
+                        d_k_ref[d_k_at, lanes(pair + k_first // LANES)] = d_keys
+                        d_k_ref[d_k_at, lanes(pair + (k_first + width) // LANES)] = d_values
+
+                    ahead(heads // 2, scores, rest)
+
                     @pl.when(sample_index < in_samples)
                     def _():
                         reducer.step(start + sample_index)
@@ -909,18 +942,25 @@
                     return carry
 
                 lax.fori_loop(0, per_step, sample, 0)
-                hat, unused = normalize(hidden[at_rows])
-                norm = (hat * line(rows, gain) + line(rows, shift)).astype(BF16)
+                here_all = pieces_of(0, chunk)
+                at_all = pieces_of(step * chunk, chunk)
+                for at, here in zip(at_all, here_all):
+                    hat, unused = normalize(hidden[at])
+                    norm = (hat * line(rows, gain) + line(rows, shift)).astype(BF16)
+                    if cross:
+                        d_mix[here] = norm
+                    else:
+                        norm_t[:, at] = norm.T
                 if cross:
-                    d_wq[:] += mm_tn(norm, d_q[:])
+                    d_wq[:] += mm_tn(d_mix[:], d_q[:])
                     d_norm = mm_nt(d_q[:], w_in[:])
                 else:
-                    norm_t[:, at_rows] = norm.T
                     d_norm = mm_nt(d_q[at_rows], w_in[:])
-                d_res, d_gain, d_shift = norm_back(hidden[at_rows], d_norm, line(rows, gain))
-                grad_ref[at_rows] += d_res
-                add_line(d_rows, gain, d_gain)
-                add_line(d_rows, shift, d_shift)
+                for piece, at in enumerate(at_all):
+                    d_res, d_gain, d_shift = norm_back(hidden[at], d_norm[piece * LN_ROWS:(piece + 1) * LN_ROWS], line(rows, gain))
+                    grad_ref[at] += d_res
+                    add_line(d_rows, gain, d_gain)
+                    add_line(d_rows, shift, d_shift)
 
             block = lambda ref: pl.BlockSpec((PAIR_ROWS, ref.shape[1]), lambda step: (step, 0))
             operands = [src['q' if cross else 'qkv'], src['out2' if cross else 'out1']]
@@ -995,7 +1035,7 @@
         copy = pltpu.make_async_copy(cot_ref, cot, sem)
         copy.start()
         copy.wait()
-        each_chunk(lambda at: grad_ref.__setitem__(at, cot[at].astype(F32)))
+        each_piece(lambda at: grad_ref.__setitem__(at, cot[at].astype(F32)))
 
     pl.run_scoped(load_cot, pltpu.VMEM(cot_ref.shape, BF16), pltpu.SemaphoreType.DMA)
     for layer in range(blocks):
@@ -1009,11 +1049,11 @@
         else:
             attention_phase(layer, index, plan[index], kind == 'h1')
 
-    def finish(stage, sem, image, sem_image, vec_out, images, out_sems):
+    def finish(stage, sem, image, sem_image):
         def cast(at):
             image[at] = grad_ref[at].astype(BF16)
 
-        each_chunk(cast)
+        each_piece(cast)
         copy_image = pltpu.make_async_copy(image, gx_ref, sem_image)
         copy_image.start()
         per_device = 17 * width // SHARDS
@@ -1035,63 +1075,15 @@
         copy = pltpu.make_async_copy(stage, region(layout.vec, stage.shape[4]), sem)
         copy.start()
         copy.wait()
-
-        def convert(layer, name):
-            target = images[MATS.index(name)]
-            first = base(layer) + getattr(layout, name)
-            part = width // SHARDS
-            total = target.shape[0]
-            many = total // (context_ref.shape[1] // SHARDS if name == 'kv2' else part)
-
-            def put(tile, size, stride, row):
-                target[pl.ds(tile, size, stride=stride), layer] = out_ref[row:row + size]
-
-            if name == 'ff1':
-                for index in range(many):
-                    half, at = divmod(index, many // 2)
-                    step, tile = divmod(at, 2)
-                    put(index, part, many, first + step * 160 + half * 80 + tile * part)
-            elif name == 'ff2':
-                tiles = width // LANES
-                for block in range(total // 160):
-                    for tile in range(tiles):
-                        put(block * 160 + tile, 32, tiles, first + block * 160 + tile * 32)
-            else:
-                for index in range(many):
-                    put(index, total // many, many, first + index * (total // many))
-
-        jobs = [(blocks - 1, name) for name in MATS] + [(0, name) for name in ('ff1', 'ff2', '', 'kv2', 'q2', 'out2')]
-
-        def tail(index):
-            reducer.step(plan[-1] + index)
-            for number, (layer, name) in enumerate(jobs):
-                if name:
-                    @pl.when(index == min(number, layout.macros + STREAMS * STAGES - plan[-1] - 1))
-                    def _(layer=layer, name=name):
-                        convert(layer, name)
-
-        repeat(layout.macros + STREAMS * STAGES - plan[-1], tail)
-        convert(0, 'qkv')
-        convert(0, 'out')
-        copies = [load(source, target, out_sems.at[number])
-                  for number, (source, target) in enumerate(zip(images, out_refs))]
-        for layer in range(blocks):
-            for row in range(-(-per_device // LANES)):
-                at = layout.vec + layer * layout.vec_rows + row
-                size = min(LANES, per_device - row * LANES)
-                vec_out[layer:layer + 1, row * LANES:row * LANES + size] = line(out_ref, at)[:, :size]
-        load(vec_out, out_refs[-1], sem).wait()
-        for copy in copies:
-            copy.wait()
+        repeat(layout.macros + STREAMS * STAGES - plan[-1], lambda index: reducer.step(plan[-1] + index))
+        load(out_ref, sum_ref, sem).wait()
         copy_image.wait()
 
     pl.run_scoped(finish, pltpu.VMEM((*CUBE, blocks * layout.vec_rows + layout.pad, LANES), F32),
-                  pltpu.SemaphoreType.DMA, pltpu.VMEM(cot_ref.shape, BF16), pltpu.SemaphoreType.DMA,
-                  pltpu.VMEM(out_refs[-1].shape, F32), [pltpu.VMEM(ref.shape, F32) for ref in out_refs[:-1]],
-                  pltpu.SemaphoreType.DMA((len(MATS),)))
-
-
-def backward(cot, context, saved, tokens, ctx_len, total, out_shapes):
+                  pltpu.SemaphoreType.DMA, pltpu.VMEM(cot_ref.shape, BF16), pltpu.SemaphoreType.DMA)
+
+
+def backward(cot, context, saved, tokens, ctx_len, total):
     count, width = cot.shape
     blocks = len(saved)
     layout = Layout(width, context.shape[1], blocks)
@@ -1102,20 +1094,62 @@
     shape = saved[0]['rows'].shape
     outs = pl.pallas_call(
         functools.partial(backward_kernel, cfg),
-        in_specs=any_specs(len(operands)), out_specs=any_specs(3 + len(MATS)),
+        in_specs=any_specs(len(operands)), out_specs=any_specs(3),
         out_shape=[jax.ShapeDtypeStruct((count, width), BF16),
-                   jax.ShapeDtypeStruct((*CUBE, layout.rows, LANES), F32)]
-        + [jax.ShapeDtypeStruct(shape, F32) for shape in out_shapes],
+                   jax.ShapeDtypeStruct((*CUBE, layout.rows, LANES), F32),
+                   jax.ShapeDtypeStruct((layout.rows, LANES), F32)],
         scratch_shapes=[pltpu.VMEM((count, width), F32), pltpu.VMEM((2, count, width), F32),
                         pltpu.VMEM((blocks,) + shape, F32), pltpu.VMEM((blocks,) + shape, F32),
                         pltpu.VMEM((blocks, 96, LANES), F32), pltpu.VMEM((layout.rows, LANES), F32),
                         pltpu.SemaphoreType.DMA((2 + blocks,))] + Reducer.scratch(),
         name='backward', **settings(0),
     )(*operands)
-    return outs[0], outs[2:]
-
-
-PLAN = [(0, 4, 6), (6, 4, 0), (10, 6, 1), (17, 0, SUB), (25, 5, 0), (30, 6, 1), 37]
+    return outs[0], outs[2], layout
+
+
+PLAN = [(0, 2, 0), (6, 4, 0), (10, 6, 1), (17, 0, SUB), (26, 4, 0), (30, 6, 1), 37]
+
+
+def deliver_kernel(cfg, sum_ref, gx_ref, tokens_ref, *out_refs):
+    width, ctx_width, blocks, layout = cfg
+    out_refs[-2][:] = gx_ref[:]
+    out_refs[-1][:] = tokens_ref[:]
+    tiles = width // LANES
+    for layer in range(blocks):
+        for name, target in zip(MATS, out_refs):
+            first = (blocks - 1 - layer) * layout.block + getattr(layout, name)
+            total = target.shape[0] // blocks
+            part = {'kv2': ctx_width, 'ff2': 4 * width}.get(name, width) // SHARDS
+            many = total // part
+
+            def put(tile, size, stride, row):
+                target[pl.ds(tile * blocks + layer, size, stride=stride * blocks)] = sum_ref[row:row + size]
+
+            for index in range(many):
+                if name == 'ff1':
+                    half, at = divmod(index, many // 2)
+                    step, tile = divmod(at, 2)
+                    put(index, part, many, first + step * 160 + half * 80 + tile * part)
+                elif name == 'ff2':
+                    for block in range(part // 32):
+                        put(block * 160 + index, 32, tiles, first + block * 160 + index * 32)
+                else:
+                    put(index, part, many, first + index * part)
+        per_device = 17 * width // SHARDS
+        for row in range(-(-per_device // LANES)):
+            size = min(LANES, per_device - row * LANES)
+            out_refs[len(MATS)][layer:layer + 1, row * LANES:row * LANES + size] = line(
+                sum_ref, layout.vec + layer * layout.vec_rows + row)[:, :size]
+
+
+def deliver(sums, grad_x, tokens, shapes, cfg):
+    in_vmem = pl.BlockSpec(memory_space=pltpu.VMEM)
+    out_shape = [jax.ShapeDtypeStruct(shape, F32) for shape in shapes] + [
+        jax.ShapeDtypeStruct(grad_x.shape, BF16), jax.ShapeDtypeStruct(tokens.shape, BF16)]
+    return pl.pallas_call(
+        functools.partial(deliver_kernel, cfg), in_specs=[in_vmem] * 3, out_specs=[in_vmem] * len(out_shape),
+        out_shape=out_shape, compiler_params=pltpu.CompilerParams(vmem_limit_bytes=VMEM_BYTES), name='deliver',
+    )(sums, grad_x, tokens)
 
 
 def solution(mesh):
@@ -1127,11 +1161,14 @@
         spare = -shards[-1].shape[1] % LANES
         padded = shards[:-1] + (jnp.pad(shards[-1], ((0, 0), (0, spare))),)
         raws = [shard.reshape(blocks, -1, LANES).swapaxes(0, 1) for shard in padded]
-        saved, ctx_rows, out_tokens = forward(tokens_x, context, raws)
-        out_shapes = [raw.shape for raw in raws[:-1]] + [shards[-1].shape]
-        grad_x, grads = backward(cot_out.reshape(samples * tokens, width), ctx_rows, saved, tokens, context.shape[1],
-                                 samples * n_dev, out_shapes)
-        grads = [grad.swapaxes(0, 1).reshape(blocks, -1) for grad in grads[:-1]] + [grads[-1]]
+        raws = [raw.reshape(-1, LANES) for raw in raws[:-1]] + raws[-1:]
+        saved, ctx_rows, out_tokens = forward(tokens_x, context, raws, blocks)
+        grad_x, sums, layout = backward(cot_out.reshape(samples * tokens, width), ctx_rows, saved, tokens,
+                                        context.shape[1], samples * n_dev)
+        shapes = [raw.shape for raw in raws[:-1]] + [shards[-1].shape]
+        *grads, vec, grad_x, out_tokens = deliver(sums, grad_x, out_tokens, shapes,
+                                                  (width, context.shape[2], blocks, layout))
+        grads = [grad.reshape(-1, blocks, LANES).swapaxes(0, 1).reshape(blocks, -1) for grad in grads] + [vec]
         return (out_tokens.reshape(tokens_x.shape), grad_x.reshape(tokens_x.shape), *grads)
 
     param_spec = P(None, AXIS)

time: 651 us -> 591 us (0.908)
  Pallas kernels: 630 us -> 581 us
  local copies, waits for them, and re-layouts: 12.3 us -> 1.27 us
    pallas_call x1, Pallas kernels: 375 us -> 338 us  [backward(): pl.pallas_call(functools.partial(backward_kernel, cfg), in_specs=any_spec...]
    pallas_call x1, Pallas kernels: 255 us -> 235 us  [forward(): pl.pallas_call(functools.partial(forward_kernel, (tokens, width, blocks,...]
    unnamed x28 -> x0, local copies, waits for them, and re-layouts: 11 us -> none
    pallas_call x0 -> x1, Pallas kernels: none -> 7.8 us  [deliver(): pl.pallas_call(functools.partial(deliver_kernel, cfg), in_specs=[in_vmem]...]
where the time goes in v5:
time: 591 us; the launch traced here: 583 us
  Pallas kernels  581 us (98%)
    pallas_call x1, Pallas kernels, backward(): pl.pallas_call(functools.partial(backward_kernel, cfg), in_specs=any_spec...  338 us
    pallas_call x1, Pallas kernels, forward(): pl.pallas_call(functools.partial(forward_kernel, (tokens, width, blocks,...  235 us

profile of v5, /device:TPU:0, one launch (start us, length us, event | category | flops | bytes accessed | tf_op | source)
XLA Modules:
  0.0 583.4 jit_solution(7015022165025694608)
XLA Ops:
  0.6 1.3 pad_bitcast_fusion.refs_9_
  1.9 235.0 %forward.1 = (f32[1536,640]{1,0:T(8,128)}, f32[1536,640]{1,0:T(8,128)}, f32[1536,640]{1,0:T(8,128)}, bf16[1536,1920]{1,0:T(8,128)(2,1)}, bf16[1536,640]{1,0:T(8,...) custom-call(bf16[1536,640]{1,0:T(8,128)(2,1)} %bitcast.88, ...), custom_call_target="tpu_custom_call" | custom-call | flops 99999997952 | bytes 100000000 | tf_op jit(solution)/shard_map/forward/pallas_call | solution.py:690
  236.9 338.2 %backward.1 = (bf16[1536,640]{1,0:T(8,128)(2,1)}, f32[2,2,2,2,9840,128]{5,4,3,2,1,0:T(8,128)}, f32[9840,128]{1,0:T(8,128)}) custom-call(bf16[1536,640]{1,0:T(8,128)(2,1)} %bitcast.89, bf16[480,2048]{1,0:T(8,128)(2,1)} %get-tuple-element.58.refs_1_, f32[1536,640]{1,0:T(8,128)} %get-tuple-element.59.refs_2_, f32[1536,640]{1,0:T(8,128)} %get-tuple-element.60.refs_3_, ...), custom_call_target="tpu_custom_call" | custom-call | flops 99999997952 | bytes 100000000 | tf_op jit(solution)/shard_map/backward/pallas_call | solution.py:1095
  575.1 7.8 %deliver.1 = (f32[1200,128]{1,0:T(8,128)}, f32[400,128]{1,0:T(8,128)}, f32[400,128]{1,0:T(8,128)}, f32[2560,128]{1,0:T(8,128)}, f32[400,128]{1,0:T(8,128)}, /*in...) custom-call(f32[9840,128]{1,0:T(8,128)} %get-tuple-element.93.sum_re, ...), custom_call_target="tpu_custom_call" | custom-call | tf_op jit(solution)/shard_map/deliver/pallas_call | solution.py:1149

commit v6 on v5

--- a/solution.py
+++ b/solution.py
@@ -27,11 +27,14 @@
 LN_ROWS = 128
 PAIR_ROWS = 512
 FF_ROWS = 256
+FF_PART = 160
+FF_SUB = 32
 FF_COLS = 256
 
-TAIL_P = 0.265
-TAIL = (0.10574158579953814, 0.10524628753634038, 0.10270369607548423, 0.0603023517537824, 0.13797880111692826,
-        -0.11640058407079061, 0.2178489286936914, -0.1442454807654402, 0.03082441619112092)
+TAIL_C = 3.3
+TAIL = (0.398796301085, 1.32638029784, 3.66563581228, 14.7229083576, -17.4165998636, 251.026512347, -660.864693498,
+        511.950585826)
+HALF_LOG2E = 0.5 * math.log2(math.e)
 
 
 def mm(lhs, rhs):
@@ -135,13 +138,17 @@
     return slice(number * FF_ROWS, (number + 1) * FF_ROWS)
 
 
-def ahead(count, first, second):
+def ahead(count, first, second, third=None):
     ready = first(0)
     for index in range(count):
         now = ready
         if index + 1 < count:
             ready = first(index + 1)
         second(index, now)
+        if third and index:
+            third(index - 1)
+    if third:
+        third(count - 1)
 
 
 def scaled(query):
@@ -176,12 +183,12 @@
 
 
 def normal_cdf(u):
-    t = 1.0 / (1.0 + TAIL_P * jnp.abs(u))
+    inverse = 1.0 / (TAIL_C + jnp.abs(u))
     poly = TAIL[-1]
     for coef in TAIL[-2::-1]:
-        poly = poly * t + coef
-    bell = jnp.exp(u * u * -0.5)
-    tail = bell * (t * poly)
+        poly = poly * inverse + coef
+    bell = jnp.exp2(u * u * -HALF_LOG2E)
+    tail = bell * (inverse * poly)
     return jnp.where(u >= 0, 1.0 - tail, tail), bell
 
 
@@ -309,6 +316,15 @@
         for stage in range(STAGES):
             when_live(tau - stage, functools.partial(give, stage))
 
+    def beside(self, index, counts, start):
+        number, first = 0, start
+        for site, digit in enumerate(map(int, counts)):
+            if digit:
+                number += jnp.where(index == site, digit, 0)
+                first += jnp.where(index > site, digit, 0)
+        if start < start + sum(map(int, counts)):
+            lax.fori_loop(0, number, lambda step, carry: (self.step(first + step), carry)[1], 0)
+
 
 class Piece(NamedTuple):
     ref: Any
@@ -321,14 +337,17 @@
 
 class Gatherer:
     def __init__(self, place, macros, send, recv):
-        self.place, self.macros, self.send, self.recv = place, [], send, recv
+        self.place, self.send, self.recv = place, send, recv
+        self.jobs = {}
         number = 0
-        for macro in macros:
+        for index, macro in enumerate(macros):
+            first, gap = (0, 1) if index < 2 else (index - 1, 2)
             pieces = []
-            for ref, color, first, rows, cols in macro:
-                pieces.append(Piece(ref, first, rows, cols, color, number))
+            for ref, color, row, rows, cols in macro:
+                pieces.append(Piece(ref, row, rows, cols, color, number))
                 number += 1
-            self.macros.append(pieces)
+            for stage in range(STAGES + 1):
+                self.jobs.setdefault(first + gap * stage, []).append((stage, pieces))
 
     def copy(self, piece, stage):
         order = ORDERS[piece.color]
@@ -340,21 +359,22 @@
             recv_sem=self.recv.at[piece.number, stage], device_id=self.place.devices[axis], device_id_type=MESH)
 
     def step(self, t):
-        for macro, pieces in enumerate(self.macros):
-            stage = t - macro
-            if stage in range(1, STAGES + 1):
+        for stage, pieces in self.jobs[t]:
+            if stage:
                 for piece in pieces:
                     copy = self.copy(piece, stage - 1)
                     copy.wait_send()
                     copy.wait_recv()
-            if stage in range(STAGES):
+            if stage < STAGES:
                 for piece in pieces:
                     self.copy(piece, stage).start()
 
-    def beside(self, index, plan):
-        first, count = plan
+    def beside(self, index, part, sites, offset=0):
+        first, count = sum(FORWARD_STEPS[:part]), FORWARD_STEPS[part]
         for number in range(count):
-            @pl.when(index == 2 * number + 1)
+            site = (number + 1) * sites // count - 1 if count <= sites else number * sites // count
+
+            @pl.when(index == offset + site)
             def _(number=number):
                 self.step(first + number)
 
@@ -364,7 +384,7 @@
     return [slice(first, last) for first, last in zip(edges[:-1], edges[1:])]
 
 
-FORWARD_PLAN = [(5, 3), (8, 3), (11, 5), (SHARDS, 2), (0, 0), (0, 0)]
+FORWARD_STEPS = (7, 7, 4, 3, 3, 4, 3, 2, 0)
 MATS = ('qkv', 'out', 'q2', 'kv2', 'out2', 'ff1', 'ff2')
 WEIGHTS = ('w_a', 'w_b', 'w_kv2', 'w_ff1', 'w_ff2')
 KEPT = ('h', 'h1', 'h2', 'qkv', 'out1', 'q', 'kv', 'out2', 'fa', 'fg', 'z', 'rows')
@@ -376,10 +396,10 @@
     return copy
 
 
-def fetch(source, cols, target, sems):
+def fetch(source, cols, target, sems, into=FULL):
     def copy(shard):
         index = [lax.rem(lax.div(shard, weight), 2) for weight in CHIP_WEIGHT]
-        return pltpu.make_async_copy(source.at[(*index, FULL, cols)], target.at[span(shard, source.shape[CORE])],
+        return pltpu.make_async_copy(source.at[(*index, FULL, cols)], target.at[span(shard, source.shape[CORE]), into],
                                      sems.at[shard])
 
     repeat(CHIPS, lambda shard: copy(shard).start())
@@ -390,22 +410,26 @@
     macros = []
     for block in weights:
         high = {name: block[name].shape[CORE] // 2 for name in WEIGHTS}
-        cols = {name: thirds(block[name].shape[-1] // LANES) for name in ('w_a', 'w_b', 'w_kv2')}
-        wide = block['w_ff1'].shape[-1] // 2
-
-        def add(name, first, rows, cols):
-            macros.append([(block[name], color, first, rows, part) for color, part in enumerate(cols)])
-
-        add('w_a', 0, high['w_a'], cols['w_a'])
+        def add(name, row, rows, first, cols):
+            parts = thirds(cols // LANES)
+            macros.append([(block[name], color, row, rows, pl.ds(first + part.start, part.stop - part.start))
+                           for color, part in enumerate(parts[len(macros) % COLORS:] + parts[:len(macros) % COLORS])])
+
+        wide = block['w_a'].shape[-1] // 2
         for part in range(2):
-            add('w_kv2', part * high['w_kv2'] // 2, high['w_kv2'] // 2, cols['w_kv2'])
-        add('w_b', 0, high['w_b'], cols['w_b'])
+            add('w_a', 0, high['w_a'], part * wide, wide)
+        quarter = high['w_kv2'] // 4
+        for part in range(4):
+            add('w_kv2', part * quarter, quarter, 0, wide)
+        add('w_b', 0, high['w_b'], 0, wide)
+        tenth = high['w_ff2'] // 20
         for part in range(2):
-            add('w_ff1', 0, high['w_ff1'],
-                [pl.ds(part * wide + third.start, third.stop - third.start) for third in thirds(wide // LANES)])
-        tenth = high['w_ff2'] // 10
-        macros.append([(block['w_ff2'], color, first * tenth, rows * tenth, FULL)
-                       for color, (first, rows) in enumerate(((0, 3), (3, 4), (7, 3)))])
+            macros.append([(block['w_ff2'], color, (part * 10 + row) * tenth, rows * tenth, FULL)
+                           for color, row, rows in zip(range(COLORS), (0, 3, 7), (3, 4, 3))])
+        inner = block['w_ff1'].shape[-1] // 2
+        for part in range(2):
+            for half in range(2):
+                add('w_ff1', 0, high['w_ff1'], half * inner + part * inner // 2, inner // 2)
     macros[0].append((vec, 0, 0, vec.shape[CORE] // 2, FULL))
     return macros
 
@@ -471,8 +495,8 @@
             vec_piece[layer * SUB:layer * SUB + per_vec] = flat[:per_vec].astype(BF16)
         pending = [prepare(0, 'w_a'), load(vec_piece, place.own(vec_all_ref), sems.at[2])]
         place.entry_barrier()
-        later = [[(0, 'w_kv2')], [(0, 'w_b'), (0, 'w_ff1'), (0, 'w_ff2')], [(1, 'w_a'), (1, 'w_kv2'), (1, 'w_b')],
-                 [(1, 'w_ff1'), (1, 'w_ff2')]]
+        later = [[(0, 'w_kv2')], [(0, 'w_b'), (0, 'w_ff2')], [(0, 'w_ff1')], [(1, name) for name in WEIGHTS[:CORE]],
+                 [(1, name) for name in WEIGHTS[CORE:]]]
         for t, jobs in enumerate(later):
             for copy in pending:
                 copy.wait()
@@ -486,7 +510,8 @@
             context[sample * pad:sample * pad + ctx_len] = wide[sample]
         for copy in pending:
             copy.wait()
-        gatherer.step(len(later))
+        for t in range(len(later), FORWARD_STEPS[0]):
+            gatherer.step(t)
 
     def raw_shape(index):
         return pltpu.VMEM(raw_refs[index].shape, BF16)
@@ -523,7 +548,7 @@
     pl.run_scoped(unpack, pltpu.VMEM(vec_all_ref.shape, BF16), pltpu.SemaphoreType.DMA)
     rows_copies = [load(rows_ref.at[layer], kept[layer]['rows'], sems.at[4 + layer]) for layer in range(blocks)]
 
-    def attention(layer, source, target, cross, plan):
+    def attention(layer, source, target, cross, part):
         rows = rows_ref.at[layer]
         packed = weights[layer]['w_b' if cross else 'w_a']
         inner = packed.shape[-1] - width
@@ -560,7 +585,7 @@
                         mixed[at, lanes(pair)] = pair_forward(ready, values, limit)
 
                     ahead(heads // 2, scores, rest)
-                    gatherer.beside(index, plan)
+                    gatherer.beside(index, part, samples)
 
                 repeat(per_step, sample)
                 target[at_rows] = source[at_rows] + mm(mixed[:], w_out[:]) + line(rows, bias)
@@ -576,15 +601,19 @@
                       pltpu.VMEM((width, width), BF16), pltpu.VMEM((context_ref.shape[2], 2 * width), BF16) if cross else small,
                       pltpu.VMEM((samples * pad, 2 * width), BF16) if cross else small, pltpu.SemaphoreType.DMA((3, CHIPS)))
 
-    def feed_forward(layer, source, target, plan):
+    def feed_forward(layer, source, target, part):
         rows = rows_ref.at[layer]
         vec = vec_ref.at[layer]
         inner = weights[layer]['w_ff1'].shape[-1] // 2
         steps = inner // FF_COLS
-        part = FF_COLS // LANES
+        wide = FF_COLS // LANES
 
         def scoped(norm, w1, w2, w_sems):
-            waits = [fetch(weights[layer]['w_ff1'], FULL, w1, w_sems.at[0]), fetch(weights[layer]['w_ff2'], FULL, w2, w_sems.at[1])]
+            def fetch_half(part):
+                both = [pl.ds(half * inner + part * inner // 2, inner // 2) for half in range(2)]
+                return [fetch(weights[layer]['w_ff1'], cols, w1, w_sems.at[half], cols) for half, cols in enumerate(both)]
+
+            waits = fetch_half(0) + [fetch(weights[layer]['w_ff2'], FULL, w2, w_sems.at[2])]
 
             def begin(at):
                 hat, unused = normalize(source[at])
@@ -599,9 +628,14 @@
                 step = idx.index[0]
                 cols, gate_cols = span(step, FF_COLS), span(step + steps, FF_COLS)
 
+                @pl.when(step == steps // 2)
+                def _():
+                    for wait in fetch_half(1):
+                        wait()
+
                 def bias(half):
-                    first = 9 * tiles + (half * steps + step) * part
-                    return jnp.concatenate([vec[pl.ds(first + index, 1)] for index in range(part)], axis=1)
+                    first = 9 * tiles + (half * steps + step) * wide
+                    return jnp.concatenate([vec[pl.ds(first + index, 1)] for index in range(wide)], axis=1)
 
                 bias_a, bias_g = bias(0), bias(1)
 
@@ -617,19 +651,22 @@
                     z[at] = (value * factor).astype(BF16)
                     fa[at] = factor
                     fg[at] = value * (cdf + gate * bell * BELL)
-                    target[at] += mm(z[at], w2[cols])
-
-                ahead(count // FF_ROWS, hidden_of, rest)
-                gatherer.beside(step, plan)
+
+                def project(number):
+                    target[rows_at(number)] += mm(z[rows_at(number)], w2[cols])
+
+                ahead(count // FF_ROWS, hidden_of, rest, project)
+                for half in range(2):
+                    gatherer.beside(step, part + half, steps // 2, half * steps // 2)
 
             block = ff_block(count)
             pipeline(body, grid=(steps,), out_specs=[block, block, block])(
                 kept[layer]['fa'], kept[layer]['fg'], kept[layer]['z'])
 
         pl.run_scoped(scoped, pltpu.VMEM((count, width), BF16), pltpu.VMEM((width, 2 * inner), BF16),
-                      pltpu.VMEM((inner, width), BF16), pltpu.SemaphoreType.DMA((2, CHIPS)))
-
-    phases = len(FORWARD_PLAN)
+                      pltpu.VMEM((inner, width), BF16), pltpu.SemaphoreType.DMA((3, CHIPS)))
+
+    phases = 3 * blocks
     saves = [load(hidden.at[0], kept[0]['h'], sems.at[6]), None]
     for phase in range(phases):
         layer, kind = divmod(phase, 3)
@@ -638,9 +675,9 @@
         if saves[other] is not None:
             saves[other].wait()
         if kind < 2:
-            attention(layer, source, target, kind == 1, FORWARD_PLAN[phase])
+            attention(layer, source, target, kind == 1, 1 + 4 * layer + kind)
         else:
-            feed_forward(layer, source, target, FORWARD_PLAN[phase])
+            feed_forward(layer, source, target, 1 + 4 * layer + kind)
         following = divmod(phase + 1, 3)
         saves[other] = None
         if phase + 1 < phases:
@@ -686,7 +723,7 @@
                whole_of(width, 2 * inner), whole_of(inner, width)]
     extra = [whole_of(SHARDS * blocks * SUB, LANES), jax.ShapeDtypeStruct((samples * pad, ctx_width), BF16), half]
     shapes = kept * blocks + weights * blocks + extra
-    pieces = 1 + 3 * 7 * blocks
+    pieces = 1 + COLORS * 13 * blocks
     outs = pl.pallas_call(
         functools.partial(forward_kernel, (tokens, width, blocks, raws[-1].shape[0])),
         in_specs=any_specs(2 + len(raws)), out_specs=any_specs(len(shapes)), out_shape=shapes,
@@ -719,12 +756,12 @@
     def __init__(self, width, ctx_width, blocks):
         unit = width // SHARDS * (width // LANES)
         self.ff1, self.ff2 = 0, 8 * unit
-        self.kv2 = 12 * unit
-        self.q2 = self.kv2 + ctx_width // SHARDS * (2 * width // LANES)
+        self.q2 = 12 * unit
         self.out2 = self.q2 + unit
-        self.qkv = self.out2 + unit
-        self.out = self.qkv + 3 * unit
-        self.block = self.out + unit
+        self.kv2 = self.out2 + unit
+        self.out = self.kv2 + ctx_width // SHARDS * (2 * width // LANES)
+        self.qkv = self.out + unit
+        self.block = self.qkv + 3 * unit
         self.vec = blocks * self.block
         self.vec_rows = -(-17 * width // SHARDS // LANES // SUB) * SUB
         used = self.vec + blocks * self.vec_rows
@@ -777,7 +814,7 @@
         w1_all, w2_all = src['w_ff1'], src['w_ff2']
         inner = w2_all.shape[0]
         steps = inner // FF_COLS
-        start, lag, limit = first
+        start, counts = first
 
         def scoped(norm_t, grad_bf, du, w1, acc, stage1, stage2, sem1, sem2):
             def begin(at):
@@ -790,14 +827,14 @@
             each_piece(begin)
 
             def copy1(step):
-                return pltpu.make_async_copy(stage1, region(base(layer) + layout.ff1 + step * 160, 160), sem1)
+                return pltpu.make_async_copy(stage1, region(base(layer) + layout.ff1 + step * FF_PART, FF_PART), sem1)
 
             def copy2(step, part):
                 block = step * 8 + part
                 shard = lax.div(block, 5)
-                row = pl.multiple_of(base(layer) + layout.ff2 + lax.rem(block, 5) * 160, SUB)
+                row = pl.multiple_of(base(layer) + layout.ff2 + lax.rem(block, 5) * FF_PART, SUB)
                 bits = bits_of(shard)
-                return pltpu.make_async_copy(stage2.at[part], grads_ref.at[(*bits, pl.ds(row, 160))], sem2.at[part])
+                return pltpu.make_async_copy(stage2.at[part], grads_ref.at[(*bits, pl.ds(row, FF_PART))], sem2.at[part])
 
             def wait(step):
                 copy1(step).wait()
@@ -820,9 +857,11 @@
                         part = dz * factor[at]
                         du[at, half * FF_COLS:(half + 1) * FF_COLS] = part.astype(BF16)
                         sums[half] += row_sum(part)
-                    acc[at] += mm_nt(du[at], w1[:])
-
-                ahead(count // FF_ROWS, d_gated, rest)
+
+                def project(number):
+                    acc[rows_at(number)] += mm_nt(du[rows_at(number)], w1[:])
+
+                ahead(count // FF_ROWS, d_gated, rest, project)
                 for half in range(2):
                     for tile in range(2):
                         row = 9 * width // LANES + half * (inner // LANES) + 2 * step + tile
@@ -832,20 +871,12 @@
                 def _():
                     wait(step - 1)
 
-                if lag:
-                    @pl.when((step >= lag) & (lax.rem(step, 3) != 1))
-                    def _():
-                        reducer.step(start + lax.div(2 * (step - 1), 3))
-                else:
-                    @pl.when((step < limit) | (step == steps - 1))
-                    def _():
-                        reducer.step(start + jnp.minimum(step, limit))
-
+                reducer.beside(step, counts, start)
                 put_tiles(stage1, mm(norm_t[:], du[:, :FF_COLS]))
                 put_tiles(stage1, mm(norm_t[:], du[:, FF_COLS:]), 80)
                 d_w2 = mm_tn(z[:], grad_bf[:])
                 for tile in range(width // LANES):
-                    stage2[:, tile * 32:(tile + 1) * 32] = d_w2[:, lanes(tile)].reshape(8, 32, LANES)
+                    stage2[:, tile * FF_SUB:(tile + 1) * FF_SUB] = d_w2[:, lanes(tile)].reshape(8, FF_SUB, LANES)
                 copy1(step).start()
                 for number in range(8):
                     copy2(step, number).start()
@@ -869,8 +900,8 @@
 
         pl.run_scoped(scoped, pltpu.VMEM((width, count), BF16), pltpu.VMEM((count, width), BF16),
                       pltpu.VMEM((count, 2 * FF_COLS), BF16), pltpu.VMEM((width, 2 * FF_COLS), BF16),
-                      pltpu.VMEM((count, width), F32), pltpu.VMEM((*CUBE, 160, LANES), F32),
-                      pltpu.VMEM((8, 160, LANES), F32), pltpu.SemaphoreType.DMA, pltpu.SemaphoreType.DMA((8,)))
+                      pltpu.VMEM((count, width), F32), pltpu.VMEM((*CUBE, FF_PART, LANES), F32),
+                      pltpu.VMEM((8, FF_PART, LANES), F32), pltpu.SemaphoreType.DMA, pltpu.SemaphoreType.DMA((8,)))
 
     def attention_phase(layer, index, first, cross):
         hidden = hidden_ref.at[index % 2]
@@ -881,7 +912,7 @@
         inner = packed.shape[1] - width
         steps = count // PAIR_ROWS
         per_step = PAIR_ROWS // tokens
-        start, in_samples, in_tails = first
+        start, counts = first
         gain, shift, bias = CROSS_ROWS if cross else SELF_ROWS
         samples = count // tokens
         pad = context_ref.shape[0] // samples
@@ -935,10 +966,7 @@
 
                     ahead(heads // 2, scores, rest)
 
-                    @pl.when(sample_index < in_samples)
-                    def _():
-                        reducer.step(start + sample_index)
-
+                    reducer.beside(sample_index, counts[:samples], start)
                     return carry
 
                 lax.fori_loop(0, per_step, sample, 0)
@@ -993,18 +1021,17 @@
                 def _():
                     copy_tail(step - 1).wait()
 
+                @pl.when(step == 1)
+                def _():
+                    copy_out.wait()
+
                 put_tiles(stage, result)
                 copy_tail(step).start()
-                if in_tails:
-                    @pl.when(step < in_tails)
-                    def _():
-                        reducer.step(start + in_samples + step)
-
+                reducer.beside(step, counts[samples:], start + sum(map(int, counts[:samples])))
                 return carry
 
             lax.fori_loop(0, tails, tail, 0)
             copy_tail(tails - 1).wait()
-            copy_out.wait()
 
         small = pltpu.VMEM((SUB, LANES), BF16)
         w_scratch = [pltpu.VMEM((width, inner), BF16), pltpu.VMEM((width, width), BF16), pltpu.SemaphoreType.DMA((2,))]
@@ -1087,7 +1114,8 @@
     count, width = cot.shape
     blocks = len(saved)
     layout = Layout(width, context.shape[1], blocks)
-    cfg = (tokens, ctx_len, width, blocks, layout, total, PLAN)
+    starts = [sum(map(int, ''.join(PLAN[:phase]))) for phase in range(len(PLAN) + 1)]
+    cfg = (tokens, ctx_len, width, blocks, layout, total, [*zip(starts, PLAN), starts[-1]])
     operands = [cot, context]
     for block in saved:
         operands += [block[name] for name in NAMES]
@@ -1107,7 +1135,7 @@
     return outs[0], outs[2], layout
 
 
-PLAN = [(0, 2, 0), (6, 4, 0), (10, 6, 1), (17, 0, SUB), (26, 4, 0), (30, 6, 1), 37]
+PLAN = ('0011002011', '11101000100', '11100101001', '1021011012', '11002001000', '21010111100')
 
 
 def deliver_kernel(cfg, sum_ref, gx_ref, tokens_ref, *out_refs):
@@ -1129,10 +1157,10 @@
                 if name == 'ff1':
                     half, at = divmod(index, many // 2)
                     step, tile = divmod(at, 2)
-                    put(index, part, many, first + step * 160 + half * 80 + tile * part)
+                    put(index, part, many, first + step * FF_PART + half * 80 + tile * part)
                 elif name == 'ff2':
-                    for block in range(part // 32):
-                        put(block * 160 + index, 32, tiles, first + block * 160 + index * 32)
+                    for block in range(part // FF_SUB):
+                        put(block * FF_PART + index, FF_SUB, tiles, first + block * FF_PART + index * FF_SUB)
                 else:
                     put(index, part, many, first + index * part)
         per_device = 17 * width // SHARDS

time: 591 us -> 560 us (0.948)
  Pallas kernels: 581 us -> 549 us
    pallas_call x1, Pallas kernels: 338 us -> 318 us  [backward(): pl.pallas_call(functools.partial(backward_kernel, cfg), in_specs=any_spec...]
    pallas_call x1, Pallas kernels: 235 us -> 223 us  [forward(): pl.pallas_call(functools.partial(forward_kernel, (tokens, width, blocks,...]
where the time goes in v6:
time: 560 us; the launch traced here: 551 us
  Pallas kernels  549 us (98%)
    pallas_call x1, Pallas kernels, backward(): pl.pallas_call(functools.partial(backward_kernel, cfg), in_specs=any_spec...  318 us
    pallas_call x1, Pallas kernels, forward(): pl.pallas_call(functools.partial(forward_kernel, (tokens, width, blocks,...  223 us

profile of v6, /device:TPU:0, one launch (start us, length us, event | category | flops | bytes accessed | tf_op | source)
XLA Modules:
  0.0 551.5 jit_solution(13544677310258039184)
XLA Ops:
  0.6 1.3 pad_bitcast_fusion.refs_9_
  1.9 223.0 %forward.1 = (f32[1536,640]{1,0:T(8,128)}, f32[1536,640]{1,0:T(8,128)}, f32[1536,640]{1,0:T(8,128)}, bf16[1536,1920]{1,0:T(8,128)(2,1)}, bf16[1536,640]{1,0:T(8,...) custom-call(bf16[1536,640]{1,0:T(8,128)(2,1)} %bitcast.88, ...), custom_call_target="tpu_custom_call" | custom-call | flops 99999997952 | bytes 100000000 | tf_op jit(solution)/shard_map/forward/pallas_call | solution.py:727
  225.0 318.3 %backward.1 = (bf16[1536,640]{1,0:T(8,128)(2,1)}, f32[2,2,2,2,9840,128]{5,4,3,2,1,0:T(8,128)}, f32[9840,128]{1,0:T(8,128)}) custom-call(bf16[1536,640]{1,0:T(8,128)(2,1)} %bitcast.89, bf16[480,2048]{1,0:T(8,128)(2,1)} %get-tuple-element.58.refs_1_, f32[1536,640]{1,0:T(8,128)} %get-tuple-element.59.refs_2_, f32[1536,640]{1,0:T(8,128)} %get-tuple-element.60.refs_3_, ...), custom_call_target="tpu_custom_call" | custom-call | flops 99999997952 | bytes 100000000 | tf_op jit(solution)/shard_map/backward/pallas_call | solution.py:1123
  543.2 7.8 %deliver.1 = (f32[1200,128]{1,0:T(8,128)}, f32[400,128]{1,0:T(8,128)}, f32[400,128]{1,0:T(8,128)}, f32[2560,128]{1,0:T(8,128)}, f32[400,128]{1,0:T(8,128)}, /*in...) custom-call(f32[9840,128]{1,0:T(8,128)} %get-tuple-element.93.sum_re, ...), custom_call_target="tpu_custom_call" | custom-call | tf_op jit(solution)/shard_map/deliver/pallas_call | solution.py:1177

commit v7 on v6

--- a/solution.py
+++ b/solution.py
@@ -379,12 +379,7 @@
                 self.step(first + number)
 
 
-def thirds(tiles):
-    edges = [round(tiles * part / 3) * LANES for part in range(4)]
-    return [slice(first, last) for first, last in zip(edges[:-1], edges[1:])]
-
-
-FORWARD_STEPS = (7, 7, 4, 3, 3, 4, 3, 2, 0)
+FORWARD_STEPS = (6, 8, 4, 3, 3, 3, 4, 2, 0)
 MATS = ('qkv', 'out', 'q2', 'kv2', 'out2', 'ff1', 'ff2')
 WEIGHTS = ('w_a', 'w_b', 'w_kv2', 'w_ff1', 'w_ff2')
 KEPT = ('h', 'h1', 'h2', 'qkv', 'out1', 'q', 'kv', 'out2', 'fa', 'fg', 'z', 'rows')
@@ -410,10 +405,11 @@
     macros = []
     for block in weights:
         high = {name: block[name].shape[CORE] // 2 for name in WEIGHTS}
+
         def add(name, row, rows, first, cols):
-            parts = thirds(cols // LANES)
-            macros.append([(block[name], color, row, rows, pl.ds(first + part.start, part.stop - part.start))
-                           for color, part in enumerate(parts[len(macros) % COLORS:] + parts[:len(macros) % COLORS])])
+            edges = [round(rows // SUB * part / COLORS) * SUB for part in range(COLORS + 1)]
+            macros.append([(block[name], (part + len(macros)) % COLORS, row + edges[part], edges[part + 1] - edges[part],
+                            pl.ds(first, cols)) for part in range(COLORS)])
 
         wide = block['w_a'].shape[-1] // 2
         for part in range(2):
@@ -422,10 +418,9 @@
         for part in range(4):
             add('w_kv2', part * quarter, quarter, 0, wide)
         add('w_b', 0, high['w_b'], 0, wide)
-        tenth = high['w_ff2'] // 20
+        half = high['w_ff2'] // 2
         for part in range(2):
-            macros.append([(block['w_ff2'], color, (part * 10 + row) * tenth, rows * tenth, FULL)
-                           for color, row, rows in zip(range(COLORS), (0, 3, 7), (3, 4, 3))])
+            add('w_ff2', part * half, half, 0, wide // 2)
         inner = block['w_ff1'].shape[-1] // 2
         for part in range(2):
             for half in range(2):

time: 560 us -> 566 us (1.011)
  Pallas kernels: 549 us -> 556 us
    pallas_call x1, Pallas kernels: 223 us -> 230 us  [forward(): pl.pallas_call(functools.partial(forward_kernel, (tokens, width, blocks,...]
where the time goes in v7:
time: 566 us; the launch traced here: 558 us
  Pallas kernels  556 us (98%)
    pallas_call x1, Pallas kernels, backward(): pl.pallas_call(functools.partial(backward_kernel, cfg), in_specs=any_spec...  318 us
    pallas_call x1, Pallas kernels, forward(): pl.pallas_call(functools.partial(forward_kernel, (tokens, width, blocks,...  230 us

profile of v7, /device:TPU:0, one launch (start us, length us, event | category | flops | bytes accessed | tf_op | source)
XLA Modules:
  0.0 558.1 jit_solution(13532850246217931095)
XLA Ops:
  0.6 1.3 pad_bitcast_fusion.refs_9_
  1.9 229.5 %forward.1 = (f32[1536,640]{1,0:T(8,128)}, f32[1536,640]{1,0:T(8,128)}, f32[1536,640]{1,0:T(8,128)}, bf16[1536,1920]{1,0:T(8,128)(2,1)}, bf16[1536,640]{1,0:T(8,...) custom-call(bf16[1536,640]{1,0:T(8,128)(2,1)} %bitcast.88, ...), custom_call_target="tpu_custom_call" | custom-call | flops 99999997952 | bytes 100000000 | tf_op jit(solution)/shard_map/forward/pallas_call | solution.py:722
  231.5 318.4 %backward.1 = (bf16[1536,640]{1,0:T(8,128)(2,1)}, f32[2,2,2,2,9840,128]{5,4,3,2,1,0:T(8,128)}, f32[9840,128]{1,0:T(8,128)}) custom-call(bf16[1536,640]{1,0:T(8,128)(2,1)} %bitcast.89, bf16[480,2048]{1,0:T(8,128)(2,1)} %get-tuple-element.58.refs_1_, f32[1536,640]{1,0:T(8,128)} %get-tuple-element.59.refs_2_, f32[1536,640]{1,0:T(8,128)} %get-tuple-element.60.refs_3_, ...), custom_call_target="tpu_custom_call" | custom-call | flops 99999997952 | bytes 100000000 | tf_op jit(solution)/shard_map/backward/pallas_call | solution.py:1118
  549.8 7.8 %deliver.1 = (f32[1200,128]{1,0:T(8,128)}, f32[400,128]{1,0:T(8,128)}, f32[400,128]{1,0:T(8,128)}, f32[2560,128]{1,0:T(8,128)}, f32[400,128]{1,0:T(8,128)}, /*in...) custom-call(f32[9840,128]{1,0:T(8,128)} %get-tuple-element.93.sum_re, ...), custom_call_target="tpu_custom_call" | custom-call | tf_op jit(solution)/shard_map/deliver/pallas_call | solution.py:1172
